TPU v7x, 32 devices: a whole 2x2x4 slice. The times are simulated.
32 devices in a mesh: seq: 8 (over y, x, core), batch: 4 (over z).
Axes of the slice: x: 2, y: 2, z: 4, core: 2. Of those that a mesh axis runs over, the one named last changes fastest.
Arguments:
- queries: bfloat16 [4, 4096, 256], P('batch', 'seq'), may hold values from -6 to 6
- key_rows: bfloat16 [4, 4096, 256], P('batch', 'seq'), may hold values from -6 to 6
- value_rows: bfloat16 [4, 4096, 256], P('batch', 'seq'), may hold values from -6 to 6
- step_rates: float32 [4, 4096], P('batch', 'seq'), may hold values from 0.02 to 0.2
- cotangent: bfloat16 [4, 4096, 256], P('batch', 'seq'), may hold values from -0.046875 to 0.046875
- fast_init: float32 [768, 256], P('batch'), may hold values from -0.375 to 0.375
Outputs:
- layer_out: bfloat16 [4, 4096, 256], P('batch', 'seq')
- init_grad: float32 [768, 256], P('batch')
All inputs are finite; a program needn't handle non-finite values.
Results may differ from a plain program's by a relative error of at most 0.0012.
Values sent between devices are 32-bit elements; how exact they have to be, the bound alone decides.
No kernel may reach another device: no remote copies, remote signals or barrier semaphores. Data moves between devices by JAX's collectives and lax.ppermute only.
A program may use at most 64 MiB of HBM per device.

v0:
```python
from functools import partial
import math

import jax
import jax.numpy as jnp
from jax import lax
from jax.sharding import PartitionSpec as P


def swiglu_apply(weights, row_block):
    high = lax.Precision.HIGHEST
    projected = jnp.dot(row_block, weights[0], precision=high, preferred_element_type=jnp.float32)
    gate_pre = jnp.dot(row_block, weights[1], precision=high, preferred_element_type=jnp.float32)
    hidden = jax.nn.silu(gate_pre) * projected
    return jnp.dot(hidden, weights[2].T, precision=high, preferred_element_type=jnp.float32)


def inner_loss(weights, key_block, value_block, scaled):
    return -jnp.sum(scaled[:, None] * swiglu_apply(weights, key_block) * value_block)


def inner_grad(weights, key_block, value_block, scaled):
    return jax.grad(inner_loss)(weights, key_block, value_block, scaled)


def body(queries, key_rows, value_rows, step_rates, cotangent, fast_init):
    width = queries.shape[2]
    hidden_units = fast_init.shape[1]
    shards = lax.axis_size("seq")
    divisor = math.sqrt(shards * queries.shape[1])
    query_block = queries[0].astype(jnp.float32)
    key_block = key_rows[0].astype(jnp.float32)
    value_block = value_rows[0].astype(jnp.float32)
    scaled = step_rates[0] / divisor
    cot_block = cotangent[0].astype(jnp.float32)
    gathered = lax.all_gather(fast_init, "batch", axis=0, tiled=True)
    initial = gathered.reshape(3, width, hidden_units)
    local_grad = partial(inner_grad, key_block=key_block, value_block=value_block, scaled=scaled)
    middle = initial - lax.psum(local_grad(initial), "seq")
    final = middle - lax.psum(local_grad(middle), "seq")
    result, pull_out = jax.vjp(partial(swiglu_apply, row_block=query_block), final)
    adjoint_two = lax.psum(pull_out(cot_block)[0], "seq")
    _, pull_middle = jax.vjp(local_grad, middle)
    adjoint_one = adjoint_two - lax.psum(pull_middle(adjoint_two)[0], "seq")
    _, pull_first = jax.vjp(local_grad, initial)
    local_term = pull_first(adjoint_one)[0].reshape(3 * width, hidden_units)
    adjoint_flat = adjoint_one.reshape(3 * width, hidden_units)
    combined = adjoint_flat * (1.0 / shards) - local_term
    summed = lax.psum_scatter(combined, "batch", scatter_dimension=0, tiled=True)
    summed = lax.psum(summed, "seq")
    return (result.astype(jnp.bfloat16)[None], summed)


def solution(mesh):
    placed = (
        P("batch", "seq", None),
        P("batch", "seq", None),
        P("batch", "seq", None),
        P("batch", "seq"),
        P("batch", "seq", None),
        P("batch", None),
    )
    return jax.shard_map(
        body,
        mesh=mesh,
        in_specs=placed,
        out_specs=(P("batch", "seq", None), P("batch", None)),
        check_vma=False,
    )
```

profile of v0, /device:TPU:0, one launch (start us, length us, event | category | flops | bytes accessed | tf_op | source)
XLA Modules:
  0.0 371.0 jit_solution(1469869818026881124)
XLA Ops:
  7.2 0.7 broadcast_multiply_fusion
  7.9 21.5 %all_gather.3 = f32[768,256]{1,0:T(8,128)S(1)} all-gather(f32[192,256]{1,0:T(8,128)} %param.11), channel_id=1, replica_groups=mesh['seq'=8,'batch'=4] {'batch'}, dimensions={0}, use_global_device_ids=true | all-gather | bytes 983040 | tf_op jit(solution)/shard_map/all_gather | solution.py:36
  32.0 1.1 convolution_bitcast_fusion.23
  33.2 0.6 convolution_bitcast_fusion.22
  33.8 1.0 pad_add_fusion.3
  34.9 55.1 %all-reduce.21.cloned.1.call-done = f32[3,256,256]{2,1,0:T(8,128)} async-done(((f32[3,256,256]{2,1,0:T(8,128)}), f32[3,256,256]{2,1,0:T(8,128)}) %all-reduce.21.cloned.1.call-update) | async-done | bytes 786448 | tf_op jit(solution)/shard_map/psum | solution.py:39
  90.0 1.2 sub.32
  93.3 1.1 convolution_bitcast_fusion.20
  95.1 1.0 pad_add_fusion.2
  96.2 55.1 %all-reduce.23.cloned.1.call-done = f32[3,256,256]{2,1,0:T(8,128)} async-done(((f32[3,256,256]{2,1,0:T(8,128)}), f32[3,256,256]{2,1,0:T(8,128)}) %all-reduce.23.cloned.1.call-update) | async-done | bytes 786448 | tf_op jit(solution)/shard_map/psum | solution.py:40
  151.2 1.2 sub.34
  153.3 0.7 copy-done.24
  154.4 0.6 convolution_bitcast_fusion.17
  155.1 0.7 convolution_bitcast_fusion.16
  155.8 0.6 convolution_bitcast_fusion.15
  156.5 1.0 pad_add_fusion.1
  157.7 54.9 %all-reduce.25.cloned.1.call-done = f32[3,256,256]{1,2,0:T(8,128)} async-done(((f32[3,256,256]{1,2,0:T(8,128)}), f32[3,256,256]{1,2,0:T(8,128)}) %all-reduce.25.cloned.1.call-update) | async-done | bytes 786448 | tf_op jit(solution)/shard_map/psum | solution.py:42
  212.6 1.4 convolution_bitcast_fusion.3
  215.3 0.8 convolution_bitcast_fusion.12
  217.3 0.9 convolution_bitcast_fusion.13
  218.2 1.3 convolution_bitcast_fusion.14
  219.5 1.0 pad_add_fusion
  220.5 55.1 %all-reduce.27.cloned.1.call-done = f32[3,256,256]{1,2,0:T(8,128)} async-done(((f32[3,256,256]{1,2,0:T(8,128)}), f32[3,256,256]{1,2,0:T(8,128)}) %all-reduce.27.cloned.1.call-update) | async-done | bytes 786448 | tf_op jit(solution)/shard_map/psum | solution.py:44
  275.6 1.2 sub.36
  279.0 0.8 convolution_bitcast_fusion.9
  280.2 0.9 convolution_bitcast_fusion.10
  281.1 1.3 convolution_bitcast_fusion.11
  282.5 1.2 copy.42
  283.7 22.6 %reduce-scatter.2.cloned.1.call-done = f32[192,256]{1,0:T(8,128)} async-done(((f32[768,256]{1,0:T(8,128)}), f32[192,256]{1,0:T(8,128)}) %reduce-scatter.2.cloned.1.call-update) | async-done | bytes 196624 | tf_op jit(solution)/shard_map/reduce_scatter | solution.py:49
  306.4 1.4 fusion
  307.7 54.7 %all-reduce.29.cloned.1.call-done = f32[192,256]{1,0:T(8,128)} async-done(((f32[192,256]{1,0:T(8,128)}), f32[192,256]{1,0:T(8,128)}) %all-reduce.29.cloned.1.call-update) | async-done | bytes 196624 | tf_op jit(solution)/shard_map/psum | solution.py:50
  362.5 1.6 copy.65
  (79 shorter events, 11.9 us)
Async XLA Ops:
  7.2 22.3 %copy-start = (bf16[1,512,256]{2,1,0:T(8,128)(2,1)S(1)}, bf16[1,512,256]{2,1,0:T(8,128)(2,1)}, u32[]{:S(2)}) copy-start(bf16[1,512,256]{2,1,0:T(8,128)(2,1)} %param.7) | copy-start | bytes 786436
  7.2 82.8 %all-reduce.21.cloned.1.call-start = ((), (), s32[]{:S(2)}) async-start(), calls=%async_computation.1 | async-start | bytes 1572864 | tf_op jit(solution)/shard_map/psum | solution.py:39
  29.5 1.0 copy-start.1
  31.4 1.7 copy-start.12
  31.4 1.7 copy-start.14
  31.4 1.7 copy-start.16
  34.8 116.4 %all-reduce.23.cloned.1.call-start = ((), (), s32[]{:S(2)}) async-start(), calls=%async_computation.2 | async-start | bytes 1572864 | tf_op jit(solution)/shard_map/psum | solution.py:40
  91.9 0.9 copy-start.5
  92.3 1.0 copy-start.3
  92.7 1.7 copy-start.18
  92.7 1.7 copy-start.20
  92.7 1.7 copy-start.22
  96.1 56.4 %copy-start.7 = (bf16[1,512,256]{2,1,0:T(8,128)(2,1)S(1)}, bf16[1,512,256]{2,1,0:T(8,128)(2,1)}, u32[]{:S(2)}) copy-start(bf16[1,512,256]{2,1,0:T(8,128)(2,1)} %param.6) | copy-start | bytes 786436
  96.1 116.5 %all-reduce.25.cloned.1.call-start = ((), (), s32[]{:S(2)}) async-start(), calls=%async_computation.3 | async-start | bytes 1572864 | tf_op jit(solution)/shard_map/psum | solution.py:42
  152.9 2.9 copy-start.8
  152.9 1.1 copy-start.24
  154.0 1.0 copy-start.10
  157.5 118.2 %all-reduce.27.cloned.1.call-start = ((), (), s32[]{:S(2)}) async-start(), calls=%async_computation.4 | async-start | bytes 1572864 | tf_op jit(solution)/shard_map/psum | solution.py:44
  212.6 1.4 copy-start.2
  214.1 1.0 copy-start.6
  214.1 1.2 copy-start.19
  215.3 1.2 copy-start.23
  216.0 1.1 copy-start.4
  216.0 1.2 copy-start.21
  220.5 85.8 %reduce-scatter.2.cloned.1.call-start = ((), (), s32[]{:S(2)}) async-start(), calls=%async_computation.5 | async-start | bytes 983040 | tf_op jit(solution)/shard_map/reduce_scatter | solution.py:49
  277.9 1.0 copy-start.13
  279.0 1.0 copy-start.15
  279.0 1.2 copy-start.17
  282.5 23.9 %copy-start.11 = (f32[512,256]{1,0:T(8,128)S(1)}, f32[512,256]{1,0:T(8,128)}, u32[]{:S(2)}) copy-start(f32[512,256]{1,0:T(8,128)} %copy-done.10) | copy-start | bytes 1572868
  283.7 22.7 %copy-start.9 = (f32[512,256]{1,0:T(8,128)S(1)}, f32[512,256]{1,0:T(8,128)}, u32[]{:S(2)}) copy-start(f32[512,256]{1,0:T(8,128)} %copy-done.8) | copy-start | bytes 1572868
  283.7 78.8 %all-reduce.29.cloned.1.call-start = ((), (), s32[]{:S(2)}) async-start(), calls=%async_computation.6 | async-start | bytes 393216 | tf_op jit(solution)/shard_map/psum | solution.py:50
Sparse Core Ops, SparseCore 0:
  34.9 55.0 all-reduce.20
  96.2 54.9 all-reduce.22
  157.6 54.9 all-reduce.24
  220.6 54.9 all-reduce.26
  283.8 22.4 reduce-scatter.1
  309.2 53.2 all-reduce.28
where the time goes:
time: 371 us
  waiting for transfers between devices  298 us (80%)
  matrix products  21.8 us (6%)
  blocking collectives  21.5 us (6%)
  between operations  14.6 us (4%)
  other arithmetic  8.44 us (2%)
  local copies, waits for them, and re-layouts  6.53 us (2%)
    psum x1, waiting for transfers between devices, body(): middle = initial - lax.psum(local_grad(initial), 'seq')  55.1 us
    psum x1, waiting for transfers between devices, body(): adjoint_one = adjoint_two - lax.psum(pull_middle(adjoint_two)[0], 'seq')  55.1 us
    psum x1, waiting for transfers between devices, body(): final = middle - lax.psum(local_grad(middle), 'seq')  55.1 us
    psum x1, waiting for transfers between devices, body(): adjoint_two = lax.psum(pull_out(cot_block)[0], 'seq')  54.9 us
    psum x1, waiting for transfers between devices, body(): summed = lax.psum(summed, 'seq')  54.7 us
    reduce_scatter x1, waiting for transfers between devices, body(): lax.psum_scatter(combined, 'batch', scatter_dimension=0, tiled=True)  22.6 us
    all_gather x1, blocking collectives, body(): gathered = lax.all_gather(fast_init, 'batch', axis=0, tiled=True)  21.5 us
    dot_general x11, matrix products, swiglu_apply(): jnp.dot(hidden, weights[2].T, precision=high, preferred_element_type=jnp....  9.66 us
  transfers between devices with their start and end apart: 6, of which 6 were waited for; matrix products, arithmetic and copies ran while one was open for 0% of the time, Pallas kernels for 0%

commit v1 on v0

v1 whole, which is shorter than its diff:
```python
import math

import jax
import jax.numpy as jnp
from jax import lax
from jax.experimental import pallas as pl
from jax.experimental.pallas import tpu as pltpu
from jax.sharding import PartitionSpec as P

F32 = jnp.float32
BF16 = jnp.bfloat16
PAD = 8
PAIRED = 8


def nt(left, right):
    return lax.dot_general(left, right, (((1,), (1,)), ((), ())), preferred_element_type=F32)


def nn(left, right):
    return lax.dot_general(left, right, (((1,), (0,)), ((), ())), preferred_element_type=F32)


def tn(left, right):
    return lax.dot_general(left, right, (((0,), (0,)), ((), ())), preferred_element_type=F32)


def two_terms(x):
    high = x.astype(BF16).astype(F32)
    return jnp.concatenate([x, x - high], axis=0).astype(BF16)


def fold(x):
    half = x.shape[0] // 2
    return x[:half] + x[half:]


def gate(g):
    decay = jnp.exp(-jnp.abs(g))
    sig = jnp.where(g >= 0, 1.0, decay) / (1.0 + decay)
    silu = g * sig
    slope = sig + silu * (1.0 - sig)
    return sig, silu, slope


def ascent_terms(stack_ab, stack_c, units, keys, values, eta):
    pre = fold(nt(stack_ab, keys))
    p, g = pre[:units], pre[units:]
    e = eta * fold(nt(stack_c, values))
    _, silu, slope = gate(g)
    pair = jnp.concatenate([e * silu, e * p * slope], axis=0)
    hidden = eta * (silu * p)
    return fold(nn(two_terms(pair), keys)), fold(nn(two_terms(hidden), values))


def curvature_terms(stack_ab, stack_c, units, keys, values, eta):
    pre = fold(nt(stack_ab, keys))
    p, g = pre[:units], pre[units : 2 * units]
    tp, tg = pre[2 * units : 3 * units], pre[3 * units :]
    both = fold(nt(stack_c, values))
    e, te = eta * both[:units], eta * both[units:]
    sig, silu, slope = gate(g)
    bend = sig * (1.0 - sig) * (2.0 + g * (1.0 - 2.0 * sig))
    slope_tg = slope * tg
    pair = jnp.concatenate(
        [te * silu + e * slope_tg, slope * (te * p + e * tp) + e * p * (bend * tg)], axis=0
    )
    hidden = eta * (slope_tg * p + silu * tp)
    return fold(nn(two_terms(pair), keys)), fold(nn(two_terms(hidden), values))


def flat(ref):
    return jnp.concatenate([ref[0], ref[1]], axis=0), ref[2]


def split_message(ref, tokens, width):
    return (
        ref[:tokens, :width].astype(BF16),
        ref[:tokens, width:].astype(BF16),
        ref[tokens : tokens + PAD, :tokens],
    )


def sweep(terms, stack_ab, stack_c, units, width, stores, acc):
    for kv, eta in stores:
        count, _, tokens = eta.shape

        def step(i, acc, kv=kv, eta=eta, tokens=tokens):
            start = i * tokens if isinstance(i, int) else pl.multiple_of(i * tokens, tokens)
            rows = pl.ds(start, tokens)
            ab, c = terms(
                stack_ab, stack_c, units, kv[rows, :width], kv[rows, width:], eta[i, 0:1, :]
            )
            return acc[0] + ab, acc[1] + c

        if count <= PAIRED:
            for i in range(count):
                acc = step(i, acc)
        else:
            acc = lax.fori_loop(0, count, step, acc)
    return acc


def first_kernel(messages, columns, units, width, *refs):
    if columns:
        place_ref, pieces, refs = refs[0], refs[1 : 1 + columns], refs[1 + columns :]
        parts, (base_ref, acc_ref, kv_ref, eta_ref, blocks) = refs[:messages], refs[messages:]
        mine = place_ref[0]
        for k, piece in enumerate(pieces):
            blocks[lax.rem(mine - k + columns, columns)] = piece[...]
        rows = jnp.concatenate([blocks[k] for k in range(columns)], axis=1)
        for j in range(3):
            base_ref[j] = rows[:, j * width : (j + 1) * width]
        start_ref = base_ref
    else:
        start_ref, base_ref = refs[0], refs[1]
        parts, (acc_ref, kv_ref, eta_ref) = refs[2 : 2 + messages], refs[2 + messages :]
    tokens = parts[0].shape[0] - PAD
    ab, c = flat(base_ref)
    stack_ab, stack_c = two_terms(ab), two_terms(c)
    acc = flat(start_ref)
    for i, part in enumerate(parts):
        keys, values, eta = split_message(part, tokens, width)
        kv_ref[i * tokens : (i + 1) * tokens, :width] = keys
        kv_ref[i * tokens : (i + 1) * tokens, width:] = values
        eta_ref[i] = eta
        more = ascent_terms(stack_ab, stack_c, units, keys, values, eta[0:1, :])
        acc = acc[0] + more[0], acc[1] + more[1]
    acc_ref[0], acc_ref[1], acc_ref[2] = acc[0][:units], acc[0][units:], acc[1]


def second_kernel(stored, units, width, *refs):
    start_ref = refs[0]
    stores = [(refs[1 + 2 * i], refs[2 + 2 * i]) for i in range(stored)]
    out_ref = refs[1 + 2 * stored]
    ab, c = flat(start_ref)
    ab, c = sweep(ascent_terms, two_terms(ab), two_terms(c), units, width, stores, (ab, c))
    out_ref[0], out_ref[1], out_ref[2] = ab[:units], ab[units:], c


def outer_kernel(groups, stacked, units, width, *refs):
    weights = [refs[0].at[j] for j in range(groups)] if stacked else refs[:groups]
    refs = refs[1:] if stacked else refs[groups:]
    queries, cots = refs[0], refs[1]
    tokens = queries.shape[0]
    twin = len(refs) > 2 and refs[2].shape == (tokens, 2 * width) and refs[2].dtype == F32
    other = refs[2] if twin else None
    refs = refs[3:] if twin else refs[2:]
    outs = refs[:2] if twin else refs[:1]
    refs = refs[len(outs) :]
    grads = [refs[0].at[j] for j in range(groups)] if stacked else refs
    hidden_units = groups * units
    ab = jnp.concatenate([w[0] for w in weights] + [w[1] for w in weights], axis=0)
    c = jnp.concatenate([w[2] for w in weights], axis=0)
    stack_ab, stack_c = two_terms(ab), two_terms(c)
    c_high = stack_c[:hidden_units]
    c_three = jnp.concatenate([c_high, c_high, stack_c[hidden_units:]], axis=0)
    total = None
    for index, out_ref in enumerate(outs):
        if index == 0:
            q, cot = queries[...], cots[...]
        else:
            q, cot = other[:, :width].astype(BF16), other[:, width:].astype(BF16)
        pre = fold(nt(stack_ab, q))
        p, g = pre[:hidden_units], pre[hidden_units:]
        e = fold(nt(stack_c, cot))
        _, silu, slope = gate(g)
        hidden = silu * p
        pair = jnp.concatenate([e * silu, e * p * slope], axis=0)
        d_ab = fold(nn(two_terms(pair), q))
        hidden_two = two_terms(hidden)
        d_c = fold(nn(hidden_two, cot))
        lifted = jnp.concatenate([hidden_two, hidden_two[:hidden_units]], axis=0)
        out_ref[...] = tn(lifted, c_three).astype(out_ref.dtype)
        total = (d_ab, d_c) if total is None else (total[0] + d_ab, total[1] + d_c)
    for j, grad in enumerate(grads):
        grad[0] = total[0][j * units : (j + 1) * units]
        grad[1] = total[0][hidden_units + j * units : hidden_units + (j + 1) * units]
        grad[2] = total[1][j * units : (j + 1) * units]


def adjoint_kernel(stored, terms, units, width, parts, *refs):
    place_ref, first_ref, second_ref = refs[:3]
    adjoints = refs[3 : 3 + terms]
    stores = [(refs[3 + terms + 2 * i], refs[4 + terms + 2 * i]) for i in range(stored)]
    refs = refs[3 + terms + 2 * stored :]
    outs, (held, bases, blocks) = refs[:parts], refs[parts:]
    u_ab, u_c = flat(adjoints[0])
    for more in adjoints[1:]:
        ab, c = flat(more)
        u_ab, u_c = u_ab + ab, u_c + c
    held[0], held[1], held[2] = u_ab[:units], u_ab[units:], u_c
    bases[0], bases[1] = second_ref[...], first_ref[...]

    def step(i, carry):
        u_ab, u_c = flat(held)
        ab, c = flat(bases.at[i])
        stack_ab = two_terms(jnp.concatenate([ab, u_ab], axis=0))
        stack_c = two_terms(jnp.concatenate([c, u_c], axis=0))
        u_ab, u_c = sweep(curvature_terms, stack_ab, stack_c, units, width, stores, (u_ab, u_c))
        held[0], held[1], held[2] = u_ab[:units], u_ab[units:], u_c
        return carry

    lax.fori_loop(0, 2, step, 0)
    u_ab, u_c = flat(held)
    rows = jnp.concatenate([u_ab[:units], u_ab[units:], u_c], axis=1)
    share = rows.shape[1] // parts
    mine = place_ref[0]
    for target in range(parts):
        blocks[target] = rows[:, target * share : (target + 1) * share]
    for k, out_ref in enumerate(outs):
        out_ref[...] = blocks[lax.rem(mine + k, parts)]


def final_kernel(paired, units, *refs):
    place_ref = refs[0]
    parts = refs[1:-2]
    out_ref, held = refs[-2:]
    if paired:
        here = place_ref[0]
        for mask, part in enumerate(parts):
            source = here ^ mask
            place = (source & 1) * (PAIRED // 2) + (source >> 1)
            held[pl.ds(pl.multiple_of(place * units, units), units), :] = part[...]
    else:
        for j in range(parts[0].shape[0]):
            held[j * units : (j + 1) * units, :] = parts[0][j]
    out_ref[...] = held[...].T


def prepare_kernel(paired, *refs):
    place_ref, keys, values, rates, weights, first, second, column, held = refs
    half, width = keys.shape[0] // 2, keys.shape[1]
    units = column.shape[0]
    for at, message in ((0, first), (half, second)):
        message[:half, :width] = keys[at : at + half, :].astype(F32)
        message[:half, width:] = values[at : at + half, :].astype(F32)
        message[half:, :half] = jnp.broadcast_to(rates[:, at : at + half], (PAD, half))
        message[half:, half:] = jnp.zeros((PAD, 2 * width - half), F32)
    held[...] = weights[...].T
    here = place_ref[0]
    group = (here & 1) * (PAIRED // 2) + (here >> 1) if paired else here
    column[...] = held[pl.ds(pl.multiple_of(group * units, units), units), :]


def size_of(x):
    return math.prod(x.shape) * x.dtype.itemsize


def call(kernel, out_shape, cost, inputs, smem=(), scratch=()):
    specs = [
        pl.BlockSpec(memory_space=pltpu.SMEM if i in smem else pltpu.VMEM)
        for i in range(len(inputs))
    ]
    out_specs = jax.tree.map(lambda _: pl.BlockSpec(memory_space=pltpu.VMEM), out_shape)
    held = sum(size_of(x) for x in list(inputs) + jax.tree.leaves(out_shape))
    return pl.pallas_call(
        kernel,
        out_shape=out_shape,
        in_specs=specs,
        out_specs=out_specs,
        scratch_shapes=list(scratch),
        compiler_params=pltpu.CompilerParams(
            vmem_limit_bytes=min(60 * 1024 * 1024, held + 12 * 1024 * 1024)
        ),
        cost_estimate=pl.CostEstimate(flops=cost, bytes_accessed=0, transcendentals=0),
    )(*inputs)


def body(queries, key_rows, value_rows, step_rates, cotangent, fast_init):
    tokens, width = queries.shape[1:]
    hidden = fast_init.shape[1]
    shards = lax.axis_size("seq")
    parts = lax.axis_size("batch")
    units = hidden // shards
    divisor = math.sqrt(shards * tokens)
    here = lax.axis_index("seq").astype(jnp.int32)[None]
    row = lax.axis_index("batch").astype(jnp.int32)[None]
    paired = shards == PAIRED
    half = tokens // 2
    share = 3 * width // parts
    block = jax.ShapeDtypeStruct((3, units, width), F32)
    column_block = jax.ShapeDtypeStruct((units, share), F32)

    def swap(x, mask):
        return lax.ppermute(x, "seq", [(i, i ^ mask) for i in range(shards)])

    def turn(x, k):
        return lax.ppermute(x, "batch", [(i, (i + k) % parts) for i in range(parts)])

    packed = jax.ShapeDtypeStruct((half + PAD, 2 * width), F32)
    *own, column = call(
        lambda *refs: prepare_kernel(paired, *refs),
        (packed, packed, column_block),
        1000,
        [here, key_rows[0], value_rows[0], step_rates / divisor, fast_init],
        smem=(0,),
        scratch=[pltpu.VMEM((hidden, share), F32)],
    )

    def first(start, messages):
        count = len(messages)
        outs = (
            block,
            jax.ShapeDtypeStruct((count * half, 2 * width), BF16),
            jax.ShapeDtypeStruct((count, PAD, half), F32),
        )
        columns = 0 if len(start) == 2 else len(start) - 1
        return call(
            lambda *refs: first_kernel(count, columns, units, width, *refs),
            (block,) * (columns > 0) + outs,
            2 * 2 * 6 * count * half * width * units,
            start + messages,
            smem=(0,) if columns else (),
            scratch=[pltpu.VMEM((parts, units, share), F32)] if columns else (),
        )

    if paired:
        x = [None, None]
        y = [None, None]
        x[0], y[1] = swap(own[0], 2), swap(own[1], 4)
        columns = [column] + [turn(column, k) for k in range(1, parts)]
        x[1], y[0] = swap(own[1], 2), swap(own[0], 4)
        diagonal = [swap(x[0], 4), swap(y[1], 2)]
        near = own + [swap(m, 1) for m in own]
        side = x + y
        side = side + [swap(m, 1) for m in side]
        far = diagonal + [swap(m, 1) for m in diagonal]
        initial, partial, *store_a = first([row] + columns, near)
        partial, *store_b = first([partial, initial], side)
        middle, *store_c = first([partial, initial], far)
        stores = [*store_a, *store_b, *store_c]
    else:
        initial = lax.all_gather(column, "batch", axis=1, tiled=True)
        initial = jnp.stack(jnp.split(initial, 3, axis=1))
        every = lax.all_gather(jnp.stack(own), "seq", axis=0, tiled=True)
        kv = every[:, :half].astype(BF16).reshape(2 * shards * half, 2 * width)
        stores = [kv, every[:, half:, :half]]
        middle = None

    def ascend(base):
        return call(
            lambda *refs: second_kernel(len(stores) // 2, units, width, *refs),
            block,
            2 * 2 * 6 * shards * tokens * width * units,
            [base] + stores,
        )

    if middle is None:
        middle = ascend(initial)
    last = ascend(middle)

    cost = 2 * 2 * 7 * tokens * width * hidden
    if paired:
        pair = jnp.concatenate([queries[0].astype(F32), cotangent[0].astype(F32)], axis=1)
        other = swap(pair, 1)
        weights = [last, swap(last, 2), swap(last, 4), swap(last, 6)]
        part = jax.ShapeDtypeStruct((tokens, width), F32)
        kept, given, *grads = call(
            lambda *refs: outer_kernel(4, False, units, width, *refs),
            (part, part) + (block,) * 4,
            cost,
            weights + [queries[0], cotangent[0], other],
        )
        adjoints = [grads[0], swap(grads[1], 2), swap(grads[2], 4), swap(grads[3], 6)]
        result = (kept + swap(given, 1)).astype(BF16)
        result, adjoints[0] = lax.optimization_barrier((result, adjoints[0]))
    else:
        weights = lax.all_gather(last, "seq", axis=0, tiled=False)
        result, grads = call(
            lambda *refs: outer_kernel(shards, True, units, width, *refs),
            (
                jax.ShapeDtypeStruct((tokens, width), BF16),
                jax.ShapeDtypeStruct((shards, 3, units, width), F32),
            ),
            cost,
            [weights, queries[0], cotangent[0]],
        )
        adjoints = [lax.psum_scatter(grads, "seq", scatter_dimension=0, tiled=False)]

    rolled = call(
        lambda *refs: adjoint_kernel(len(stores) // 2, len(adjoints), units, width, parts, *refs),
        (column_block,) * parts,
        2 * 2 * 24 * shards * tokens * width * units,
        [row, initial, middle] + adjoints + stores,
        smem=(0,),
        scratch=[
            pltpu.VMEM((3, units, width), F32),
            pltpu.VMEM((2, 3, units, width), F32),
            pltpu.VMEM((parts, units, share), F32),
        ],
    )
    summed = rolled[0]
    for k in range(1, parts):
        summed = summed + turn(rolled[k], k)
    if paired:
        ring = [summed] + [swap(summed, mask) for mask in (2, 4, 6)]
        pieces = []
        for piece in ring:
            pieces += [piece, swap(piece, 1)]
    else:
        pieces = [lax.all_gather(summed, "seq", axis=0, tiled=False)]
    grad = call(
        lambda *refs: final_kernel(paired, units, *refs),
        jax.ShapeDtypeStruct((share, hidden), F32),
        1000,
        [here] + pieces,
        smem=(0,),
        scratch=[pltpu.VMEM((hidden, share), F32)],
    )
    return result[None], grad


def solution(mesh):
    placed = (
        P("batch", "seq", None),
        P("batch", "seq", None),
        P("batch", "seq", None),
        P("batch", "seq"),
        P("batch", "seq", None),
        P("batch", None),
    )
    return jax.shard_map(
        body,
        mesh=mesh,
        in_specs=placed,
        out_specs=(P("batch", "seq", None), P("batch", None)),
        check_vma=False,
    )
```

time: 371 us -> 109 us (0.29)
  waiting for transfers between devices: 298 us -> 40 us
  starting transfers between devices: 0.43 us -> 30.7 us
  Pallas kernels: 0 us -> 25 us
  matrix products: 21.8 us -> 0 us
  blocking collectives: 21.5 us -> 0 us
  between operations: 14.6 us -> 0.83 us
  other arithmetic: 8.44 us -> 3.61 us
    psum x5 -> x0, waiting for transfers between devices: 275 us -> none  [the longest x1 55.1 us: body(): middle = initial - lax.psum(local_grad(initial), 'seq')]
    ppermute x0 -> x35, waiting for transfers between devices: none -> 40 us  [the longest x29 35.8 us: swap(): return lax.ppermute(x, 'seq', [(i, i ^ mask) for i in range(shards)])]
    ppermute x0 -> x35, starting transfers between devices: none -> 30.7 us  [the longest x29 18.5 us: swap(): return lax.ppermute(x, 'seq', [(i, i ^ mask) for i in range(shards)])]
    pallas_call x0 -> x8, Pallas kernels: none -> 25 us  [call(): pl.pallas_call(kernel, out_shape=out_shape, in_specs=specs, out_specs=out...]
    reduce_scatter x1 -> x0, waiting for transfers between devices: 22.6 us -> none  [body(): lax.psum_scatter(combined, 'batch', scatter_dimension=0, tiled=True)]
    dot_general x31 -> x0, matrix products: 21.8 us -> none  [the longest x11 9.66 us: swiglu_apply(): jnp.dot(hidden, weights[2].T, precision=high, preferred_element_type=jnp....]
    all_gather x1 -> x0, blocking collectives: 21.5 us -> none  [body(): gathered = lax.all_gather(fast_init, 'batch', axis=0, tiled=True)]
    add_any x4 -> x0, other arithmetic: 3.92 us -> none  [swiglu_apply(): weights[0]]
  transfers between devices with their start and end apart: 6 -> 35, of which waited for: 6 -> 18; matrix products, arithmetic and copies ran while one was open for 0% -> 3% of each run, Pallas kernels for 0% -> 11%
where the time goes in v1:
time: 109 us
  waiting for transfers between devices  40 us (37%)
  starting transfers between devices  30.7 us (28%)
  Pallas kernels  25 us (23%)
  local copies, waits for them, and re-layouts  8.64 us (8%)
  other arithmetic  3.61 us (3%)
    ppermute x29, waiting for transfers between devices, swap(): return lax.ppermute(x, 'seq', [(i, i ^ mask) for i in range(shards)])  35.8 us
    pallas_call x8, Pallas kernels, call(): pl.pallas_call(kernel, out_shape=out_shape, in_specs=specs, out_specs=out...  25 us
    ppermute x29, starting transfers between devices, swap(): return lax.ppermute(x, 'seq', [(i, i ^ mask) for i in range(shards)])  18.5 us
    ppermute x6, starting transfers between devices, turn(): lax.ppermute(x, 'batch', [(i, (i + k) % parts) for i in range(parts)])  12.1 us
    unnamed x26, local copies, waits for them, and re-layouts  8.64 us
    ppermute x6, waiting for transfers between devices, turn(): lax.ppermute(x, 'batch', [(i, (i + k) % parts) for i in range(parts)])  4.16 us
  transfers between devices with their start and end apart: 35, of which 18 were waited for; matrix products, arithmetic and copies ran while one was open for 3% of the time, Pallas kernels for 11%

profile of v1, /device:TPU:0, one launch (start us, length us, event | category | flops | bytes accessed | tf_op | source)
XLA Modules:
  0.0 108.7 jit_solution(16824363552634867830)
XLA Ops:
  4.9 2.6 %collective-permute-start = (f32[32,192]{1,0:T(8,128)S(1)}, f32[32,192]{1,0:T(8,128)S(1)}, u32[]{:S(2)}, u32[]{:S(2)}) collective-permute-start(f32[32,192]{1,0:T(8,128)S(1)} %get-tuple-element.27.refs_1_), channel_id=1, source_target_pairs={{0,1},{1,2},{2,3},{3,0},{4,5},{5,6},{6,7},{7,4},{8,9},{9,10},{10,1... | collective-permute-start | bytes 73736 | tf_op jit(solution)/shard_map/ppermute | solution.py:289
  7.5 1.5 %collective-permute-start.8 = (f32[264,512]{1,0:T(8,128)S(1)}, f32[264,512]{1,0:T(8,128)S(1)}, u32[]{:S(2)}, u32[]{:S(2)}) collective-permute-start(f32[264,512]{1,0:T(8,128)S(1)} %get-tuple-element.29.refs_6_), channel_id=1, source_target_pairs={{0,16},{4,20},{8,24},{12,28},{16,0},{20,4},{24,8},{28,12},{1,17},{... | collective-permute-start | bytes 1622024 | tf_op jit(solution)/shard_map/ppermute | solution.py:286
  9.0 1.5 %collective-permute-start.5 = (f32[264,512]{1,0:T(8,128)S(1)}, f32[264,512]{1,0:T(8,128)S(1)}, u32[]{:S(2)}, u32[]{:S(2)}) collective-permute-start(f32[264,512]{1,0:T(8,128)S(1)} %get-tuple-element.28.refs_5_), channel_id=1, source_target_pairs={{0,8},{4,12},{8,0},{12,4},{16,24},{20,28},{24,16},{28,20},{1,9},{5... | collective-permute-start | bytes 1622024 | tf_op jit(solution)/shard_map/ppermute | solution.py:286
  10.5 2.6 %collective-permute-start.1 = (f32[32,192]{1,0:T(8,128)S(1)}, f32[32,192]{1,0:T(8,128)S(1)}, u32[]{:S(2)}, u32[]{:S(2)}) collective-permute-start(f32[32,192]{1,0:T(8,128)S(1)} %get-tuple-element.27.refs_1_), channel_id=1, source_target_pairs={{0,2},{1,3},{2,0},{3,1},{4,6},{5,7},{6,4},{7,5},{8,10},{9,11},{10,... | collective-permute-start | bytes 73736 | tf_op jit(solution)/shard_map/ppermute | solution.py:289
  13.1 1.3 %collective-permute-start.2 = (f32[32,192]{1,0:T(8,128)S(1)}, f32[32,192]{1,0:T(8,128)S(1)}, u32[]{:S(2)}, u32[]{:S(2)}) collective-permute-start(f32[32,192]{1,0:T(8,128)S(1)} %get-tuple-element.27.refs_1_), channel_id=1, source_target_pairs={{0,3},{1,0},{2,1},{3,2},{4,7},{5,4},{6,5},{7,6},{8,11},{9,8},{10,9... | collective-permute-start | bytes 73736 | tf_op jit(solution)/shard_map/ppermute | solution.py:289
  15.7 1.3 %collective-permute-done.2.refs_4_ = f32[32,192]{1,0:T(8,128)S(1)} collective-permute-done((f32[32,192]{1,0:T(8,128)S(1)}, f32[32,192]{1,0:T(8,128)S(1)}, u32[]{:S(2)}, u32[]{:S(2)}) %collective-permute-start.2) | collective-permute-done | bytes 24608 | tf_op jit(solution)/shard_map/ppermute | solution.py:289
  19.4 3.3 %collective-permute-done.8.refs_5_ = f32[264,512]{1,0:T(8,128)S(1)} collective-permute-done((f32[264,512]{1,0:T(8,128)S(1)}, f32[264,512]{1,0:T(8,128)S(1)}, u32[]{:S(2)}, u32[]{:S(2)}) %collective-permute-start.8) | collective-permute-done | bytes 540704 | tf_op jit(solution)/shard_map/ppermute | solution.py:286
  22.6 1.5 %collective-permute-done.5.refs_2_ = f32[264,512]{1,0:T(8,128)S(1)} collective-permute-done((f32[264,512]{1,0:T(8,128)S(1)}, f32[264,512]{1,0:T(8,128)S(1)}, u32[]{:S(2)}, u32[]{:S(2)}) %collective-permute-start.5) | collective-permute-done | bytes 540704 | tf_op jit(solution)/shard_map/ppermute | solution.py:286
  25.5 9.2 %collective-permute-done.6.refs_3_ = f32[264,512]{1,0:T(8,128)S(1)} collective-permute-done((f32[264,512]{1,0:T(8,128)S(1)}, f32[264,512]{1,0:T(8,128)S(1)}, u32[]{:S(2)}, u32[]{:S(2)}) %collective-permute-start.6) | collective-permute-done | bytes 540704 | tf_op jit(solution)/shard_map/ppermute | solution.py:286
  34.7 1.5 %collective-permute-start.14 = (f32[264,512]{1,0:T(8,128)S(1)}, f32[264,512]{1,0:T(8,128)}, u32[]{:S(2)}, u32[]{:S(2)}) collective-permute-start(f32[264,512]{1,0:T(8,128)S(1)} %collective-permute-done.8.refs_5_), channel_id=1, source_target_pairs={{0,8},{4,12},{8,0},{12,4},{16,24},{20,28},{24,16},{28,20},{1,9},{5... | collective-permute-start | bytes 1622024 | tf_op jit(solution)/shard_map/ppermute | solution.py:286
  36.2 2.2 %maximum_convert_fusion = f32[512,512]{1,0:T(8,128)} fusion(bf16[512,256]{1,0:T(8,128)(2,1)} %bitcast.11, bf16[512,256]{1,0:T(8,128)(2,1)} %bitcast.9), kind=kLoop, calls=%fused_computation | loop fusion | flops 1048576 | bytes 1572864 | tf_op jit(solution)/shard_map/concatenate | solution.py:355
  38.9 6.2 %collective-permute-done.13.refs_2_ = f32[264,512]{1,0:T(8,128)} collective-permute-done((f32[264,512]{1,0:T(8,128)S(1)}, f32[264,512]{1,0:T(8,128)}, u32[]{:S(2)}, u32[]{:S(2)}) %collective-permute-start.13) | collective-permute-done | bytes 540704 | tf_op jit(solution)/shard_map/ppermute | solution.py:286
  45.1 2.9 %collective-permute-done.14.refs_3_ = f32[264,512]{1,0:T(8,128)} collective-permute-done((f32[264,512]{1,0:T(8,128)S(1)}, f32[264,512]{1,0:T(8,128)}, u32[]{:S(2)}, u32[]{:S(2)}) %collective-permute-start.14) | collective-permute-done | bytes 540704 | tf_op jit(solution)/shard_map/ppermute | solution.py:286
  53.4 3.4 %shard_map.79 = (f32[3,32,256]{2,1,0:T(8,128)S(1)}, bf16[2048,512]{1,0:T(8,128)(2,1)S(1)}, f32[8,8,256]{2,1,0:T(8,128)S(1)}) custom-call(f32[3,32,256]{2,1,0:T(8,128)S(1)} %get-tuple-element.30.refs_0_, f32[3,32,256]{2,1,0:T(8,128)S(1)} %get-tuple-element.31.refs_1_, f32[264,512]{1,0:T(8,128)S(1)} %collective-permute-done.5.refs_2_, ...), custom_call_target="tpu_custom_call" | custom-call | flops 402653184 | tf_op jit(solution)/shard_map/pallas_call | solution.py:257
  56.8 2.7 %shard_map.80 = (f32[3,32,256]{2,1,0:T(8,128)S(1)}, bf16[1024,512]{1,0:T(8,128)(2,1)S(1)}, f32[4,8,256]{2,1,0:T(8,128)S(1)}) custom-call(f32[3,32,256]{2,1,0:T(8,128)S(1)} %get-tuple-element.32.refs_0_, f32[3,32,256]{2,1,0:T(8,128)S(1)} %get-tuple-element.31.refs_1_, f32[264,512]{1,0:T(8,128)} %collective-permute-done.13.refs_2_, ...), custom_call_target="tpu_custom_call" | custom-call | flops 201326592 | tf_op jit(solution)/shard_map/pallas_call | solution.py:257
  59.5 4.2 %shard_map.81.refs_0_ = f32[3,32,256]{2,1,0:T(8,128)S(1)} custom-call(f32[3,32,256]{2,1,0:T(8,128)S(1)} %get-tuple-element.33.refs_0_.refs_2_, bf16[1024,512]{1,0:T(8,128)(2,1)S(1)} %get-tuple-element.34.refs_1_.refs_7_, f32[4,8,256]{2,1,0:T(8,128)S(1)} %get-tuple-element.35.refs_2_.refs_8_, bf16[2048,512]{1,0:T(8,128)(2,1)S(1)} %get-tuple-element.36.refs_3_.refs_9_, ...), custom_call_target="tpu_custom_call" | custom-call | flops 805306368 | tf_op jit(solution)/shard_map/pallas_call | solution.py:257
  63.7 1.6 %collective-permute-start.17 = (f32[3,32,256]{2,1,0:T(8,128)S(1)}, f32[3,32,256]{2,1,0:T(8,128)S(1)}, u32[]{:S(2)}, u32[]{:S(2)}) collective-permute-start(f32[3,32,256]{2,1,0:T(8,128)S(1)} %shard_map.81.refs_0_), channel_id=1, source_target_pairs={{0,8},{4,12},{8,0},{12,4},{16,24},{20,28},{24,16},{28,20},{1,9},{5... | collective-permute-start | bytes 294920 | tf_op jit(solution)/shard_map/ppermute | solution.py:286
  65.8 1.5 %collective-permute-start.19 = (f32[3,32,256]{2,1,0:T(8,128)S(1)}, f32[3,32,256]{2,1,0:T(8,128)S(1)}, u32[]{:S(2)}, u32[]{:S(2)}) collective-permute-start(f32[3,32,256]{2,1,0:T(8,128)S(1)} %shard_map.81.refs_0_), channel_id=1, source_target_pairs={{0,24},{4,28},{8,16},{12,20},{16,8},{20,12},{24,0},{28,4},{1,25},{... | collective-permute-start | bytes 294920 | tf_op jit(solution)/shard_map/ppermute | solution.py:286
  67.3 1.7 %collective-permute-done.17.refs_1_ = f32[3,32,256]{2,1,0:T(8,128)S(1)} collective-permute-done((f32[3,32,256]{2,1,0:T(8,128)S(1)}, f32[3,32,256]{2,1,0:T(8,128)S(1)}, u32[]{:S(2)}, u32[]{:S(2)}) %collective-permute-start.17) | collective-permute-done | bytes 98336 | tf_op jit(solution)/shard_map/ppermute | solution.py:286
  69.0 3.3 %collective-permute-done.18.refs_2_ = f32[3,32,256]{2,1,0:T(8,128)S(1)} collective-permute-done((f32[3,32,256]{2,1,0:T(8,128)S(1)}, f32[3,32,256]{2,1,0:T(8,128)S(1)}, u32[]{:S(2)}, u32[]{:S(2)}) %collective-permute-start.18) | collective-permute-done | bytes 98336 | tf_op jit(solution)/shard_map/ppermute | solution.py:286
  72.3 2.8 %shard_map.82 = (f32[512,256]{1,0:T(8,128)S(1)}, f32[512,256]{1,0:T(8,128)S(1)}, f32[3,32,256]{2,1,0:T(8,128)S(1)}, f32[3,32,256]{2,1,0:T(8,128)S(1)}, f32[3,32,...) custom-call(f32[3,32,256]{2,1,0:T(8,128)S(1)} %shard_map.81.refs_0_, f32[3,32,256]{2,1,0:T(8,128)S(1)} %collective-permute-done.17.refs_1_, ...), custom_call_target="tpu_custom_call" | custom-call | flops 939524096 | tf_op jit(solution)/shard_map/pallas_call | solution.py:257
  77.0 1.8 %collective-permute-start.24 = (f32[3,32,256]{2,1,0:T(8,128)S(1)}, f32[3,32,256]{2,1,0:T(8,128)S(1)}, u32[]{:S(2)}, u32[]{:S(2)}) collective-permute-start(f32[3,32,256]{2,1,0:T(8,128)S(1)} %get-tuple-element.47), channel_id=1, source_target_pairs={{0,24},{4,28},{8,16},{12,20},{16,8},{20,12},{24,0},{28,4},{1,25},{... | collective-permute-start | bytes 294920 | tf_op jit(solution)/shard_map/ppermute | solution.py:286
  79.5 1.4 %collective-permute-done.22.refs_4_ = f32[3,32,256]{2,1,0:T(8,128)S(1)} collective-permute-done((f32[3,32,256]{2,1,0:T(8,128)S(1)}, f32[3,32,256]{2,1,0:T(8,128)S(1)}, u32[]{:S(2)}, u32[]{:S(2)}) %collective-permute-start.22) | collective-permute-done | bytes 98336 | tf_op jit(solution)/shard_map/ppermute | solution.py:286
  81.0 1.8 %collective-permute-done.23.refs_5_ = f32[3,32,256]{2,1,0:T(8,128)S(1)} collective-permute-done((f32[3,32,256]{2,1,0:T(8,128)S(1)}, f32[3,32,256]{2,1,0:T(8,128)S(1)}, u32[]{:S(2)}, u32[]{:S(2)}) %collective-permute-start.23) | collective-permute-done | bytes 98336 | tf_op jit(solution)/shard_map/ppermute | solution.py:286
  82.8 9.7 %shard_map.83 = (f32[32,192]{1,0:T(8,128)S(1)}, f32[32,192]{1,0:T(8,128)S(1)}, f32[32,192]{1,0:T(8,128)S(1)}, f32[32,192]{1,0:T(8,128)S(1)}) custom-call(s32[1]{0:T(128)} %bitcast.refs_0_, f32[3,32,256]{2,1,0:T(8,128)S(1)} %get-tuple-element.31.refs_1_, f32[3,32,256]{2,1,0:T(8,128)S(1)} %get-tuple-element.33.refs_0_.refs_2_, ...), custom_call_target="tpu_custom_call" | custom-call | flops 3221225472 | tf_op jit(solution)/shard_map/pallas_call | solution.py:257
  92.5 1.6 %collective-permute-start.25 = (f32[32,192]{1,0:T(8,128)S(1)}, f32[32,192]{1,0:T(8,128)S(1)}, u32[]{:S(2)}, u32[]{:S(2)}) collective-permute-start(f32[32,192]{1,0:T(8,128)S(1)} %get-tuple-element.49), channel_id=1, source_target_pairs={{0,1},{1,2},{2,3},{3,0},{4,5},{5,6},{6,7},{7,4},{8,9},{9,10},{10,1... | collective-permute-start | bytes 73736 | tf_op jit(solution)/shard_map/ppermute | solution.py:289
  94.2 1.3 %collective-permute-start.26 = (f32[32,192]{1,0:T(8,128)S(1)}, f32[32,192]{1,0:T(8,128)S(1)}, u32[]{:S(2)}, u32[]{:S(2)}) collective-permute-start(f32[32,192]{1,0:T(8,128)S(1)} %get-tuple-element.50), channel_id=1, source_target_pairs={{0,2},{1,3},{2,0},{3,1},{4,6},{5,7},{6,4},{7,5},{8,10},{9,11},{10,... | collective-permute-start | bytes 73736 | tf_op jit(solution)/shard_map/ppermute | solution.py:289
  95.5 2.6 %collective-permute-start.27 = (f32[32,192]{1,0:T(8,128)S(1)}, f32[32,192]{1,0:T(8,128)S(1)}, u32[]{:S(2)}, u32[]{:S(2)}) collective-permute-start(f32[32,192]{1,0:T(8,128)S(1)} %get-tuple-element.51), channel_id=1, source_target_pairs={{0,3},{1,0},{2,1},{3,2},{4,7},{5,4},{6,5},{7,6},{8,11},{9,8},{10,9... | collective-permute-start | bytes 73736 | tf_op jit(solution)/shard_map/ppermute | solution.py:289
  99.7 1.5 %collective-permute-start.29 = (f32[32,192]{1,0:T(8,128)S(1)}, f32[32,192]{1,0:T(8,128)S(1)}, u32[]{:S(2)}, u32[]{:S(2)}) collective-permute-start(f32[32,192]{1,0:T(8,128)S(1)} %add_add_fusion.refs_1_), channel_id=1, source_target_pairs={{0,8},{4,12},{8,0},{12,4},{16,24},{20,28},{24,16},{28,20},{1,9},{5... | collective-permute-start | bytes 73736 | tf_op jit(solution)/shard_map/ppermute | solution.py:286
  101.8 1.4 %collective-permute-start.33 = (f32[32,192]{1,0:T(8,128)S(1)}, f32[32,192]{1,0:T(8,128)S(1)}, u32[]{:S(2)}, u32[]{:S(2)}) collective-permute-start(f32[32,192]{1,0:T(8,128)S(1)} %add_add_fusion.refs_1_), channel_id=1, source_target_pairs={{0,24},{4,28},{8,16},{12,20},{16,8},{20,12},{24,0},{28,4},{1,25},{... | collective-permute-start | bytes 73736 | tf_op jit(solution)/shard_map/ppermute | solution.py:286
  103.8 1.4 %collective-permute-done.31.refs_5_ = f32[32,192]{1,0:T(8,128)S(1)} collective-permute-done((f32[32,192]{1,0:T(8,128)S(1)}, f32[32,192]{1,0:T(8,128)S(1)}, u32[]{:S(2)}, u32[]{:S(2)}) %collective-permute-start.31) | collective-permute-done | bytes 24608 | tf_op jit(solution)/shard_map/ppermute | solution.py:286
  105.2 1.5 %collective-permute-done.33.refs_7_ = f32[32,192]{1,0:T(8,128)S(1)} collective-permute-done((f32[32,192]{1,0:T(8,128)S(1)}, f32[32,192]{1,0:T(8,128)S(1)}, u32[]{:S(2)}, u32[]{:S(2)}) %collective-permute-start.33) | collective-permute-done | bytes 24608 | tf_op jit(solution)/shard_map/ppermute | solution.py:286
  (76 shorter events, 23.0 us)
Async XLA Ops:
  4.3 13.2 %collective-permute-start.3 = (f32[264,512]{1,0:T(8,128)S(1)}, f32[264,512]{1,0:T(8,128)S(1)}, u32[]{:S(2)}, u32[]{:S(2)}) collective-permute-start(f32[264,512]{1,0:T(8,128)S(1)} %get-tuple-element.28.refs_5_), channel_id=1, source_target_pairs={{0,4},{4,0},{8,12},{12,8},{16,20},{20,16},{24,28},{28,24},{1,5},{5... | collective-permute-start | bytes 1622024 | tf_op jit(solution)/shard_map/ppermute | solution.py:286
  4.9 8.2 %collective-permute-start = (f32[32,192]{1,0:T(8,128)S(1)}, f32[32,192]{1,0:T(8,128)S(1)}, u32[]{:S(2)}, u32[]{:S(2)}) collective-permute-start(f32[32,192]{1,0:T(8,128)S(1)} %get-tuple-element.27.refs_1_), channel_id=1, source_target_pairs={{0,1},{1,2},{2,3},{3,0},{4,5},{5,6},{6,7},{7,4},{8,9},{9,10},{10,1... | collective-permute-start | bytes 73736 | tf_op jit(solution)/shard_map/ppermute | solution.py:289
  7.5 15.1 %collective-permute-start.8 = (f32[264,512]{1,0:T(8,128)S(1)}, f32[264,512]{1,0:T(8,128)S(1)}, u32[]{:S(2)}, u32[]{:S(2)}) collective-permute-start(f32[264,512]{1,0:T(8,128)S(1)} %get-tuple-element.29.refs_6_), channel_id=1, source_target_pairs={{0,16},{4,20},{8,24},{12,28},{16,0},{20,4},{24,8},{28,12},{1,17},{... | collective-permute-start | bytes 1622024 | tf_op jit(solution)/shard_map/ppermute | solution.py:286
  9.0 15.1 %collective-permute-start.5 = (f32[264,512]{1,0:T(8,128)S(1)}, f32[264,512]{1,0:T(8,128)S(1)}, u32[]{:S(2)}, u32[]{:S(2)}) collective-permute-start(f32[264,512]{1,0:T(8,128)S(1)} %get-tuple-element.28.refs_5_), channel_id=1, source_target_pairs={{0,8},{4,12},{8,0},{12,4},{16,24},{20,28},{24,16},{28,20},{1,9},{5... | collective-permute-start | bytes 1622024 | tf_op jit(solution)/shard_map/ppermute | solution.py:286
  10.5 5.2 %collective-permute-start.1 = (f32[32,192]{1,0:T(8,128)S(1)}, f32[32,192]{1,0:T(8,128)S(1)}, u32[]{:S(2)}, u32[]{:S(2)}) collective-permute-start(f32[32,192]{1,0:T(8,128)S(1)} %get-tuple-element.27.refs_1_), channel_id=1, source_target_pairs={{0,2},{1,3},{2,0},{3,1},{4,6},{5,7},{6,4},{7,5},{8,10},{9,11},{10,... | collective-permute-start | bytes 73736 | tf_op jit(solution)/shard_map/ppermute | solution.py:289
  13.1 3.9 %collective-permute-start.2 = (f32[32,192]{1,0:T(8,128)S(1)}, f32[32,192]{1,0:T(8,128)S(1)}, u32[]{:S(2)}, u32[]{:S(2)}) collective-permute-start(f32[32,192]{1,0:T(8,128)S(1)} %get-tuple-element.27.refs_1_), channel_id=1, source_target_pairs={{0,3},{1,0},{2,1},{3,2},{4,7},{5,4},{6,5},{7,6},{8,11},{9,8},{10,9... | collective-permute-start | bytes 73736 | tf_op jit(solution)/shard_map/ppermute | solution.py:289
  15.7 8.5 %collective-permute-start.4 = (f32[264,512]{1,0:T(8,128)S(1)}, f32[264,512]{1,0:T(8,128)S(1)}, u32[]{:S(2)}, u32[]{:S(2)}) collective-permute-start(f32[264,512]{1,0:T(8,128)S(1)} %get-tuple-element.29.refs_6_), channel_id=1, source_target_pairs={{0,4},{4,0},{8,12},{12,8},{16,20},{20,16},{24,28},{28,24},{1,5},{5... | collective-permute-start | bytes 1622024 | tf_op jit(solution)/shard_map/ppermute | solution.py:286
  17.0 17.7 %collective-permute-start.6 = (f32[264,512]{1,0:T(8,128)S(1)}, f32[264,512]{1,0:T(8,128)S(1)}, u32[]{:S(2)}, u32[]{:S(2)}) collective-permute-start(f32[264,512]{1,0:T(8,128)S(1)} %get-tuple-element.29.refs_6_), channel_id=1, source_target_pairs={{0,8},{4,12},{8,0},{12,4},{16,24},{20,28},{24,16},{28,20},{1,9},{5... | collective-permute-start | bytes 1622024 | tf_op jit(solution)/shard_map/ppermute | solution.py:286
  18.4 20.0 %collective-permute-start.7 = (f32[264,512]{1,0:T(8,128)S(1)}, f32[264,512]{1,0:T(8,128)S(1)}, u32[]{:S(2)}, u32[]{:S(2)}) collective-permute-start(f32[264,512]{1,0:T(8,128)S(1)} %get-tuple-element.28.refs_5_), channel_id=1, source_target_pairs={{0,16},{4,20},{8,24},{12,28},{16,0},{20,4},{24,8},{28,12},{1,17},{... | collective-permute-start | bytes 1622024 | tf_op jit(solution)/shard_map/ppermute | solution.py:286
  22.6 15.7 %collective-permute-start.12 = (f32[264,512]{1,0:T(8,128)S(1)}, f32[264,512]{1,0:T(8,128)S(1)}, u32[]{:S(2)}, u32[]{:S(2)}) collective-permute-start(f32[264,512]{1,0:T(8,128)S(1)} %collective-permute-done.8.refs_5_), channel_id=1, source_target_pairs={{0,4},{4,0},{8,12},{12,8},{16,20},{20,16},{24,28},{28,24},{1,5},{5... | collective-permute-start | bytes 1622024 | tf_op jit(solution)/shard_map/ppermute | solution.py:286
  24.2 14.7 %collective-permute-start.9 = (f32[264,512]{1,0:T(8,128)S(1)}, f32[264,512]{1,0:T(8,128)S(1)}, u32[]{:S(2)}, u32[]{:S(2)}) collective-permute-start(f32[264,512]{1,0:T(8,128)S(1)} %collective-permute-done.5.refs_2_), channel_id=1, source_target_pairs={{0,4},{4,0},{8,12},{12,8},{16,20},{20,16},{24,28},{28,24},{1,5},{5... | collective-permute-start | bytes 1622024 | tf_op jit(solution)/shard_map/ppermute | solution.py:286
  25.0 20.1 %collective-permute-start.13 = (f32[264,512]{1,0:T(8,128)S(1)}, f32[264,512]{1,0:T(8,128)}, u32[]{:S(2)}, u32[]{:S(2)}) collective-permute-start(f32[264,512]{1,0:T(8,128)S(1)} %collective-permute-done.5.refs_2_), channel_id=1, source_target_pairs={{0,16},{4,20},{8,24},{12,28},{16,0},{20,4},{24,8},{28,12},{1,17},{... | collective-permute-start | bytes 1622024 | tf_op jit(solution)/shard_map/ppermute | solution.py:286
  34.7 13.3 %collective-permute-start.14 = (f32[264,512]{1,0:T(8,128)S(1)}, f32[264,512]{1,0:T(8,128)}, u32[]{:S(2)}, u32[]{:S(2)}) collective-permute-start(f32[264,512]{1,0:T(8,128)S(1)} %collective-permute-done.8.refs_5_), channel_id=1, source_target_pairs={{0,8},{4,12},{8,0},{12,4},{16,24},{20,28},{24,16},{28,20},{1,9},{5... | collective-permute-start | bytes 1622024 | tf_op jit(solution)/shard_map/ppermute | solution.py:286
  38.3 28.9 %collective-permute-start.20 = (f32[512,512]{1,0:T(8,128)}, f32[512,512]{1,0:T(8,128)}, u32[]{:S(2)}, u32[]{:S(2)}) collective-permute-start(f32[512,512]{1,0:T(8,128)} %maximum_convert_fusion), channel_id=1, source_target_pairs={{0,4},{4,0},{8,12},{12,8},{16,20},{20,16},{24,28},{28,24},{1,5},{5... | collective-permute-start | bytes 3145736 | tf_op jit(solution)/shard_map/ppermute | solution.py:286
  38.3 15.1 %collective-permute-start.10 = (f32[264,512]{1,0:T(8,128)S(1)}, f32[264,512]{1,0:T(8,128)}, u32[]{:S(2)}, u32[]{:S(2)}) collective-permute-start(f32[264,512]{1,0:T(8,128)S(1)} %collective-permute-done.6.refs_3_), channel_id=1, source_target_pairs={{0,4},{4,0},{8,12},{12,8},{16,20},{20,16},{24,28},{28,24},{1,5},{5... | collective-permute-start | bytes 1622024 | tf_op jit(solution)/shard_map/ppermute | solution.py:286
  38.8 14.6 %collective-permute-start.11 = (f32[264,512]{1,0:T(8,128)S(1)}, f32[264,512]{1,0:T(8,128)}, u32[]{:S(2)}, u32[]{:S(2)}) collective-permute-start(f32[264,512]{1,0:T(8,128)S(1)} %collective-permute-done.7.refs_4_), channel_id=1, source_target_pairs={{0,4},{4,0},{8,12},{12,8},{16,20},{20,16},{24,28},{28,24},{1,5},{5... | collective-permute-start | bytes 1622024 | tf_op jit(solution)/shard_map/ppermute | solution.py:286
  45.1 11.7 %collective-permute-start.15 = (f32[264,512]{1,0:T(8,128)}, f32[264,512]{1,0:T(8,128)}, u32[]{:S(2)}, u32[]{:S(2)}) collective-permute-start(f32[264,512]{1,0:T(8,128)} %collective-permute-done.13.refs_2_), channel_id=1, source_target_pairs={{0,4},{4,0},{8,12},{12,8},{16,20},{20,16},{24,28},{28,24},{1,5},{5... | collective-permute-start | bytes 1622024 | tf_op jit(solution)/shard_map/ppermute | solution.py:286
  48.0 8.8 %collective-permute-start.16 = (f32[264,512]{1,0:T(8,128)}, f32[264,512]{1,0:T(8,128)}, u32[]{:S(2)}, u32[]{:S(2)}) collective-permute-start(f32[264,512]{1,0:T(8,128)} %collective-permute-done.14.refs_3_), channel_id=1, source_target_pairs={{0,4},{4,0},{8,12},{12,8},{16,20},{20,16},{24,28},{28,24},{1,5},{5... | collective-permute-start | bytes 1622024 | tf_op jit(solution)/shard_map/ppermute | solution.py:286
  63.7 5.3 %collective-permute-start.17 = (f32[3,32,256]{2,1,0:T(8,128)S(1)}, f32[3,32,256]{2,1,0:T(8,128)S(1)}, u32[]{:S(2)}, u32[]{:S(2)}) collective-permute-start(f32[3,32,256]{2,1,0:T(8,128)S(1)} %shard_map.81.refs_0_), channel_id=1, source_target_pairs={{0,8},{4,12},{8,0},{12,4},{16,24},{20,28},{24,16},{28,20},{1,9},{5... | collective-permute-start | bytes 294920 | tf_op jit(solution)/shard_map/ppermute | solution.py:286
  65.3 7.0 %collective-permute-start.18 = (f32[3,32,256]{2,1,0:T(8,128)S(1)}, f32[3,32,256]{2,1,0:T(8,128)S(1)}, u32[]{:S(2)}, u32[]{:S(2)}) collective-permute-start(f32[3,32,256]{2,1,0:T(8,128)S(1)} %shard_map.81.refs_0_), channel_id=1, source_target_pairs={{0,16},{4,20},{8,24},{12,28},{16,0},{20,4},{24,8},{28,12},{1,17},{... | collective-permute-start | bytes 294920 | tf_op jit(solution)/shard_map/ppermute | solution.py:286
  65.8 6.5 %collective-permute-start.19 = (f32[3,32,256]{2,1,0:T(8,128)S(1)}, f32[3,32,256]{2,1,0:T(8,128)S(1)}, u32[]{:S(2)}, u32[]{:S(2)}) collective-permute-start(f32[3,32,256]{2,1,0:T(8,128)S(1)} %shard_map.81.refs_0_), channel_id=1, source_target_pairs={{0,24},{4,28},{8,16},{12,20},{16,8},{20,12},{24,0},{28,4},{1,25},{... | collective-permute-start | bytes 294920 | tf_op jit(solution)/shard_map/ppermute | solution.py:286
  75.1 3.6 %collective-permute-start.21 = (f32[512,256]{1,0:T(8,128)S(1)}, f32[512,256]{1,0:T(8,128)S(1)}, u32[]{:S(2)}, u32[]{:S(2)}) collective-permute-start(f32[512,256]{1,0:T(8,128)S(1)} %get-tuple-element.41), channel_id=1, source_target_pairs={{0,4},{4,0},{8,12},{12,8},{16,20},{20,16},{24,28},{28,24},{1,5},{5... | collective-permute-start | bytes 1572872 | tf_op jit(solution)/shard_map/ppermute | solution.py:286
  75.2 5.7 %collective-permute-start.22 = (f32[3,32,256]{2,1,0:T(8,128)S(1)}, f32[3,32,256]{2,1,0:T(8,128)S(1)}, u32[]{:S(2)}, u32[]{:S(2)}) collective-permute-start(f32[3,32,256]{2,1,0:T(8,128)S(1)} %get-tuple-element.45), channel_id=1, source_target_pairs={{0,8},{4,12},{8,0},{12,4},{16,24},{20,28},{24,16},{28,20},{1,9},{5... | collective-permute-start | bytes 294920 | tf_op jit(solution)/shard_map/ppermute | solution.py:286
  75.8 7.0 %collective-permute-start.23 = (f32[3,32,256]{2,1,0:T(8,128)S(1)}, f32[3,32,256]{2,1,0:T(8,128)S(1)}, u32[]{:S(2)}, u32[]{:S(2)}) collective-permute-start(f32[3,32,256]{2,1,0:T(8,128)S(1)} %get-tuple-element.46), channel_id=1, source_target_pairs={{0,16},{4,20},{8,24},{12,28},{16,0},{20,4},{24,8},{28,12},{1,17},{... | collective-permute-start | bytes 294920 | tf_op jit(solution)/shard_map/ppermute | solution.py:286
  77.0 5.8 %collective-permute-start.24 = (f32[3,32,256]{2,1,0:T(8,128)S(1)}, f32[3,32,256]{2,1,0:T(8,128)S(1)}, u32[]{:S(2)}, u32[]{:S(2)}) collective-permute-start(f32[3,32,256]{2,1,0:T(8,128)S(1)} %get-tuple-element.47), channel_id=1, source_target_pairs={{0,24},{4,28},{8,16},{12,20},{16,8},{20,12},{24,0},{28,4},{1,25},{... | collective-permute-start | bytes 294920 | tf_op jit(solution)/shard_map/ppermute | solution.py:286
  92.5 5.8 %collective-permute-start.25 = (f32[32,192]{1,0:T(8,128)S(1)}, f32[32,192]{1,0:T(8,128)S(1)}, u32[]{:S(2)}, u32[]{:S(2)}) collective-permute-start(f32[32,192]{1,0:T(8,128)S(1)} %get-tuple-element.49), channel_id=1, source_target_pairs={{0,1},{1,2},{2,3},{3,0},{4,5},{5,6},{6,7},{7,4},{8,9},{9,10},{10,1... | collective-permute-start | bytes 73736 | tf_op jit(solution)/shard_map/ppermute | solution.py:289
  94.2 4.8 %collective-permute-start.26 = (f32[32,192]{1,0:T(8,128)S(1)}, f32[32,192]{1,0:T(8,128)S(1)}, u32[]{:S(2)}, u32[]{:S(2)}) collective-permute-start(f32[32,192]{1,0:T(8,128)S(1)} %get-tuple-element.50), channel_id=1, source_target_pairs={{0,2},{1,3},{2,0},{3,1},{4,6},{5,7},{6,4},{7,5},{8,10},{9,11},{10,... | collective-permute-start | bytes 73736 | tf_op jit(solution)/shard_map/ppermute | solution.py:289
  95.5 4.2 %collective-permute-start.27 = (f32[32,192]{1,0:T(8,128)S(1)}, f32[32,192]{1,0:T(8,128)S(1)}, u32[]{:S(2)}, u32[]{:S(2)}) collective-permute-start(f32[32,192]{1,0:T(8,128)S(1)} %get-tuple-element.51), channel_id=1, source_target_pairs={{0,3},{1,0},{2,1},{3,2},{4,7},{5,4},{6,5},{7,6},{8,11},{9,8},{10,9... | collective-permute-start | bytes 73736 | tf_op jit(solution)/shard_map/ppermute | solution.py:289
  99.7 4.0 %collective-permute-start.29 = (f32[32,192]{1,0:T(8,128)S(1)}, f32[32,192]{1,0:T(8,128)S(1)}, u32[]{:S(2)}, u32[]{:S(2)}) collective-permute-start(f32[32,192]{1,0:T(8,128)S(1)} %add_add_fusion.refs_1_), channel_id=1, source_target_pairs={{0,8},{4,12},{8,0},{12,4},{16,24},{20,28},{24,16},{28,20},{1,9},{5... | collective-permute-start | bytes 73736 | tf_op jit(solution)/shard_map/ppermute | solution.py:286
  101.3 3.9 %collective-permute-start.31 = (f32[32,192]{1,0:T(8,128)S(1)}, f32[32,192]{1,0:T(8,128)S(1)}, u32[]{:S(2)}, u32[]{:S(2)}) collective-permute-start(f32[32,192]{1,0:T(8,128)S(1)} %add_add_fusion.refs_1_), channel_id=1, source_target_pairs={{0,16},{4,20},{8,24},{12,28},{16,0},{20,4},{24,8},{28,12},{1,17},{... | collective-permute-start | bytes 73736 | tf_op jit(solution)/shard_map/ppermute | solution.py:286
  101.8 4.8 %collective-permute-start.33 = (f32[32,192]{1,0:T(8,128)S(1)}, f32[32,192]{1,0:T(8,128)S(1)}, u32[]{:S(2)}, u32[]{:S(2)}) collective-permute-start(f32[32,192]{1,0:T(8,128)S(1)} %add_add_fusion.refs_1_), channel_id=1, source_target_pairs={{0,24},{4,28},{8,16},{12,20},{16,8},{20,12},{24,0},{28,4},{1,25},{... | collective-permute-start | bytes 73736 | tf_op jit(solution)/shard_map/ppermute | solution.py:286
  103.3 3.4 %collective-permute-start.28 = (f32[32,192]{1,0:T(8,128)S(1)}, f32[32,192]{1,0:T(8,128)S(1)}, u32[]{:S(2)}, u32[]{:S(2)}) collective-permute-start(f32[32,192]{1,0:T(8,128)S(1)} %add_add_fusion.refs_1_), channel_id=1, source_target_pairs={{0,4},{4,0},{8,12},{12,8},{16,20},{20,16},{24,28},{28,24},{1,5},{5... | collective-permute-start | bytes 73736 | tf_op jit(solution)/shard_map/ppermute | solution.py:286
  (16 other events, 127.2 us)

commit v2 on v1

--- a/solution.py
+++ b/solution.py
@@ -7,10 +7,13 @@
 from jax.experimental.pallas import tpu as pltpu
 from jax.sharding import PartitionSpec as P
 
+
 F32 = jnp.float32
 BF16 = jnp.bfloat16
 PAD = 8
 PAIRED = 8
+CHUNK = 1024
+MIB = 1024 * 1024
 
 
 def nt(left, right):
@@ -43,21 +46,25 @@
     return sig, silu, slope
 
 
-def ascent_terms(stack_ab, stack_c, units, keys, values, eta):
-    pre = fold(nt(stack_ab, keys))
+def forward(stack_ab, stack_c, keys, values):
+    return nt(stack_ab, keys), nt(stack_c, values)
+
+
+def ascent_terms(units, pre, cross, keys, values, eta):
+    pre = fold(pre)
     p, g = pre[:units], pre[units:]
-    e = eta * fold(nt(stack_c, values))
+    e = eta * fold(cross)
     _, silu, slope = gate(g)
     pair = jnp.concatenate([e * silu, e * p * slope], axis=0)
     hidden = eta * (silu * p)
     return fold(nn(two_terms(pair), keys)), fold(nn(two_terms(hidden), values))
 
 
-def curvature_terms(stack_ab, stack_c, units, keys, values, eta):
-    pre = fold(nt(stack_ab, keys))
+def curvature_terms(units, pre, cross, keys, values, eta):
+    pre = fold(pre)
     p, g = pre[:units], pre[units : 2 * units]
     tp, tg = pre[2 * units : 3 * units], pre[3 * units :]
-    both = fold(nt(stack_c, values))
+    both = fold(cross)
     e, te = eta * both[:units], eta * both[units:]
     sig, silu, slope = gate(g)
     bend = sig * (1.0 - sig) * (2.0 + g * (1.0 - 2.0 * sig))
@@ -73,31 +80,37 @@
     return jnp.concatenate([ref[0], ref[1]], axis=0), ref[2]
 
 
-def split_message(ref, tokens, width):
-    return (
-        ref[:tokens, :width].astype(BF16),
-        ref[:tokens, width:].astype(BF16),
-        ref[tokens : tokens + PAD, :tokens],
-    )
-
-
-def sweep(terms, stack_ab, stack_c, units, width, stores, acc):
+def sweep(terms, stack_ab, stack_c, units, stores, acc):
+    def load(kv, eta, start, size):
+        width = kv.shape[1] // 2
+        rows = pl.ds(start, size)
+        return kv[rows, :width], kv[rows, width:], eta[0:1, rows]
+
+    chunks = [
+        (kv, eta, start, min(CHUNK, kv.shape[0] - start))
+        for kv, eta in stores
+        for start in range(0, kv.shape[0], CHUNK)
+    ]
+    if len(chunks) <= PAIRED:
+        now = load(*chunks[0])
+        pre = forward(stack_ab, stack_c, *now[:2])
+        for i in range(len(chunks)):
+            if i + 1 < len(chunks):
+                later = load(*chunks[i + 1])
+                ahead = forward(stack_ab, stack_c, *later[:2])
+            ab, c = terms(units, *pre, *now)
+            acc = acc[0] + ab, acc[1] + c
+            if i + 1 < len(chunks):
+                now, pre = later, ahead
+        return acc
     for kv, eta in stores:
-        count, _, tokens = eta.shape
-
-        def step(i, acc, kv=kv, eta=eta, tokens=tokens):
-            start = i * tokens if isinstance(i, int) else pl.multiple_of(i * tokens, tokens)
-            rows = pl.ds(start, tokens)
-            ab, c = terms(
-                stack_ab, stack_c, units, kv[rows, :width], kv[rows, width:], eta[i, 0:1, :]
-            )
+
+        def step(i, acc, kv=kv, eta=eta):
+            now = load(kv, eta, pl.multiple_of(i * CHUNK, CHUNK), CHUNK)
+            ab, c = terms(units, *forward(stack_ab, stack_c, *now[:2]), *now)
             return acc[0] + ab, acc[1] + c
 
-        if count <= PAIRED:
-            for i in range(count):
-                acc = step(i, acc)
-        else:
-            acc = lax.fori_loop(0, count, step, acc)
+        acc = lax.fori_loop(0, kv.shape[0] // CHUNK, step, acc)
     return acc
 
 
@@ -116,25 +129,23 @@
         start_ref, base_ref = refs[0], refs[1]
         parts, (acc_ref, kv_ref, eta_ref) = refs[2 : 2 + messages], refs[2 + messages :]
     tokens = parts[0].shape[0] - PAD
+    for i, part in enumerate(parts):
+        rows = pl.ds(i * tokens, tokens)
+        kv_ref[rows, :] = part[:tokens, :].astype(BF16)
+        eta_ref[:, rows] = part[tokens:, :tokens]
     ab, c = flat(base_ref)
-    stack_ab, stack_c = two_terms(ab), two_terms(c)
-    acc = flat(start_ref)
-    for i, part in enumerate(parts):
-        keys, values, eta = split_message(part, tokens, width)
-        kv_ref[i * tokens : (i + 1) * tokens, :width] = keys
-        kv_ref[i * tokens : (i + 1) * tokens, width:] = values
-        eta_ref[i] = eta
-        more = ascent_terms(stack_ab, stack_c, units, keys, values, eta[0:1, :])
-        acc = acc[0] + more[0], acc[1] + more[1]
+    acc = sweep(
+        ascent_terms, two_terms(ab), two_terms(c), units, [(kv_ref, eta_ref)], flat(start_ref)
+    )
     acc_ref[0], acc_ref[1], acc_ref[2] = acc[0][:units], acc[0][units:], acc[1]
 
 
-def second_kernel(stored, units, width, *refs):
+def second_kernel(stored, units, *refs):
     start_ref = refs[0]
     stores = [(refs[1 + 2 * i], refs[2 + 2 * i]) for i in range(stored)]
     out_ref = refs[1 + 2 * stored]
     ab, c = flat(start_ref)
-    ab, c = sweep(ascent_terms, two_terms(ab), two_terms(c), units, width, stores, (ab, c))
+    ab, c = sweep(ascent_terms, two_terms(ab), two_terms(c), units, stores, (ab, c))
     out_ref[0], out_ref[1], out_ref[2] = ab[:units], ab[units:], c
 
 
@@ -179,7 +190,7 @@
         grad[2] = total[1][j * units : (j + 1) * units]
 
 
-def adjoint_kernel(stored, terms, units, width, parts, *refs):
+def adjoint_kernel(stored, terms, units, parts, *refs):
     place_ref, first_ref, second_ref = refs[:3]
     adjoints = refs[3 : 3 + terms]
     stores = [(refs[3 + terms + 2 * i], refs[4 + terms + 2 * i]) for i in range(stored)]
@@ -197,7 +208,7 @@
         ab, c = flat(bases.at[i])
         stack_ab = two_terms(jnp.concatenate([ab, u_ab], axis=0))
         stack_c = two_terms(jnp.concatenate([c, u_c], axis=0))
-        u_ab, u_c = sweep(curvature_terms, stack_ab, stack_c, units, width, stores, (u_ab, u_c))
+        u_ab, u_c = sweep(curvature_terms, stack_ab, stack_c, units, stores, (u_ab, u_c))
         held[0], held[1], held[2] = u_ab[:units], u_ab[units:], u_c
         return carry
 
@@ -228,14 +239,14 @@
     out_ref[...] = held[...].T
 
 
-def prepare_kernel(paired, *refs):
+def prepare_kernel(paired, divisor, *refs):
     place_ref, keys, values, rates, weights, first, second, column, held = refs
     half, width = keys.shape[0] // 2, keys.shape[1]
     units = column.shape[0]
     for at, message in ((0, first), (half, second)):
         message[:half, :width] = keys[at : at + half, :].astype(F32)
         message[:half, width:] = values[at : at + half, :].astype(F32)
-        message[half:, :half] = jnp.broadcast_to(rates[:, at : at + half], (PAD, half))
+        message[half:, :half] = jnp.broadcast_to(rates[:, at : at + half] / divisor, (PAD, half))
         message[half:, half:] = jnp.zeros((PAD, 2 * width - half), F32)
     held[...] = weights[...].T
     here = place_ref[0]
@@ -247,7 +258,7 @@
     return math.prod(x.shape) * x.dtype.itemsize
 
 
-def call(kernel, out_shape, cost, inputs, smem=(), scratch=()):
+def call(kernel, out_shape, cost, inputs, smem=(), scratch=(), grant=0):
     specs = [
         pl.BlockSpec(memory_space=pltpu.SMEM if i in smem else pltpu.VMEM)
         for i in range(len(inputs))
@@ -261,7 +272,7 @@
         out_specs=out_specs,
         scratch_shapes=list(scratch),
         compiler_params=pltpu.CompilerParams(
-            vmem_limit_bytes=min(60 * 1024 * 1024, held + 12 * 1024 * 1024)
+            vmem_limit_bytes=max(min(60 * MIB, held + 12 * MIB), grant * MIB)
         ),
         cost_estimate=pl.CostEstimate(flops=cost, bytes_accessed=0, transcendentals=0),
     )(*inputs)
@@ -290,12 +301,13 @@
 
     packed = jax.ShapeDtypeStruct((half + PAD, 2 * width), F32)
     *own, column = call(
-        lambda *refs: prepare_kernel(paired, *refs),
+        lambda *refs: prepare_kernel(paired, divisor, *refs),
         (packed, packed, column_block),
         1000,
-        [here, key_rows[0], value_rows[0], step_rates / divisor, fast_init],
+        [here, key_rows[0], value_rows[0], step_rates, fast_init],
         smem=(0,),
         scratch=[pltpu.VMEM((hidden, share), F32)],
+        grant=60,
     )
 
     def first(start, messages):
@@ -303,7 +315,7 @@
         outs = (
             block,
             jax.ShapeDtypeStruct((count * half, 2 * width), BF16),
-            jax.ShapeDtypeStruct((count, PAD, half), F32),
+            jax.ShapeDtypeStruct((PAD, count * half), F32),
         )
         columns = 0 if len(start) == 2 else len(start) - 1
         return call(
@@ -321,13 +333,16 @@
         x[0], y[1] = swap(own[0], 2), swap(own[1], 4)
         columns = [column] + [turn(column, k) for k in range(1, parts)]
         x[1], y[0] = swap(own[1], 2), swap(own[0], 4)
-        diagonal = [swap(x[0], 4), swap(y[1], 2)]
+        across = swap(x[0], 4)
+        diagonal = [across, swap(y[1], 2)]
         near = own + [swap(m, 1) for m in own]
+        initial, partial, *store_a = first([row] + columns, near)
+        x[1], y[0], partial = lax.optimization_barrier((x[1], y[0], partial))
         side = x + y
         side = side + [swap(m, 1) for m in side]
+        partial, *store_b = first([partial, initial], side)
+        *diagonal, partial = lax.optimization_barrier((*diagonal, partial))
         far = diagonal + [swap(m, 1) for m in diagonal]
-        initial, partial, *store_a = first([row] + columns, near)
-        partial, *store_b = first([partial, initial], side)
         middle, *store_c = first([partial, initial], far)
         stores = [*store_a, *store_b, *store_c]
     else:
@@ -335,12 +350,12 @@
         initial = jnp.stack(jnp.split(initial, 3, axis=1))
         every = lax.all_gather(jnp.stack(own), "seq", axis=0, tiled=True)
         kv = every[:, :half].astype(BF16).reshape(2 * shards * half, 2 * width)
-        stores = [kv, every[:, half:, :half]]
+        stores = [kv, every[:, half, :half].reshape(1, -1)]
         middle = None
 
     def ascend(base):
         return call(
-            lambda *refs: second_kernel(len(stores) // 2, units, width, *refs),
+            lambda *refs: second_kernel(len(stores) // 2, units, *refs),
             block,
             2 * 2 * 6 * shards * tokens * width * units,
             [base] + stores,
@@ -379,7 +394,7 @@
         adjoints = [lax.psum_scatter(grads, "seq", scatter_dimension=0, tiled=False)]
 
     rolled = call(
-        lambda *refs: adjoint_kernel(len(stores) // 2, len(adjoints), units, width, parts, *refs),
+        lambda *refs: adjoint_kernel(len(stores) // 2, len(adjoints), units, parts, *refs),
         (column_block,) * parts,
         2 * 2 * 24 * shards * tokens * width * units,
         [row, initial, middle] + adjoints + stores,
@@ -420,6 +435,7 @@
         P("batch", "seq", None),
         P("batch", None),
     )
+
     return jax.shard_map(
         body,
         mesh=mesh,

time: 109 us -> 96.2 us (0.88)
  Pallas kernels: 25 us -> 13.7 us
  waiting for transfers between devices: 40 us -> 46.2 us
  local copies, waits for them, and re-layouts: 8.64 us -> 5.62 us
  other arithmetic: 3.61 us -> 0.88 us
  starting transfers between devices: 30.7 us -> 28.6 us
    pallas_call x8, Pallas kernels: 25 us -> 13.7 us  [call(): pl.pallas_call(kernel, out_shape=out_shape, in_specs=specs, out_specs=out...]
    ppermute x6, waiting for transfers between devices: 4.16 us -> 14.6 us  [turn(): lax.ppermute(x, 'batch', [(i, (i + k) % parts) for i in range(parts)])]
    ppermute x29, waiting for transfers between devices: 35.8 us -> 31.6 us  [swap(): return lax.ppermute(x, 'seq', [(i, i ^ mask) for i in range(shards)])]
    ppermute x6, starting transfers between devices: 12.1 us -> 8.73 us  [turn(): lax.ppermute(x, 'batch', [(i, (i + k) % parts) for i in range(parts)])]
    unnamed x26 -> x18, local copies, waits for them, and re-layouts: 8.64 us -> 5.62 us
    concatenate x1, other arithmetic: 2.16 us -> 0.12 us  [body(): jnp.concatenate([queries[0].astype(F32), cotangent[0].astype(F32)], axis=1)]
    ppermute x29, starting transfers between devices: 18.5 us -> 19.8 us  [swap(): return lax.ppermute(x, 'seq', [(i, i ^ mask) for i in range(shards)])]
  transfers between devices with their start and end apart: 35 -> 35, of which waited for: 18 -> 23; matrix products, arithmetic and copies ran while one was open for 3% -> 1% of each run, Pallas kernels for 11% -> 5%
where the time goes in v2:
time: 96.2 us; the launch traced here: 95.8 us
  waiting for transfers between devices  46.2 us (48%)
  starting transfers between devices  28.6 us (30%)
  Pallas kernels  13.7 us (14%)
  local copies, waits for them, and re-layouts  5.62 us (6%)
    ppermute x29, waiting for transfers between devices, swap(): return lax.ppermute(x, 'seq', [(i, i ^ mask) for i in range(shards)])  31.6 us
    ppermute x29, starting transfers between devices, swap(): return lax.ppermute(x, 'seq', [(i, i ^ mask) for i in range(shards)])  19.8 us
    ppermute x6, waiting for transfers between devices, turn(): lax.ppermute(x, 'batch', [(i, (i + k) % parts) for i in range(parts)])  14.6 us
    pallas_call x8, Pallas kernels, call(): pl.pallas_call(kernel, out_shape=out_shape, in_specs=specs, out_specs=out...  13.7 us
    ppermute x6, starting transfers between devices, turn(): lax.ppermute(x, 'batch', [(i, (i + k) % parts) for i in range(parts)])  8.73 us
    unnamed x18, local copies, waits for them, and re-layouts  5.62 us
  transfers between devices with their start and end apart: 35, of which 23 were waited for; matrix products, arithmetic and copies ran while one was open for 1% of the time, Pallas kernels for 5%

profile of v2, /device:TPU:0, one launch (start us, length us, event | category | flops | bytes accessed | tf_op | source)
XLA Modules:
  0.0 95.8 jit_solution(11316914243730283770)
XLA Ops:
  0.6 2.2 %shard_map.77 = (f32[264,512]{1,0:T(8,128)}, f32[264,512]{1,0:T(8,128)}, f32[32,192]{1,0:T(8,128)}) custom-call(s32[1]{0:T(128)} %bitcast.refs_0_, bf16[512,256]{1,0:T(8,128)(2,1)} %bitcast.12, bf16[512,256]{1,0:T(8,128)(2,1)} %bitcast.13, f32[1,512]{1,0:T(1,128)} %refs_3_.1, f32[192,256]{1,0:T(8,128)} %refs_4_.1), custom_call_target="tpu_custom_call" | custom-call | flops 1000 | tf_op jit(solution)/shard_map/pallas_call | solution.py:268
  3.4 3.0 %collective-permute-start.4 = (f32[264,512]{1,0:T(8,128)}, f32[264,512]{1,0:T(8,128)S(1)}, u32[]{:S(2)}, u32[]{:S(2)}) collective-permute-start(f32[264,512]{1,0:T(8,128)} %get-tuple-element.34.refs_6_), channel_id=1, source_target_pairs={{0,8},{4,12},{8,0},{12,4},{16,24},{20,28},{24,16},{28,20},{1,9},{5... | collective-permute-start | bytes 1622024 | tf_op jit(solution)/shard_map/ppermute | solution.py:297
  6.4 1.5 %collective-permute-start.5 = (f32[264,512]{1,0:T(8,128)}, f32[264,512]{1,0:T(8,128)S(1)}, u32[]{:S(2)}, u32[]{:S(2)}) collective-permute-start(f32[264,512]{1,0:T(8,128)} %get-tuple-element.33.refs_5_), channel_id=1, source_target_pairs={{0,16},{4,20},{8,24},{12,28},{16,0},{20,4},{24,8},{28,12},{1,17},{... | collective-permute-start | bytes 1622024 | tf_op jit(solution)/shard_map/ppermute | solution.py:297
  7.9 1.6 %collective-permute-start.6 = (f32[32,192]{1,0:T(8,128)}, f32[32,192]{1,0:T(8,128)S(1)}, u32[]{:S(2)}, u32[]{:S(2)}) collective-permute-start(f32[32,192]{1,0:T(8,128)} %get-tuple-element.35.refs_1_), channel_id=1, source_target_pairs={{0,1},{1,2},{2,3},{3,0},{4,5},{5,6},{6,7},{7,4},{8,9},{9,10},{10,1... | collective-permute-start | bytes 73736 | tf_op jit(solution)/shard_map/ppermute | solution.py:300
  9.5 4.3 %collective-permute-done.6.refs_2_ = f32[32,192]{1,0:T(8,128)S(1)} collective-permute-done((f32[32,192]{1,0:T(8,128)}, f32[32,192]{1,0:T(8,128)S(1)}, u32[]{:S(2)}, u32[]{:S(2)}) %collective-permute-start.6) | collective-permute-done | bytes 24608 | tf_op jit(solution)/shard_map/ppermute | solution.py:300
  14.6 4.2 %collective-permute-done.7.refs_3_ = f32[32,192]{1,0:T(8,128)S(1)} collective-permute-done((f32[32,192]{1,0:T(8,128)}, f32[32,192]{1,0:T(8,128)S(1)}, u32[]{:S(2)}, u32[]{:S(2)}) %collective-permute-start.7) | collective-permute-done | bytes 24608 | tf_op jit(solution)/shard_map/ppermute | solution.py:300
  19.4 2.0 %collective-permute-start.8 = (f32[32,192]{1,0:T(8,128)}, f32[32,192]{1,0:T(8,128)S(1)}, u32[]{:S(2)}, u32[]{:S(2)}) collective-permute-start(f32[32,192]{1,0:T(8,128)} %get-tuple-element.35.refs_1_), channel_id=1, source_target_pairs={{0,3},{1,0},{2,1},{3,2},{4,7},{5,4},{6,5},{7,6},{8,11},{9,8},{10,9... | collective-permute-start | bytes 73736 | tf_op jit(solution)/shard_map/ppermute | solution.py:300
  21.5 2.1 %collective-permute-done.8.refs_4_ = f32[32,192]{1,0:T(8,128)S(1)} collective-permute-done((f32[32,192]{1,0:T(8,128)}, f32[32,192]{1,0:T(8,128)S(1)}, u32[]{:S(2)}, u32[]{:S(2)}) %collective-permute-start.8) | collective-permute-done | bytes 24608 | tf_op jit(solution)/shard_map/ppermute | solution.py:300
  30.8 4.2 %collective-permute-done.refs_2_ = f32[264,512]{1,0:T(8,128)S(1)} collective-permute-done((f32[264,512]{1,0:T(8,128)}, f32[264,512]{1,0:T(8,128)S(1)}, u32[]{:S(2)}, u32[]{:S(2)}) %collective-permute-start) | collective-permute-done | bytes 540704 | tf_op jit(solution)/shard_map/ppermute | solution.py:297
  36.0 1.2 %collective-permute-start.3 = (f32[264,512]{1,0:T(8,128)S(1)}, f32[264,512]{1,0:T(8,128)S(1)}, u32[]{:S(2)}, u32[]{:S(2)}) collective-permute-start(f32[264,512]{1,0:T(8,128)S(1)} %collective-permute-done.2.refs_5_), channel_id=1, source_target_pairs={{0,8},{4,12},{8,0},{12,4},{16,24},{20,28},{24,16},{28,20},{1,9},{5... | collective-permute-start | bytes 1622024 | tf_op jit(solution)/shard_map/ppermute | solution.py:297
  37.7 1.2 %shard_map.79 = (f32[3,32,256]{2,1,0:T(8,128)S(1)}, bf16[2048,512]{1,0:T(8,128)(2,1)S(1)}, f32[8,2048]{1,0:T(8,128)S(1)}) custom-call(f32[3,32,256]{2,1,0:T(8,128)S(1)} %get-tuple-element.37.refs_0_, f32[3,32,256]{2,1,0:T(8,128)S(1)} %get-tuple-element.38.refs_1_, f32[264,512]{1,0:T(8,128)S(1)} %collective-permute-done.refs_2_, ...), custom_call_target="tpu_custom_call" | custom-call | flops 402653184 | tf_op jit(solution)/shard_map/pallas_call | solution.py:268
  38.9 11.1 %collective-permute-done.1.refs_2_ = f32[264,512]{1,0:T(8,128)S(1)} collective-permute-done((f32[264,512]{1,0:T(8,128)S(1)}, f32[264,512]{1,0:T(8,128)S(1)}, u32[]{:S(2)}, u32[]{:S(2)}) %collective-permute-start.1) | collective-permute-done | bytes 540704 | tf_op jit(solution)/shard_map/ppermute | solution.py:297
  50.6 1.4 %collective-permute-done.15.refs_4_ = f32[264,512]{1,0:T(8,128)S(1)} collective-permute-done((f32[264,512]{1,0:T(8,128)S(1)}, f32[264,512]{1,0:T(8,128)S(1)}, u32[]{:S(2)}, u32[]{:S(2)}) %collective-permute-start.15) | collective-permute-done | bytes 540704 | tf_op jit(solution)/shard_map/ppermute | solution.py:297
  53.5 2.1 %shard_map.81.refs_0_ = f32[3,32,256]{2,1,0:T(8,128)S(1)} custom-call(f32[3,32,256]{2,1,0:T(8,128)S(1)} %get-tuple-element.45.refs_0_.refs_2_, bf16[1024,512]{1,0:T(8,128)(2,1)S(1)} %get-tuple-element.46.refs_1_.refs_7_, f32[8,1024]{1,0:T(8,128)S(1)} %get-tuple-element.47.refs_2_.refs_8_, bf16[2048,512]{1,0:T(8,128)(2,1)S(1)} %get-tuple-element.48.refs_3_.refs_9_, ...), custom_call_target="tpu_custom_call" | custom-call | flops 805306368 | tf_op jit(solution)/shard_map/pallas_call | solution.py:268
  55.6 1.6 %collective-permute-start.17 = (f32[3,32,256]{2,1,0:T(8,128)S(1)}, f32[3,32,256]{2,1,0:T(8,128)S(1)}, u32[]{:S(2)}, u32[]{:S(2)}) collective-permute-start(f32[3,32,256]{2,1,0:T(8,128)S(1)} %shard_map.81.refs_0_), channel_id=1, source_target_pairs={{0,8},{4,12},{8,0},{12,4},{16,24},{20,28},{24,16},{28,20},{1,9},{5... | collective-permute-start | bytes 294920 | tf_op jit(solution)/shard_map/ppermute | solution.py:297
  57.2 1.5 %collective-permute-start.18 = (f32[3,32,256]{2,1,0:T(8,128)S(1)}, f32[3,32,256]{2,1,0:T(8,128)S(1)}, u32[]{:S(2)}, u32[]{:S(2)}) collective-permute-start(f32[3,32,256]{2,1,0:T(8,128)S(1)} %shard_map.81.refs_0_), channel_id=1, source_target_pairs={{0,16},{4,20},{8,24},{12,28},{16,0},{20,4},{24,8},{28,12},{1,17},{... | collective-permute-start | bytes 294920 | tf_op jit(solution)/shard_map/ppermute | solution.py:297
  59.2 1.3 %collective-permute-done.17.refs_1_ = f32[3,32,256]{2,1,0:T(8,128)S(1)} collective-permute-done((f32[3,32,256]{2,1,0:T(8,128)S(1)}, f32[3,32,256]{2,1,0:T(8,128)S(1)}, u32[]{:S(2)}, u32[]{:S(2)}) %collective-permute-start.17) | collective-permute-done | bytes 98336 | tf_op jit(solution)/shard_map/ppermute | solution.py:297
  60.5 2.5 %collective-permute-done.18.refs_2_ = f32[3,32,256]{2,1,0:T(8,128)S(1)} collective-permute-done((f32[3,32,256]{2,1,0:T(8,128)S(1)}, f32[3,32,256]{2,1,0:T(8,128)S(1)}, u32[]{:S(2)}, u32[]{:S(2)}) %collective-permute-start.18) | collective-permute-done | bytes 98336 | tf_op jit(solution)/shard_map/ppermute | solution.py:297
  63.0 1.3 %collective-permute-done.19.refs_3_ = f32[3,32,256]{2,1,0:T(8,128)S(1)} collective-permute-done((f32[3,32,256]{2,1,0:T(8,128)S(1)}, f32[3,32,256]{2,1,0:T(8,128)S(1)}, u32[]{:S(2)}, u32[]{:S(2)}) %collective-permute-start.19) | collective-permute-done | bytes 98336 | tf_op jit(solution)/shard_map/ppermute | solution.py:297
  64.3 1.6 %shard_map.82 = (f32[512,256]{1,0:T(8,128)S(1)}, f32[512,256]{1,0:T(8,128)S(1)}, f32[3,32,256]{2,1,0:T(8,128)S(1)}, f32[3,32,256]{2,1,0:T(8,128)S(1)}, f32[3,32,...) custom-call(f32[3,32,256]{2,1,0:T(8,128)S(1)} %shard_map.81.refs_0_, f32[3,32,256]{2,1,0:T(8,128)S(1)} %collective-permute-done.17.refs_1_, ...), custom_call_target="tpu_custom_call" | custom-call | flops 939524096 | tf_op jit(solution)/shard_map/pallas_call | solution.py:268
  67.8 1.8 %collective-permute-start.24 = (f32[3,32,256]{2,1,0:T(8,128)S(1)}, f32[3,32,256]{2,1,0:T(8,128)S(1)}, u32[]{:S(2)}, u32[]{:S(2)}) collective-permute-start(f32[3,32,256]{2,1,0:T(8,128)S(1)} %get-tuple-element.59), channel_id=1, source_target_pairs={{0,24},{4,28},{8,16},{12,20},{16,8},{20,12},{24,0},{28,4},{1,25},{... | collective-permute-start | bytes 294920 | tf_op jit(solution)/shard_map/ppermute | solution.py:297
  70.3 1.2 %collective-permute-done.22.refs_4_ = f32[3,32,256]{2,1,0:T(8,128)S(1)} collective-permute-done((f32[3,32,256]{2,1,0:T(8,128)S(1)}, f32[3,32,256]{2,1,0:T(8,128)S(1)}, u32[]{:S(2)}, u32[]{:S(2)}) %collective-permute-start.22) | collective-permute-done | bytes 98336 | tf_op jit(solution)/shard_map/ppermute | solution.py:297
  72.2 1.7 %collective-permute-done.24.refs_6_ = f32[3,32,256]{2,1,0:T(8,128)S(1)} collective-permute-done((f32[3,32,256]{2,1,0:T(8,128)S(1)}, f32[3,32,256]{2,1,0:T(8,128)S(1)}, u32[]{:S(2)}, u32[]{:S(2)}) %collective-permute-start.24) | collective-permute-done | bytes 98336 | tf_op jit(solution)/shard_map/ppermute | solution.py:297
  73.9 4.4 %shard_map.83 = (f32[32,192]{1,0:T(8,128)S(1)}, f32[32,192]{1,0:T(8,128)S(1)}, f32[32,192]{1,0:T(8,128)S(1)}, f32[32,192]{1,0:T(8,128)S(1)}) custom-call(s32[1]{0:T(128)} %bitcast.3.refs_0_, f32[3,32,256]{2,1,0:T(8,128)S(1)} %get-tuple-element.38.refs_1_, f32[3,32,256]{2,1,0:T(8,128)S(1)} %get-tuple-element.45.refs_0_.refs_2_, ...), custom_call_target="tpu_custom_call" | custom-call | flops 3221225472 | tf_op jit(solution)/shard_map/pallas_call | solution.py:268
  78.4 4.3 %collective-permute-start.26 = (f32[32,192]{1,0:T(8,128)S(1)}, f32[32,192]{1,0:T(8,128)S(1)}, u32[]{:S(2)}, u32[]{:S(2)}) collective-permute-start(f32[32,192]{1,0:T(8,128)S(1)} %get-tuple-element.62), channel_id=1, source_target_pairs={{0,2},{1,3},{2,0},{3,1},{4,6},{5,7},{6,4},{7,5},{8,10},{9,11},{10,... | collective-permute-start | bytes 73736 | tf_op jit(solution)/shard_map/ppermute | solution.py:300
  82.6 1.5 %collective-permute-done.25 = f32[32,192]{1,0:T(8,128)S(1)} collective-permute-done((f32[32,192]{1,0:T(8,128)S(1)}, f32[32,192]{1,0:T(8,128)S(1)}, u32[]{:S(2)}, u32[]{:S(2)}) %collective-permute-start.25) | collective-permute-done | bytes 24608 | tf_op jit(solution)/shard_map/ppermute | solution.py:300
  85.2 1.4 %collective-permute-done.27 = f32[32,192]{1,0:T(8,128)S(1)} collective-permute-done((f32[32,192]{1,0:T(8,128)S(1)}, f32[32,192]{1,0:T(8,128)S(1)}, u32[]{:S(2)}, u32[]{:S(2)}) %collective-permute-start.27) | collective-permute-done | bytes 24608 | tf_op jit(solution)/shard_map/ppermute | solution.py:300
  86.6 1.2 %collective-permute-start.29 = (f32[32,192]{1,0:T(8,128)S(1)}, f32[32,192]{1,0:T(8,128)S(1)}, u32[]{:S(2)}, u32[]{:S(2)}) collective-permute-start(f32[32,192]{1,0:T(8,128)S(1)} %add_add_fusion.refs_1_), channel_id=1, source_target_pairs={{0,8},{4,12},{8,0},{12,4},{16,24},{20,28},{24,16},{28,20},{1,9},{5... | collective-permute-start | bytes 73736 | tf_op jit(solution)/shard_map/ppermute | solution.py:297
  87.7 1.2 %collective-permute-start.31 = (f32[32,192]{1,0:T(8,128)S(1)}, f32[32,192]{1,0:T(8,128)S(1)}, u32[]{:S(2)}, u32[]{:S(2)}) collective-permute-start(f32[32,192]{1,0:T(8,128)S(1)} %add_add_fusion.refs_1_), channel_id=1, source_target_pairs={{0,16},{4,20},{8,24},{12,28},{16,0},{20,4},{24,8},{28,12},{1,17},{... | collective-permute-start | bytes 73736 | tf_op jit(solution)/shard_map/ppermute | solution.py:297
  88.9 1.2 %collective-permute-start.33 = (f32[32,192]{1,0:T(8,128)S(1)}, f32[32,192]{1,0:T(8,128)S(1)}, u32[]{:S(2)}, u32[]{:S(2)}) collective-permute-start(f32[32,192]{1,0:T(8,128)S(1)} %add_add_fusion.refs_1_), channel_id=1, source_target_pairs={{0,24},{4,28},{8,16},{12,20},{16,8},{20,12},{24,0},{28,4},{1,25},{... | collective-permute-start | bytes 73736 | tf_op jit(solution)/shard_map/ppermute | solution.py:297
  91.6 2.1 %collective-permute-done.33.refs_7_ = f32[32,192]{1,0:T(8,128)S(1)} collective-permute-done((f32[32,192]{1,0:T(8,128)S(1)}, f32[32,192]{1,0:T(8,128)S(1)}, u32[]{:S(2)}, u32[]{:S(2)}) %collective-permute-start.33) | collective-permute-done | bytes 24608 | tf_op jit(solution)/shard_map/ppermute | solution.py:297
  93.8 1.2 %collective-permute-done.34.refs_8_ = f32[32,192]{1,0:T(8,128)S(1)} collective-permute-done((f32[32,192]{1,0:T(8,128)S(1)}, f32[32,192]{1,0:T(8,128)S(1)}, u32[]{:S(2)}, u32[]{:S(2)}) %collective-permute-start.34) | collective-permute-done | bytes 24608 | tf_op jit(solution)/shard_map/ppermute | solution.py:297
  (67 shorter events, 19.8 us)
Async XLA Ops:
  2.9 21.8 %collective-permute-start.10 = (f32[264,512]{1,0:T(8,128)}, f32[264,512]{1,0:T(8,128)S(1)}, u32[]{:S(2)}, u32[]{:S(2)}) collective-permute-start(f32[264,512]{1,0:T(8,128)} %get-tuple-element.34.refs_6_), channel_id=1, source_target_pairs={{0,4},{4,0},{8,12},{12,8},{16,20},{20,16},{24,28},{28,24},{1,5},{5... | collective-permute-start | bytes 1622024 | tf_op jit(solution)/shard_map/ppermute | solution.py:297
  3.4 21.7 %collective-permute-start.9 = (f32[264,512]{1,0:T(8,128)}, f32[264,512]{1,0:T(8,128)S(1)}, u32[]{:S(2)}, u32[]{:S(2)}) collective-permute-start(f32[264,512]{1,0:T(8,128)} %get-tuple-element.33.refs_5_), channel_id=1, source_target_pairs={{0,4},{4,0},{8,12},{12,8},{16,20},{20,16},{24,28},{28,24},{1,5},{5... | collective-permute-start | bytes 1622024 | tf_op jit(solution)/shard_map/ppermute | solution.py:297
  3.4 26.8 %collective-permute-start.4 = (f32[264,512]{1,0:T(8,128)}, f32[264,512]{1,0:T(8,128)S(1)}, u32[]{:S(2)}, u32[]{:S(2)}) collective-permute-start(f32[264,512]{1,0:T(8,128)} %get-tuple-element.34.refs_6_), channel_id=1, source_target_pairs={{0,8},{4,12},{8,0},{12,4},{16,24},{20,28},{24,16},{28,20},{1,9},{5... | collective-permute-start | bytes 1622024 | tf_op jit(solution)/shard_map/ppermute | solution.py:297
  6.4 23.8 %collective-permute-start.5 = (f32[264,512]{1,0:T(8,128)}, f32[264,512]{1,0:T(8,128)S(1)}, u32[]{:S(2)}, u32[]{:S(2)}) collective-permute-start(f32[264,512]{1,0:T(8,128)} %get-tuple-element.33.refs_5_), channel_id=1, source_target_pairs={{0,16},{4,20},{8,24},{12,28},{16,0},{20,4},{24,8},{28,12},{1,17},{... | collective-permute-start | bytes 1622024 | tf_op jit(solution)/shard_map/ppermute | solution.py:297
  7.9 5.9 %collective-permute-start.6 = (f32[32,192]{1,0:T(8,128)}, f32[32,192]{1,0:T(8,128)S(1)}, u32[]{:S(2)}, u32[]{:S(2)}) collective-permute-start(f32[32,192]{1,0:T(8,128)} %get-tuple-element.35.refs_1_), channel_id=1, source_target_pairs={{0,1},{1,2},{2,3},{3,0},{4,5},{5,6},{6,7},{7,4},{8,9},{9,10},{10,1... | collective-permute-start | bytes 73736 | tf_op jit(solution)/shard_map/ppermute | solution.py:300
  13.8 5.0 %collective-permute-start.7 = (f32[32,192]{1,0:T(8,128)}, f32[32,192]{1,0:T(8,128)S(1)}, u32[]{:S(2)}, u32[]{:S(2)}) collective-permute-start(f32[32,192]{1,0:T(8,128)} %get-tuple-element.35.refs_1_), channel_id=1, source_target_pairs={{0,2},{1,3},{2,0},{3,1},{4,6},{5,7},{6,4},{7,5},{8,10},{9,11},{10,... | collective-permute-start | bytes 73736 | tf_op jit(solution)/shard_map/ppermute | solution.py:300
  19.4 4.1 %collective-permute-start.8 = (f32[32,192]{1,0:T(8,128)}, f32[32,192]{1,0:T(8,128)S(1)}, u32[]{:S(2)}, u32[]{:S(2)}) collective-permute-start(f32[32,192]{1,0:T(8,128)} %get-tuple-element.35.refs_1_), channel_id=1, source_target_pairs={{0,3},{1,0},{2,1},{3,2},{4,7},{5,4},{6,5},{7,6},{8,11},{9,8},{10,9... | collective-permute-start | bytes 73736 | tf_op jit(solution)/shard_map/ppermute | solution.py:300
  24.2 10.8 %collective-permute-start = (f32[264,512]{1,0:T(8,128)}, f32[264,512]{1,0:T(8,128)S(1)}, u32[]{:S(2)}, u32[]{:S(2)}) collective-permute-start(f32[264,512]{1,0:T(8,128)} %get-tuple-element.33.refs_5_), channel_id=1, source_target_pairs={{0,8},{4,12},{8,0},{12,4},{16,24},{20,28},{24,16},{28,20},{1,9},{5... | collective-permute-start | bytes 1622024 | tf_op jit(solution)/shard_map/ppermute | solution.py:297
  24.7 10.5 %collective-permute-start.2 = (f32[264,512]{1,0:T(8,128)}, f32[264,512]{1,0:T(8,128)S(1)}, u32[]{:S(2)}, u32[]{:S(2)}) collective-permute-start(f32[264,512]{1,0:T(8,128)} %get-tuple-element.34.refs_6_), channel_id=1, source_target_pairs={{0,16},{4,20},{8,24},{12,28},{16,0},{20,4},{24,8},{28,12},{1,17},{... | collective-permute-start | bytes 1622024 | tf_op jit(solution)/shard_map/ppermute | solution.py:297
  30.2 5.8 %collective-permute-start.12 = (f32[264,512]{1,0:T(8,128)S(1)}, f32[264,512]{1,0:T(8,128)S(1)}, u32[]{:S(2)}, u32[]{:S(2)}) collective-permute-start(f32[264,512]{1,0:T(8,128)S(1)} %collective-permute-done.4.refs_3_), channel_id=1, source_target_pairs={{0,4},{4,0},{8,12},{12,8},{16,20},{20,16},{24,28},{28,24},{1,5},{5... | collective-permute-start | bytes 1622024 | tf_op jit(solution)/shard_map/ppermute | solution.py:297
  30.3 7.1 %collective-permute-start.13 = (f32[264,512]{1,0:T(8,128)S(1)}, f32[264,512]{1,0:T(8,128)S(1)}, u32[]{:S(2)}, u32[]{:S(2)}) collective-permute-start(f32[264,512]{1,0:T(8,128)S(1)} %collective-permute-done.5.refs_4_), channel_id=1, source_target_pairs={{0,4},{4,0},{8,12},{12,8},{16,20},{20,16},{24,28},{28,24},{1,5},{5... | collective-permute-start | bytes 1622024 | tf_op jit(solution)/shard_map/ppermute | solution.py:297
  35.0 2.5 %collective-permute-start.11 = (f32[264,512]{1,0:T(8,128)S(1)}, f32[264,512]{1,0:T(8,128)S(1)}, u32[]{:S(2)}, u32[]{:S(2)}) collective-permute-start(f32[264,512]{1,0:T(8,128)S(1)} %collective-permute-done.refs_2_), channel_id=1, source_target_pairs={{0,4},{4,0},{8,12},{12,8},{16,20},{20,16},{24,28},{28,24},{1,5},{5... | collective-permute-start | bytes 1622024 | tf_op jit(solution)/shard_map/ppermute | solution.py:297
  35.2 2.4 %collective-permute-start.14 = (f32[264,512]{1,0:T(8,128)S(1)}, f32[264,512]{1,0:T(8,128)S(1)}, u32[]{:S(2)}, u32[]{:S(2)}) collective-permute-start(f32[264,512]{1,0:T(8,128)S(1)} %collective-permute-done.2.refs_5_), channel_id=1, source_target_pairs={{0,4},{4,0},{8,12},{12,8},{16,20},{20,16},{24,28},{28,24},{1,5},{5... | collective-permute-start | bytes 1622024 | tf_op jit(solution)/shard_map/ppermute | solution.py:297
  35.5 14.4 %collective-permute-start.1 = (f32[264,512]{1,0:T(8,128)S(1)}, f32[264,512]{1,0:T(8,128)S(1)}, u32[]{:S(2)}, u32[]{:S(2)}) collective-permute-start(f32[264,512]{1,0:T(8,128)S(1)} %collective-permute-done.refs_2_), channel_id=1, source_target_pairs={{0,16},{4,20},{8,24},{12,28},{16,0},{20,4},{24,8},{28,12},{1,17},{... | collective-permute-start | bytes 1622024 | tf_op jit(solution)/shard_map/ppermute | solution.py:297
  36.0 14.1 %collective-permute-start.3 = (f32[264,512]{1,0:T(8,128)S(1)}, f32[264,512]{1,0:T(8,128)S(1)}, u32[]{:S(2)}, u32[]{:S(2)}) collective-permute-start(f32[264,512]{1,0:T(8,128)S(1)} %collective-permute-done.2.refs_5_), channel_id=1, source_target_pairs={{0,8},{4,12},{8,0},{12,4},{16,24},{20,28},{24,16},{28,20},{1,9},{5... | collective-permute-start | bytes 1622024 | tf_op jit(solution)/shard_map/ppermute | solution.py:297
  37.4 21.8 %collective-permute-start.20 = (f32[512,512]{1,0:T(8,128)S(1)}, f32[512,512]{1,0:T(8,128)S(1)}, u32[]{:S(2)}, u32[]{:S(2)}) collective-permute-start(f32[512,512]{1,0:T(8,128)S(1)} %maximum_convert_fusion), channel_id=1, source_target_pairs={{0,4},{4,0},{8,12},{12,8},{16,20},{20,16},{24,28},{28,24},{1,5},{5... | collective-permute-start | bytes 3145736 | tf_op jit(solution)/shard_map/ppermute | solution.py:297
  50.1 2.7 %collective-permute-start.16 = (f32[264,512]{1,0:T(8,128)S(1)}, f32[264,512]{1,0:T(8,128)S(1)}, u32[]{:S(2)}, u32[]{:S(2)}) collective-permute-start(f32[264,512]{1,0:T(8,128)S(1)} %collective-permute-done.3.refs_3_), channel_id=1, source_target_pairs={{0,4},{4,0},{8,12},{12,8},{16,20},{20,16},{24,28},{28,24},{1,5},{5... | collective-permute-start | bytes 1622024 | tf_op jit(solution)/shard_map/ppermute | solution.py:297
  55.6 4.9 %collective-permute-start.17 = (f32[3,32,256]{2,1,0:T(8,128)S(1)}, f32[3,32,256]{2,1,0:T(8,128)S(1)}, u32[]{:S(2)}, u32[]{:S(2)}) collective-permute-start(f32[3,32,256]{2,1,0:T(8,128)S(1)} %shard_map.81.refs_0_), channel_id=1, source_target_pairs={{0,8},{4,12},{8,0},{12,4},{16,24},{20,28},{24,16},{28,20},{1,9},{5... | collective-permute-start | bytes 294920 | tf_op jit(solution)/shard_map/ppermute | solution.py:297
  57.2 5.8 %collective-permute-start.18 = (f32[3,32,256]{2,1,0:T(8,128)S(1)}, f32[3,32,256]{2,1,0:T(8,128)S(1)}, u32[]{:S(2)}, u32[]{:S(2)}) collective-permute-start(f32[3,32,256]{2,1,0:T(8,128)S(1)} %shard_map.81.refs_0_), channel_id=1, source_target_pairs={{0,16},{4,20},{8,24},{12,28},{16,0},{20,4},{24,8},{28,12},{1,17},{... | collective-permute-start | bytes 294920 | tf_op jit(solution)/shard_map/ppermute | solution.py:297
  58.8 5.5 %collective-permute-start.19 = (f32[3,32,256]{2,1,0:T(8,128)S(1)}, f32[3,32,256]{2,1,0:T(8,128)S(1)}, u32[]{:S(2)}, u32[]{:S(2)}) collective-permute-start(f32[3,32,256]{2,1,0:T(8,128)S(1)} %shard_map.81.refs_0_), channel_id=1, source_target_pairs={{0,24},{4,28},{8,16},{12,20},{16,8},{20,12},{24,0},{28,4},{1,25},{... | collective-permute-start | bytes 294920 | tf_op jit(solution)/shard_map/ppermute | solution.py:297
  65.9 3.6 %collective-permute-start.21 = (f32[512,256]{1,0:T(8,128)S(1)}, f32[512,256]{1,0:T(8,128)S(1)}, u32[]{:S(2)}, u32[]{:S(2)}) collective-permute-start(f32[512,256]{1,0:T(8,128)S(1)} %get-tuple-element.53), channel_id=1, source_target_pairs={{0,4},{4,0},{8,12},{12,8},{16,20},{20,16},{24,28},{28,24},{1,5},{5... | collective-permute-start | bytes 1572872 | tf_op jit(solution)/shard_map/ppermute | solution.py:297
  66.0 5.5 %collective-permute-start.22 = (f32[3,32,256]{2,1,0:T(8,128)S(1)}, f32[3,32,256]{2,1,0:T(8,128)S(1)}, u32[]{:S(2)}, u32[]{:S(2)}) collective-permute-start(f32[3,32,256]{2,1,0:T(8,128)S(1)} %get-tuple-element.57), channel_id=1, source_target_pairs={{0,8},{4,12},{8,0},{12,4},{16,24},{20,28},{24,16},{28,20},{1,9},{5... | collective-permute-start | bytes 294920 | tf_op jit(solution)/shard_map/ppermute | solution.py:297
  66.9 5.3 %collective-permute-start.23 = (f32[3,32,256]{2,1,0:T(8,128)S(1)}, f32[3,32,256]{2,1,0:T(8,128)S(1)}, u32[]{:S(2)}, u32[]{:S(2)}) collective-permute-start(f32[3,32,256]{2,1,0:T(8,128)S(1)} %get-tuple-element.58), channel_id=1, source_target_pairs={{0,16},{4,20},{8,24},{12,28},{16,0},{20,4},{24,8},{28,12},{1,17},{... | collective-permute-start | bytes 294920 | tf_op jit(solution)/shard_map/ppermute | solution.py:297
  67.8 6.2 %collective-permute-start.24 = (f32[3,32,256]{2,1,0:T(8,128)S(1)}, f32[3,32,256]{2,1,0:T(8,128)S(1)}, u32[]{:S(2)}, u32[]{:S(2)}) collective-permute-start(f32[3,32,256]{2,1,0:T(8,128)S(1)} %get-tuple-element.59), channel_id=1, source_target_pairs={{0,24},{4,28},{8,16},{12,20},{16,8},{20,12},{24,0},{28,4},{1,25},{... | collective-permute-start | bytes 294920 | tf_op jit(solution)/shard_map/ppermute | solution.py:297
  78.3 5.9 %collective-permute-start.25 = (f32[32,192]{1,0:T(8,128)S(1)}, f32[32,192]{1,0:T(8,128)S(1)}, u32[]{:S(2)}, u32[]{:S(2)}) collective-permute-start(f32[32,192]{1,0:T(8,128)S(1)} %get-tuple-element.61), channel_id=1, source_target_pairs={{0,1},{1,2},{2,3},{3,0},{4,5},{5,6},{6,7},{7,4},{8,9},{9,10},{10,1... | collective-permute-start | bytes 73736 | tf_op jit(solution)/shard_map/ppermute | solution.py:300
  78.4 6.8 %collective-permute-start.26 = (f32[32,192]{1,0:T(8,128)S(1)}, f32[32,192]{1,0:T(8,128)S(1)}, u32[]{:S(2)}, u32[]{:S(2)}) collective-permute-start(f32[32,192]{1,0:T(8,128)S(1)} %get-tuple-element.62), channel_id=1, source_target_pairs={{0,2},{1,3},{2,0},{3,1},{4,6},{5,7},{6,4},{7,5},{8,10},{9,11},{10,... | collective-permute-start | bytes 73736 | tf_op jit(solution)/shard_map/ppermute | solution.py:300
  82.6 3.9 %collective-permute-start.27 = (f32[32,192]{1,0:T(8,128)S(1)}, f32[32,192]{1,0:T(8,128)S(1)}, u32[]{:S(2)}, u32[]{:S(2)}) collective-permute-start(f32[32,192]{1,0:T(8,128)S(1)} %get-tuple-element.63), channel_id=1, source_target_pairs={{0,3},{1,0},{2,1},{3,2},{4,7},{5,4},{6,5},{7,6},{8,11},{9,8},{10,9... | collective-permute-start | bytes 73736 | tf_op jit(solution)/shard_map/ppermute | solution.py:300
  86.6 4.0 %collective-permute-start.29 = (f32[32,192]{1,0:T(8,128)S(1)}, f32[32,192]{1,0:T(8,128)S(1)}, u32[]{:S(2)}, u32[]{:S(2)}) collective-permute-start(f32[32,192]{1,0:T(8,128)S(1)} %add_add_fusion.refs_1_), channel_id=1, source_target_pairs={{0,8},{4,12},{8,0},{12,4},{16,24},{20,28},{24,16},{28,20},{1,9},{5... | collective-permute-start | bytes 73736 | tf_op jit(solution)/shard_map/ppermute | solution.py:297
  87.7 3.9 %collective-permute-start.31 = (f32[32,192]{1,0:T(8,128)S(1)}, f32[32,192]{1,0:T(8,128)S(1)}, u32[]{:S(2)}, u32[]{:S(2)}) collective-permute-start(f32[32,192]{1,0:T(8,128)S(1)} %add_add_fusion.refs_1_), channel_id=1, source_target_pairs={{0,16},{4,20},{8,24},{12,28},{16,0},{20,4},{24,8},{28,12},{1,17},{... | collective-permute-start | bytes 73736 | tf_op jit(solution)/shard_map/ppermute | solution.py:297
  88.9 4.8 %collective-permute-start.33 = (f32[32,192]{1,0:T(8,128)S(1)}, f32[32,192]{1,0:T(8,128)S(1)}, u32[]{:S(2)}, u32[]{:S(2)}) collective-permute-start(f32[32,192]{1,0:T(8,128)S(1)} %add_add_fusion.refs_1_), channel_id=1, source_target_pairs={{0,24},{4,28},{8,16},{12,20},{16,8},{20,12},{24,0},{28,4},{1,25},{... | collective-permute-start | bytes 73736 | tf_op jit(solution)/shard_map/ppermute | solution.py:297
  90.1 3.6 %collective-permute-start.28 = (f32[32,192]{1,0:T(8,128)S(1)}, f32[32,192]{1,0:T(8,128)S(1)}, u32[]{:S(2)}, u32[]{:S(2)}) collective-permute-start(f32[32,192]{1,0:T(8,128)S(1)} %add_add_fusion.refs_1_), channel_id=1, source_target_pairs={{0,4},{4,0},{8,12},{12,8},{16,20},{20,16},{24,28},{28,24},{1,5},{5... | collective-permute-start | bytes 73736 | tf_op jit(solution)/shard_map/ppermute | solution.py:297
  90.5 3.2 %collective-permute-start.30 = (f32[32,192]{1,0:T(8,128)S(1)}, f32[32,192]{1,0:T(8,128)S(1)}, u32[]{:S(2)}, u32[]{:S(2)}) collective-permute-start(f32[32,192]{1,0:T(8,128)S(1)} %collective-permute-done.29.refs_3_), channel_id=1, source_target_pairs={{0,4},{4,0},{8,12},{12,8},{16,20},{20,16},{24,28},{28,24},{1,5},{5... | collective-permute-start | bytes 73736 | tf_op jit(solution)/shard_map/ppermute | solution.py:297
  (12 other events, 55.3 us)

commit v3 on v2

--- a/solution.py
+++ b/solution.py
@@ -10,7 +10,6 @@
 
 F32 = jnp.float32
 BF16 = jnp.bfloat16
-PAD = 8
 PAIRED = 8
 CHUNK = 1024
 MIB = 1024 * 1024
@@ -84,7 +83,7 @@
     def load(kv, eta, start, size):
         width = kv.shape[1] // 2
         rows = pl.ds(start, size)
-        return kv[rows, :width], kv[rows, width:], eta[0:1, rows]
+        return kv[rows, :width].astype(BF16), kv[rows, width:].astype(BF16), eta[0:1, rows]
 
     chunks = [
         (kv, eta, start, min(CHUNK, kv.shape[0] - start))
@@ -117,7 +116,7 @@
 def first_kernel(messages, columns, units, width, *refs):
     if columns:
         place_ref, pieces, refs = refs[0], refs[1 : 1 + columns], refs[1 + columns :]
-        parts, (base_ref, acc_ref, kv_ref, eta_ref, blocks) = refs[:messages], refs[messages:]
+        base_ref, acc_ref, kv_ref, eta_ref, blocks = refs[-5:]
         mine = place_ref[0]
         for k, piece in enumerate(pieces):
             blocks[lax.rem(mine - k + columns, columns)] = piece[...]
@@ -127,12 +126,15 @@
         start_ref = base_ref
     else:
         start_ref, base_ref = refs[0], refs[1]
-        parts, (acc_ref, kv_ref, eta_ref) = refs[2 : 2 + messages], refs[2 + messages :]
-    tokens = parts[0].shape[0] - PAD
-    for i, part in enumerate(parts):
-        rows = pl.ds(i * tokens, tokens)
-        kv_ref[rows, :] = part[:tokens, :].astype(BF16)
-        eta_ref[:, rows] = part[tokens:, :tokens]
+        acc_ref, kv_ref, eta_ref = refs[-3:]
+        refs = refs[2:]
+    for i, part in enumerate(refs[:messages]):
+        size = part.shape[0]
+        kv_ref[i * size : (i + 1) * size, :] = part[...].astype(BF16)
+    for i in range(messages // 2):
+        rates = refs[messages + i]
+        size = rates.shape[1]
+        eta_ref[:, i * size : (i + 1) * size] = rates[...]
     ab, c = flat(base_ref)
     acc = sweep(
         ascent_terms, two_terms(ab), two_terms(c), units, [(kv_ref, eta_ref)], flat(start_ref)
@@ -240,14 +242,26 @@
 
 
 def prepare_kernel(paired, divisor, *refs):
-    place_ref, keys, values, rates, weights, first, second, column, held = refs
+    place_ref, *sources = refs[:5]
+    first, second, eta, column = refs[5:9]
+    keys, values, rates, weights, held, sems = refs[9:]
+    copies = [
+        pltpu.make_async_copy(source, target, sems.at[i])
+        for i, (source, target) in enumerate(zip(sources, (keys, values, rates, weights)))
+    ]
+    for copy in copies:
+        copy.start()
     half, width = keys.shape[0] // 2, keys.shape[1]
     units = column.shape[0]
-    for at, message in ((0, first), (half, second)):
-        message[:half, :width] = keys[at : at + half, :].astype(F32)
-        message[:half, width:] = values[at : at + half, :].astype(F32)
-        message[half:, :half] = jnp.broadcast_to(rates[:, at : at + half] / divisor, (PAD, half))
-        message[half:, half:] = jnp.zeros((PAD, 2 * width - half), F32)
+    copies[0].wait()
+    first[:, :width] = keys[:half, :].astype(F32)
+    second[:, :width] = keys[half:, :].astype(F32)
+    copies[1].wait()
+    first[:, width:] = values[:half, :].astype(F32)
+    second[:, width:] = values[half:, :].astype(F32)
+    copies[2].wait()
+    eta[...] = rates[...] / divisor
+    copies[3].wait()
     held[...] = weights[...].T
     here = place_ref[0]
     group = (here & 1) * (PAIRED // 2) + (here >> 1) if paired else here
@@ -258,9 +272,11 @@
     return math.prod(x.shape) * x.dtype.itemsize
 
 
-def call(kernel, out_shape, cost, inputs, smem=(), scratch=(), grant=0):
+def call(kernel, out_shape, cost, inputs, smem=(), scratch=(), far=(), grant=0):
     specs = [
-        pl.BlockSpec(memory_space=pltpu.SMEM if i in smem else pltpu.VMEM)
+        pl.BlockSpec(
+            memory_space=pltpu.SMEM if i in smem else pltpu.HBM if i in far else pltpu.VMEM
+        )
         for i in range(len(inputs))
     ]
     out_specs = jax.tree.map(lambda _: pl.BlockSpec(memory_space=pltpu.VMEM), out_shape)
@@ -299,30 +315,38 @@
     def turn(x, k):
         return lax.ppermute(x, "batch", [(i, (i + k) % parts) for i in range(parts)])
 
-    packed = jax.ShapeDtypeStruct((half + PAD, 2 * width), F32)
-    *own, column = call(
+    packed = jax.ShapeDtypeStruct((half, 2 * width), F32)
+    *own, eta, column = call(
         lambda *refs: prepare_kernel(paired, divisor, *refs),
-        (packed, packed, column_block),
+        (packed, packed, jax.ShapeDtypeStruct((1, tokens), F32), column_block),
         1000,
         [here, key_rows[0], value_rows[0], step_rates, fast_init],
         smem=(0,),
-        scratch=[pltpu.VMEM((hidden, share), F32)],
+        far=(1, 2, 3, 4),
         grant=60,
-    )
-
-    def first(start, messages):
+        scratch=[
+            pltpu.VMEM((tokens, width), BF16),
+            pltpu.VMEM((tokens, width), BF16),
+            pltpu.VMEM((1, tokens), F32),
+            pltpu.VMEM((share, hidden), F32),
+            pltpu.VMEM((hidden, share), F32),
+            pltpu.SemaphoreType.DMA((4,)),
+        ],
+    )
+
+    def first(start, messages, rates):
         count = len(messages)
         outs = (
             block,
             jax.ShapeDtypeStruct((count * half, 2 * width), BF16),
-            jax.ShapeDtypeStruct((PAD, count * half), F32),
+            jax.ShapeDtypeStruct((1, count * half), F32),
         )
         columns = 0 if len(start) == 2 else len(start) - 1
         return call(
             lambda *refs: first_kernel(count, columns, units, width, *refs),
             (block,) * (columns > 0) + outs,
             2 * 2 * 6 * count * half * width * units,
-            start + messages,
+            start + messages + rates,
             smem=(0,) if columns else (),
             scratch=[pltpu.VMEM((parts, units, share), F32)] if columns else (),
         )
@@ -331,26 +355,28 @@
         x = [None, None]
         y = [None, None]
         x[0], y[1] = swap(own[0], 2), swap(own[1], 4)
+        x[1], y[0] = swap(own[1], 2), swap(own[0], 4)
         columns = [column] + [turn(column, k) for k in range(1, parts)]
-        x[1], y[0] = swap(own[1], 2), swap(own[0], 4)
+        rates = [eta] + [swap(eta, mask) for mask in range(1, PAIRED)]
         across = swap(x[0], 4)
         diagonal = [across, swap(y[1], 2)]
         near = own + [swap(m, 1) for m in own]
-        initial, partial, *store_a = first([row] + columns, near)
+        initial, partial, *store_a = first([row] + columns, near, rates[0:2])
         x[1], y[0], partial = lax.optimization_barrier((x[1], y[0], partial))
         side = x + y
         side = side + [swap(m, 1) for m in side]
-        partial, *store_b = first([partial, initial], side)
+        order = [rates[mask] for mask in (2, 4, 3, 5)]
+        partial, *store_b = first([partial, initial], side, order)
         *diagonal, partial = lax.optimization_barrier((*diagonal, partial))
         far = diagonal + [swap(m, 1) for m in diagonal]
-        middle, *store_c = first([partial, initial], far)
+        middle, *store_c = first([partial, initial], far, rates[6:8])
         stores = [*store_a, *store_b, *store_c]
     else:
         initial = lax.all_gather(column, "batch", axis=1, tiled=True)
         initial = jnp.stack(jnp.split(initial, 3, axis=1))
         every = lax.all_gather(jnp.stack(own), "seq", axis=0, tiled=True)
-        kv = every[:, :half].astype(BF16).reshape(2 * shards * half, 2 * width)
-        stores = [kv, every[:, half, :half].reshape(1, -1)]
+        every = every.reshape(2 * shards * half, 2 * width)
+        stores = [every, lax.all_gather(eta, "seq", axis=1, tiled=True)]
         middle = None
 
     def ascend(base):
@@ -369,7 +395,8 @@
     if paired:
         pair = jnp.concatenate([queries[0].astype(F32), cotangent[0].astype(F32)], axis=1)
         other = swap(pair, 1)
-        weights = [last, swap(last, 2), swap(last, 4), swap(last, 6)]
+        corner = swap(last, 6)
+        weights = [last, swap(last, 2), swap(last, 4), corner]
         part = jax.ShapeDtypeStruct((tokens, width), F32)
         kept, given, *grads = call(
             lambda *refs: outer_kernel(4, False, units, width, *refs),
@@ -377,7 +404,8 @@
             cost,
             weights + [queries[0], cotangent[0], other],
         )
-        adjoints = [grads[0], swap(grads[1], 2), swap(grads[2], 4), swap(grads[3], 6)]
+        corner = swap(grads[3], 6)
+        adjoints = [grads[0], swap(grads[1], 2), swap(grads[2], 4), corner]
         result = (kept + swap(given, 1)).astype(BF16)
         result, adjoints[0] = lax.optimization_barrier((result, adjoints[0]))
     else:
@@ -409,7 +437,8 @@
     for k in range(1, parts):
         summed = summed + turn(rolled[k], k)
     if paired:
-        ring = [summed] + [swap(summed, mask) for mask in (2, 4, 6)]
+        corner = swap(summed, 6)
+        ring = [summed, swap(summed, 2), swap(summed, 4), corner]
         pieces = []
         for piece in ring:
             pieces += [piece, swap(piece, 1)]

time: 96.2 us -> 112 us (1.16)
  waiting for transfers between devices: 46.2 us -> 59.5 us
  starting transfers between devices: 28.6 us -> 32.8 us
  local copies, waits for them, and re-layouts: 5.62 us -> 3.57 us
    ppermute x29 -> x36, waiting for transfers between devices: 31.6 us -> 44.9 us  [swap(): return lax.ppermute(x, 'seq', [(i, i ^ mask) for i in range(shards)])]
    ppermute x29 -> x36, starting transfers between devices: 19.8 us -> 24 us  [swap(): return lax.ppermute(x, 'seq', [(i, i ^ mask) for i in range(shards)])]
    unnamed x18 -> x14, local copies, waits for them, and re-layouts: 5.62 us -> 3.57 us
  transfers between devices with their start and end apart: 35 -> 42, of which waited for: 23 -> 25; matrix products, arithmetic and copies ran while one was open for 1% -> 1% of each run, Pallas kernels for 5% -> 4%
where the time goes in v3:
time: 112 us; the launch traced here: 111 us
  waiting for transfers between devices  59.5 us (53%)
  starting transfers between devices  32.8 us (29%)
  Pallas kernels  13.7 us (12%)
  local copies, waits for them, and re-layouts  3.57 us (3%)
    ppermute x36, waiting for transfers between devices, swap(): return lax.ppermute(x, 'seq', [(i, i ^ mask) for i in range(shards)])  44.9 us
    ppermute x36, starting transfers between devices, swap(): return lax.ppermute(x, 'seq', [(i, i ^ mask) for i in range(shards)])  24 us
    ppermute x6, waiting for transfers between devices, turn(): lax.ppermute(x, 'batch', [(i, (i + k) % parts) for i in range(parts)])  14.6 us
    pallas_call x8, Pallas kernels, call(): pl.pallas_call(kernel, out_shape=out_shape, in_specs=specs, out_specs=out...  13.7 us
    ppermute x6, starting transfers between devices, turn(): lax.ppermute(x, 'batch', [(i, (i + k) % parts) for i in range(parts)])  8.73 us
    unnamed x14, local copies, waits for them, and re-layouts  3.57 us
  transfers between devices with their start and end apart: 42, of which 25 were waited for; matrix products, arithmetic and copies ran while one was open for 1% of the time, Pallas kernels for 4%

profile of v3, /device:TPU:0, one launch (start us, length us, event | category | flops | bytes accessed | tf_op | source)
XLA Modules:
  0.0 111.2 jit_solution(11065128781728205782)
XLA Ops:
  0.6 2.1 %shard_map.77 = (f32[256,512]{1,0:T(8,128)}, f32[256,512]{1,0:T(8,128)}, f32[1,512]{1,0:T(1,128)}, f32[32,192]{1,0:T(8,128)}) custom-call(s32[1]{0:T(128)} %bitcast.refs_0_, bf16[512,256]{1,0:T(8,128)(2,1)} %bitcast.12, bf16[512,256]{1,0:T(8,128)(2,1)} %bitcast.13, f32[1,512]{1,0:T(1,128)} %refs_3_.1, f32[192,256]{1,0:T(8,128)} %refs_4_.1), custom_call_target="tpu_custom_call" | custom-call | flops 1000 | tf_op jit(solution)/shard_map/pallas_call | solution.py:284
  3.4 2.9 %collective-permute-start.4 = (f32[256,512]{1,0:T(8,128)}, f32[256,512]{1,0:T(8,128)S(1)}, u32[]{:S(2)}, u32[]{:S(2)}) collective-permute-start(f32[256,512]{1,0:T(8,128)} %get-tuple-element.35.refs_6_), channel_id=1, source_target_pairs={{0,8},{4,12},{8,0},{12,4},{16,24},{20,28},{24,16},{28,20},{1,9},{5... | collective-permute-start | bytes 1572872 | tf_op jit(solution)/shard_map/ppermute | solution.py:313
  6.3 1.5 %collective-permute-start.5 = (f32[256,512]{1,0:T(8,128)}, f32[256,512]{1,0:T(8,128)S(1)}, u32[]{:S(2)}, u32[]{:S(2)}) collective-permute-start(f32[256,512]{1,0:T(8,128)} %get-tuple-element.34.refs_5_), channel_id=1, source_target_pairs={{0,16},{4,20},{8,24},{12,28},{16,0},{20,4},{24,8},{28,12},{1,17},{... | collective-permute-start | bytes 1572872 | tf_op jit(solution)/shard_map/ppermute | solution.py:313
  7.9 1.4 %collective-permute-done.11.refs_10_ = f32[1,512]{1,0:T(1,128)S(1)} collective-permute-done((f32[1,512]{1,0:T(1,128)}, f32[1,512]{1,0:T(1,128)S(1)}, u32[]{:S(2)}, u32[]{:S(2)}) %collective-permute-start.11) | collective-permute-done | bytes 2080 | tf_op jit(solution)/shard_map/ppermute | solution.py:313
  9.2 1.6 %collective-permute-start.6 = (f32[32,192]{1,0:T(8,128)}, f32[32,192]{1,0:T(8,128)S(1)}, u32[]{:S(2)}, u32[]{:S(2)}) collective-permute-start(f32[32,192]{1,0:T(8,128)} %get-tuple-element.36.refs_1_), channel_id=1, source_target_pairs={{0,1},{1,2},{2,3},{3,0},{4,5},{5,6},{6,7},{7,4},{8,9},{9,10},{10,1... | collective-permute-start | bytes 73736 | tf_op jit(solution)/shard_map/ppermute | solution.py:316
  10.8 4.3 %collective-permute-done.6.refs_2_ = f32[32,192]{1,0:T(8,128)S(1)} collective-permute-done((f32[32,192]{1,0:T(8,128)}, f32[32,192]{1,0:T(8,128)S(1)}, u32[]{:S(2)}, u32[]{:S(2)}) %collective-permute-start.6) | collective-permute-done | bytes 24608 | tf_op jit(solution)/shard_map/ppermute | solution.py:316
  16.0 4.2 %collective-permute-done.7.refs_3_ = f32[32,192]{1,0:T(8,128)S(1)} collective-permute-done((f32[32,192]{1,0:T(8,128)}, f32[32,192]{1,0:T(8,128)S(1)}, u32[]{:S(2)}, u32[]{:S(2)}) %collective-permute-start.7) | collective-permute-done | bytes 24608 | tf_op jit(solution)/shard_map/ppermute | solution.py:316
  20.2 2.0 %collective-permute-start.8 = (f32[32,192]{1,0:T(8,128)}, f32[32,192]{1,0:T(8,128)S(1)}, u32[]{:S(2)}, u32[]{:S(2)}) collective-permute-start(f32[32,192]{1,0:T(8,128)} %get-tuple-element.36.refs_1_), channel_id=1, source_target_pairs={{0,3},{1,0},{2,1},{3,2},{4,7},{5,4},{6,5},{7,6},{8,11},{9,8},{10,9... | collective-permute-start | bytes 73736 | tf_op jit(solution)/shard_map/ppermute | solution.py:316
  22.2 2.1 %collective-permute-done.8.refs_4_ = f32[32,192]{1,0:T(8,128)S(1)} collective-permute-done((f32[32,192]{1,0:T(8,128)}, f32[32,192]{1,0:T(8,128)S(1)}, u32[]{:S(2)}, u32[]{:S(2)}) %collective-permute-start.8) | collective-permute-done | bytes 24608 | tf_op jit(solution)/shard_map/ppermute | solution.py:316
  30.2 5.3 %collective-permute-done.refs_2_ = f32[256,512]{1,0:T(8,128)S(1)} collective-permute-done((f32[256,512]{1,0:T(8,128)}, f32[256,512]{1,0:T(8,128)S(1)}, u32[]{:S(2)}, u32[]{:S(2)}) %collective-permute-start) | collective-permute-done | bytes 524320 | tf_op jit(solution)/shard_map/ppermute | solution.py:313
  36.0 1.2 %collective-permute-start.16 = (f32[1,512]{1,0:T(1,128)S(1)}, f32[1,512]{1,0:T(1,128)S(1)}, u32[]{:S(2)}, u32[]{:S(2)}) collective-permute-start(f32[1,512]{1,0:T(1,128)S(1)} %copy-done.5), channel_id=1, source_target_pairs={{0,8},{4,12},{8,0},{12,4},{16,24},{20,28},{24,16},{28,20},{1,9},{5... | collective-permute-start | bytes 6152 | tf_op jit(solution)/shard_map/ppermute | solution.py:313
  37.2 2.3 %collective-permute-done.16.refs_10_ = f32[1,512]{1,0:T(1,128)S(1)} collective-permute-done((f32[1,512]{1,0:T(1,128)S(1)}, f32[1,512]{1,0:T(1,128)S(1)}, u32[]{:S(2)}, u32[]{:S(2)}) %collective-permute-start.16) | collective-permute-done | bytes 2080 | tf_op jit(solution)/shard_map/ppermute | solution.py:313
  40.1 3.1 %collective-permute-done.17.refs_11_ = f32[1,512]{1,0:T(1,128)S(1)} collective-permute-done((f32[1,512]{1,0:T(1,128)S(1)}, f32[1,512]{1,0:T(1,128)S(1)}, u32[]{:S(2)}, u32[]{:S(2)}) %collective-permute-start.17) | collective-permute-done | bytes 2080 | tf_op jit(solution)/shard_map/ppermute | solution.py:313
  43.2 3.0 %collective-permute-done.18.refs_12_ = f32[1,512]{1,0:T(1,128)S(1)} collective-permute-done((f32[1,512]{1,0:T(1,128)S(1)}, f32[1,512]{1,0:T(1,128)S(1)}, u32[]{:S(2)}, u32[]{:S(2)}) %collective-permute-start.18) | collective-permute-done | bytes 2080 | tf_op jit(solution)/shard_map/ppermute | solution.py:313
  46.2 3.0 %collective-permute-done.19.refs_13_ = f32[1,512]{1,0:T(1,128)S(1)} collective-permute-done((f32[1,512]{1,0:T(1,128)S(1)}, f32[1,512]{1,0:T(1,128)S(1)}, u32[]{:S(2)}, u32[]{:S(2)}) %collective-permute-start.19) | collective-permute-done | bytes 2080 | tf_op jit(solution)/shard_map/ppermute | solution.py:313
  49.7 1.2 %collective-permute-start.3 = (f32[256,512]{1,0:T(8,128)S(1)}, f32[256,512]{1,0:T(8,128)S(1)}, u32[]{:S(2)}, u32[]{:S(2)}) collective-permute-start(f32[256,512]{1,0:T(8,128)S(1)} %collective-permute-done.2.refs_5_), channel_id=1, source_target_pairs={{0,8},{4,12},{8,0},{12,4},{16,24},{20,28},{24,16},{28,20},{1,9},{5... | collective-permute-start | bytes 1572872 | tf_op jit(solution)/shard_map/ppermute | solution.py:313
  52.4 10.2 %collective-permute-done.1.refs_2_ = f32[256,512]{1,0:T(8,128)S(1)} collective-permute-done((f32[256,512]{1,0:T(8,128)S(1)}, f32[256,512]{1,0:T(8,128)S(1)}, u32[]{:S(2)}, u32[]{:S(2)}) %collective-permute-start.1) | collective-permute-done | bytes 524320 | tf_op jit(solution)/shard_map/ppermute | solution.py:313
  63.9 1.2 %collective-permute-start.22 = (f32[1,512]{1,0:T(1,128)S(1)}, f32[1,512]{1,0:T(1,128)S(1)}, u32[]{:S(2)}, u32[]{:S(2)}) collective-permute-start(f32[1,512]{1,0:T(1,128)S(1)} %copy-done.6), channel_id=1, source_target_pairs={{0,24},{4,28},{8,16},{12,20},{16,8},{20,12},{24,0},{28,4},{1,25},{... | collective-permute-start | bytes 6152 | tf_op jit(solution)/shard_map/ppermute | solution.py:313
  66.1 2.2 %collective-permute-done.22.refs_6_ = f32[1,512]{1,0:T(1,128)S(1)} collective-permute-done((f32[1,512]{1,0:T(1,128)S(1)}, f32[1,512]{1,0:T(1,128)S(1)}, u32[]{:S(2)}, u32[]{:S(2)}) %collective-permute-start.22) | collective-permute-done | bytes 2080 | tf_op jit(solution)/shard_map/ppermute | solution.py:313
  69.8 2.1 %shard_map.81.refs_0_ = f32[3,32,256]{2,1,0:T(8,128)S(1)} custom-call(f32[3,32,256]{2,1,0:T(8,128)S(1)} %get-tuple-element.47.refs_0_.refs_2_, bf16[1024,512]{1,0:T(8,128)(2,1)S(1)} %get-tuple-element.48.refs_1_.refs_7_, f32[1,1024]{1,0:T(1,128)S(1)} %get-tuple-element.49.refs_2_.refs_8_, bf16[2048,512]{1,0:T(8,128)(2,1)S(1)} %get-tuple-element.50.refs_3_.refs_9_, ...), custom_call_target="tpu_custom_call" | custom-call | flops 805306368 | tf_op jit(solution)/shard_map/pallas_call | solution.py:284
  71.9 1.3 %collective-permute-start.24 = (f32[3,32,256]{2,1,0:T(8,128)S(1)}, f32[3,32,256]{2,1,0:T(8,128)S(1)}, u32[]{:S(2)}, u32[]{:S(2)}) collective-permute-start(f32[3,32,256]{2,1,0:T(8,128)S(1)} %shard_map.81.refs_0_), channel_id=1, source_target_pairs={{0,8},{4,12},{8,0},{12,4},{16,24},{20,28},{24,16},{28,20},{1,9},{5... | collective-permute-start | bytes 294920 | tf_op jit(solution)/shard_map/ppermute | solution.py:313
  75.4 1.3 %collective-permute-done.24.refs_1_ = f32[3,32,256]{2,1,0:T(8,128)S(1)} collective-permute-done((f32[3,32,256]{2,1,0:T(8,128)S(1)}, f32[3,32,256]{2,1,0:T(8,128)S(1)}, u32[]{:S(2)}, u32[]{:S(2)}) %collective-permute-start.24) | collective-permute-done | bytes 98336 | tf_op jit(solution)/shard_map/ppermute | solution.py:313
  76.7 3.2 %collective-permute-done.25.refs_2_ = f32[3,32,256]{2,1,0:T(8,128)S(1)} collective-permute-done((f32[3,32,256]{2,1,0:T(8,128)S(1)}, f32[3,32,256]{2,1,0:T(8,128)S(1)}, u32[]{:S(2)}, u32[]{:S(2)}) %collective-permute-start.25) | collective-permute-done | bytes 98336 | tf_op jit(solution)/shard_map/ppermute | solution.py:313
  79.9 1.6 %shard_map.82 = (f32[512,256]{1,0:T(8,128)S(1)}, f32[512,256]{1,0:T(8,128)S(1)}, f32[3,32,256]{2,1,0:T(8,128)S(1)}, f32[3,32,256]{2,1,0:T(8,128)S(1)}, f32[3,32,...) custom-call(f32[3,32,256]{2,1,0:T(8,128)S(1)} %shard_map.81.refs_0_, f32[3,32,256]{2,1,0:T(8,128)S(1)} %collective-permute-done.24.refs_1_, ...), custom_call_target="tpu_custom_call" | custom-call | flops 939524096 | tf_op jit(solution)/shard_map/pallas_call | solution.py:284
  83.8 1.4 %collective-permute-start.31 = (f32[3,32,256]{2,1,0:T(8,128)S(1)}, f32[3,32,256]{2,1,0:T(8,128)S(1)}, u32[]{:S(2)}, u32[]{:S(2)}) collective-permute-start(f32[3,32,256]{2,1,0:T(8,128)S(1)} %get-tuple-element.61), channel_id=1, source_target_pairs={{0,24},{4,28},{8,16},{12,20},{16,8},{20,12},{24,0},{28,4},{1,25},{... | collective-permute-start | bytes 294920 | tf_op jit(solution)/shard_map/ppermute | solution.py:313
  87.0 2.7 %collective-permute-done.30.refs_5_ = f32[3,32,256]{2,1,0:T(8,128)S(1)} collective-permute-done((f32[3,32,256]{2,1,0:T(8,128)S(1)}, f32[3,32,256]{2,1,0:T(8,128)S(1)}, u32[]{:S(2)}, u32[]{:S(2)}) %collective-permute-start.30) | collective-permute-done | bytes 98336 | tf_op jit(solution)/shard_map/ppermute | solution.py:313
  89.7 4.4 %shard_map.83 = (f32[32,192]{1,0:T(8,128)S(1)}, f32[32,192]{1,0:T(8,128)S(1)}, f32[32,192]{1,0:T(8,128)S(1)}, f32[32,192]{1,0:T(8,128)S(1)}) custom-call(s32[1]{0:T(128)} %bitcast.3.refs_0_, f32[3,32,256]{2,1,0:T(8,128)S(1)} %get-tuple-element.40.refs_1_, f32[3,32,256]{2,1,0:T(8,128)S(1)} %get-tuple-element.47.refs_0_.refs_2_, ...), custom_call_target="tpu_custom_call" | custom-call | flops 3221225472 | tf_op jit(solution)/shard_map/pallas_call | solution.py:284
  94.1 4.3 %collective-permute-start.33 = (f32[32,192]{1,0:T(8,128)S(1)}, f32[32,192]{1,0:T(8,128)S(1)}, u32[]{:S(2)}, u32[]{:S(2)}) collective-permute-start(f32[32,192]{1,0:T(8,128)S(1)} %get-tuple-element.64), channel_id=1, source_target_pairs={{0,2},{1,3},{2,0},{3,1},{4,6},{5,7},{6,4},{7,5},{8,10},{9,11},{10,... | collective-permute-start | bytes 73736 | tf_op jit(solution)/shard_map/ppermute | solution.py:316
  98.4 1.5 %collective-permute-done.32 = f32[32,192]{1,0:T(8,128)S(1)} collective-permute-done((f32[32,192]{1,0:T(8,128)S(1)}, f32[32,192]{1,0:T(8,128)S(1)}, u32[]{:S(2)}, u32[]{:S(2)}) %collective-permute-start.32) | collective-permute-done | bytes 24608 | tf_op jit(solution)/shard_map/ppermute | solution.py:316
  100.5 1.8 %collective-permute-done.34 = f32[32,192]{1,0:T(8,128)S(1)} collective-permute-done((f32[32,192]{1,0:T(8,128)S(1)}, f32[32,192]{1,0:T(8,128)S(1)}, u32[]{:S(2)}, u32[]{:S(2)}) %collective-permute-start.34) | collective-permute-done | bytes 24608 | tf_op jit(solution)/shard_map/ppermute | solution.py:316
  104.4 1.5 %collective-permute-start.40 = (f32[32,192]{1,0:T(8,128)S(1)}, f32[32,192]{1,0:T(8,128)S(1)}, u32[]{:S(2)}, u32[]{:S(2)}) collective-permute-start(f32[32,192]{1,0:T(8,128)S(1)} %add_add_fusion.refs_1_), channel_id=1, source_target_pairs={{0,24},{4,28},{8,16},{12,20},{16,8},{20,12},{24,0},{28,4},{1,25},{... | collective-permute-start | bytes 73736 | tf_op jit(solution)/shard_map/ppermute | solution.py:313
  107.3 1.9 %collective-permute-done.40.refs_7_ = f32[32,192]{1,0:T(8,128)S(1)} collective-permute-done((f32[32,192]{1,0:T(8,128)S(1)}, f32[32,192]{1,0:T(8,128)S(1)}, u32[]{:S(2)}, u32[]{:S(2)}) %collective-permute-start.40) | collective-permute-done | bytes 24608 | tf_op jit(solution)/shard_map/ppermute | solution.py:313
  (77 shorter events, 26.3 us)
Async XLA Ops:
  2.8 22.1 %collective-permute-start.10 = (f32[256,512]{1,0:T(8,128)}, f32[256,512]{1,0:T(8,128)S(1)}, u32[]{:S(2)}, u32[]{:S(2)}) collective-permute-start(f32[256,512]{1,0:T(8,128)} %get-tuple-element.35.refs_6_), channel_id=1, source_target_pairs={{0,4},{4,0},{8,12},{12,8},{16,20},{20,16},{24,28},{28,24},{1,5},{5... | collective-permute-start | bytes 1572872 | tf_op jit(solution)/shard_map/ppermute | solution.py:313
  3.4 21.9 %collective-permute-start.9 = (f32[256,512]{1,0:T(8,128)}, f32[256,512]{1,0:T(8,128)S(1)}, u32[]{:S(2)}, u32[]{:S(2)}) collective-permute-start(f32[256,512]{1,0:T(8,128)} %get-tuple-element.34.refs_5_), channel_id=1, source_target_pairs={{0,4},{4,0},{8,12},{12,8},{16,20},{20,16},{24,28},{28,24},{1,5},{5... | collective-permute-start | bytes 1572872 | tf_op jit(solution)/shard_map/ppermute | solution.py:313
  3.4 26.1 %collective-permute-start.4 = (f32[256,512]{1,0:T(8,128)}, f32[256,512]{1,0:T(8,128)S(1)}, u32[]{:S(2)}, u32[]{:S(2)}) collective-permute-start(f32[256,512]{1,0:T(8,128)} %get-tuple-element.35.refs_6_), channel_id=1, source_target_pairs={{0,8},{4,12},{8,0},{12,4},{16,24},{20,28},{24,16},{28,20},{1,9},{5... | collective-permute-start | bytes 1572872 | tf_op jit(solution)/shard_map/ppermute | solution.py:313
  6.3 23.2 %collective-permute-start.5 = (f32[256,512]{1,0:T(8,128)}, f32[256,512]{1,0:T(8,128)S(1)}, u32[]{:S(2)}, u32[]{:S(2)}) collective-permute-start(f32[256,512]{1,0:T(8,128)} %get-tuple-element.34.refs_5_), channel_id=1, source_target_pairs={{0,16},{4,20},{8,24},{12,28},{16,0},{20,4},{24,8},{28,12},{1,17},{... | collective-permute-start | bytes 1572872 | tf_op jit(solution)/shard_map/ppermute | solution.py:313
  9.2 5.9 %collective-permute-start.6 = (f32[32,192]{1,0:T(8,128)}, f32[32,192]{1,0:T(8,128)S(1)}, u32[]{:S(2)}, u32[]{:S(2)}) collective-permute-start(f32[32,192]{1,0:T(8,128)} %get-tuple-element.36.refs_1_), channel_id=1, source_target_pairs={{0,1},{1,2},{2,3},{3,0},{4,5},{5,6},{6,7},{7,4},{8,9},{9,10},{10,1... | collective-permute-start | bytes 73736 | tf_op jit(solution)/shard_map/ppermute | solution.py:316
  15.2 5.0 %collective-permute-start.7 = (f32[32,192]{1,0:T(8,128)}, f32[32,192]{1,0:T(8,128)S(1)}, u32[]{:S(2)}, u32[]{:S(2)}) collective-permute-start(f32[32,192]{1,0:T(8,128)} %get-tuple-element.36.refs_1_), channel_id=1, source_target_pairs={{0,2},{1,3},{2,0},{3,1},{4,6},{5,7},{6,4},{7,5},{8,10},{9,11},{10,... | collective-permute-start | bytes 73736 | tf_op jit(solution)/shard_map/ppermute | solution.py:316
  20.2 4.1 %collective-permute-start.8 = (f32[32,192]{1,0:T(8,128)}, f32[32,192]{1,0:T(8,128)S(1)}, u32[]{:S(2)}, u32[]{:S(2)}) collective-permute-start(f32[32,192]{1,0:T(8,128)} %get-tuple-element.36.refs_1_), channel_id=1, source_target_pairs={{0,3},{1,0},{2,1},{3,2},{4,7},{5,4},{6,5},{7,6},{8,11},{9,8},{10,9... | collective-permute-start | bytes 73736 | tf_op jit(solution)/shard_map/ppermute | solution.py:316
  24.3 11.2 %collective-permute-start = (f32[256,512]{1,0:T(8,128)}, f32[256,512]{1,0:T(8,128)S(1)}, u32[]{:S(2)}, u32[]{:S(2)}) collective-permute-start(f32[256,512]{1,0:T(8,128)} %get-tuple-element.34.refs_5_), channel_id=1, source_target_pairs={{0,8},{4,12},{8,0},{12,4},{16,24},{20,28},{24,16},{28,20},{1,9},{5... | collective-permute-start | bytes 1572872 | tf_op jit(solution)/shard_map/ppermute | solution.py:313
  24.9 10.9 %collective-permute-start.2 = (f32[256,512]{1,0:T(8,128)}, f32[256,512]{1,0:T(8,128)S(1)}, u32[]{:S(2)}, u32[]{:S(2)}) collective-permute-start(f32[256,512]{1,0:T(8,128)} %get-tuple-element.35.refs_6_), channel_id=1, source_target_pairs={{0,16},{4,20},{8,24},{12,28},{16,0},{20,4},{24,8},{28,12},{1,17},{... | collective-permute-start | bytes 1572872 | tf_op jit(solution)/shard_map/ppermute | solution.py:313
  29.6 20.1 %collective-permute-start.13 = (f32[256,512]{1,0:T(8,128)S(1)}, f32[256,512]{1,0:T(8,128)S(1)}, u32[]{:S(2)}, u32[]{:S(2)}) collective-permute-start(f32[256,512]{1,0:T(8,128)S(1)} %collective-permute-done.4.refs_3_), channel_id=1, source_target_pairs={{0,4},{4,0},{8,12},{12,8},{16,20},{20,16},{24,28},{28,24},{1,5},{5... | collective-permute-start | bytes 1572872 | tf_op jit(solution)/shard_map/ppermute | solution.py:313
  29.7 21.4 %collective-permute-start.14 = (f32[256,512]{1,0:T(8,128)S(1)}, f32[256,512]{1,0:T(8,128)S(1)}, u32[]{:S(2)}, u32[]{:S(2)}) collective-permute-start(f32[256,512]{1,0:T(8,128)S(1)} %collective-permute-done.5.refs_4_), channel_id=1, source_target_pairs={{0,4},{4,0},{8,12},{12,8},{16,20},{20,16},{24,28},{28,24},{1,5},{5... | collective-permute-start | bytes 1572872 | tf_op jit(solution)/shard_map/ppermute | solution.py:313
  35.5 15.7 %collective-permute-start.12 = (f32[256,512]{1,0:T(8,128)S(1)}, f32[256,512]{1,0:T(8,128)S(1)}, u32[]{:S(2)}, u32[]{:S(2)}) collective-permute-start(f32[256,512]{1,0:T(8,128)S(1)} %collective-permute-done.refs_2_), channel_id=1, source_target_pairs={{0,4},{4,0},{8,12},{12,8},{16,20},{20,16},{24,28},{28,24},{1,5},{5... | collective-permute-start | bytes 1572872 | tf_op jit(solution)/shard_map/ppermute | solution.py:313
  35.8 15.4 %collective-permute-start.15 = (f32[256,512]{1,0:T(8,128)S(1)}, f32[256,512]{1,0:T(8,128)S(1)}, u32[]{:S(2)}, u32[]{:S(2)}) collective-permute-start(f32[256,512]{1,0:T(8,128)S(1)} %collective-permute-done.2.refs_5_), channel_id=1, source_target_pairs={{0,4},{4,0},{8,12},{12,8},{16,20},{20,16},{24,28},{28,24},{1,5},{5... | collective-permute-start | bytes 1572872 | tf_op jit(solution)/shard_map/ppermute | solution.py:313
  49.2 13.4 %collective-permute-start.1 = (f32[256,512]{1,0:T(8,128)S(1)}, f32[256,512]{1,0:T(8,128)S(1)}, u32[]{:S(2)}, u32[]{:S(2)}) collective-permute-start(f32[256,512]{1,0:T(8,128)S(1)} %collective-permute-done.refs_2_), channel_id=1, source_target_pairs={{0,16},{4,20},{8,24},{12,28},{16,0},{20,4},{24,8},{28,12},{1,17},{... | collective-permute-start | bytes 1572872 | tf_op jit(solution)/shard_map/ppermute | solution.py:313
  49.7 13.7 %collective-permute-start.3 = (f32[256,512]{1,0:T(8,128)S(1)}, f32[256,512]{1,0:T(8,128)S(1)}, u32[]{:S(2)}, u32[]{:S(2)}) collective-permute-start(f32[256,512]{1,0:T(8,128)S(1)} %collective-permute-done.2.refs_5_), channel_id=1, source_target_pairs={{0,8},{4,12},{8,0},{12,4},{16,24},{20,28},{24,16},{28,20},{1,9},{5... | collective-permute-start | bytes 1572872 | tf_op jit(solution)/shard_map/ppermute | solution.py:313
  51.1 24.3 %collective-permute-start.27 = (f32[512,512]{1,0:T(8,128)S(1)}, f32[512,512]{1,0:T(8,128)S(1)}, u32[]{:S(2)}, u32[]{:S(2)}) collective-permute-start(f32[512,512]{1,0:T(8,128)S(1)} %maximum_convert_fusion), channel_id=1, source_target_pairs={{0,4},{4,0},{8,12},{12,8},{16,20},{20,16},{24,28},{28,24},{1,5},{5... | collective-permute-start | bytes 3145736 | tf_op jit(solution)/shard_map/ppermute | solution.py:313
  63.4 5.7 %collective-permute-start.20 = (f32[256,512]{1,0:T(8,128)S(1)}, f32[256,512]{1,0:T(8,128)S(1)}, u32[]{:S(2)}, u32[]{:S(2)}) collective-permute-start(f32[256,512]{1,0:T(8,128)S(1)} %collective-permute-done.1.refs_2_), channel_id=1, source_target_pairs={{0,4},{4,0},{8,12},{12,8},{16,20},{20,16},{24,28},{28,24},{1,5},{5... | collective-permute-start | bytes 1572872 | tf_op jit(solution)/shard_map/ppermute | solution.py:313
  63.4 5.7 %collective-permute-start.21 = (f32[256,512]{1,0:T(8,128)S(1)}, f32[256,512]{1,0:T(8,128)S(1)}, u32[]{:S(2)}, u32[]{:S(2)}) collective-permute-start(f32[256,512]{1,0:T(8,128)S(1)} %collective-permute-done.3.refs_3_), channel_id=1, source_target_pairs={{0,4},{4,0},{8,12},{12,8},{16,20},{20,16},{24,28},{28,24},{1,5},{5... | collective-permute-start | bytes 1572872 | tf_op jit(solution)/shard_map/ppermute | solution.py:313
  63.9 4.5 %collective-permute-start.22 = (f32[1,512]{1,0:T(1,128)S(1)}, f32[1,512]{1,0:T(1,128)S(1)}, u32[]{:S(2)}, u32[]{:S(2)}) collective-permute-start(f32[1,512]{1,0:T(1,128)S(1)} %copy-done.6), channel_id=1, source_target_pairs={{0,24},{4,28},{8,16},{12,20},{16,8},{20,12},{24,0},{28,4},{1,25},{... | collective-permute-start | bytes 6152 | tf_op jit(solution)/shard_map/ppermute | solution.py:313
  65.1 3.9 %collective-permute-start.23 = (f32[1,512]{1,0:T(1,128)S(1)}, f32[1,512]{1,0:T(1,128)S(1)}, u32[]{:S(2)}, u32[]{:S(2)}) collective-permute-start(f32[1,512]{1,0:T(1,128)S(1)} %copy-done.6), channel_id=1, source_target_pairs={{0,28},{4,24},{8,20},{12,16},{16,12},{20,8},{24,4},{28,0},{1,29},{... | collective-permute-start | bytes 6152 | tf_op jit(solution)/shard_map/ppermute | solution.py:313
  71.9 4.8 %collective-permute-start.24 = (f32[3,32,256]{2,1,0:T(8,128)S(1)}, f32[3,32,256]{2,1,0:T(8,128)S(1)}, u32[]{:S(2)}, u32[]{:S(2)}) collective-permute-start(f32[3,32,256]{2,1,0:T(8,128)S(1)} %shard_map.81.refs_0_), channel_id=1, source_target_pairs={{0,8},{4,12},{8,0},{12,4},{16,24},{20,28},{24,16},{28,20},{1,9},{5... | collective-permute-start | bytes 294920 | tf_op jit(solution)/shard_map/ppermute | solution.py:313
  73.2 6.7 %collective-permute-start.25 = (f32[3,32,256]{2,1,0:T(8,128)S(1)}, f32[3,32,256]{2,1,0:T(8,128)S(1)}, u32[]{:S(2)}, u32[]{:S(2)}) collective-permute-start(f32[3,32,256]{2,1,0:T(8,128)S(1)} %shard_map.81.refs_0_), channel_id=1, source_target_pairs={{0,16},{4,20},{8,24},{12,28},{16,0},{20,4},{24,8},{28,12},{1,17},{... | collective-permute-start | bytes 294920 | tf_op jit(solution)/shard_map/ppermute | solution.py:313
  74.2 5.7 %collective-permute-start.26 = (f32[3,32,256]{2,1,0:T(8,128)S(1)}, f32[3,32,256]{2,1,0:T(8,128)S(1)}, u32[]{:S(2)}, u32[]{:S(2)}) collective-permute-start(f32[3,32,256]{2,1,0:T(8,128)S(1)} %shard_map.81.refs_0_), channel_id=1, source_target_pairs={{0,24},{4,28},{8,16},{12,20},{16,8},{20,12},{24,0},{28,4},{1,25},{... | collective-permute-start | bytes 294920 | tf_op jit(solution)/shard_map/ppermute | solution.py:313
  81.6 5.4 %collective-permute-start.29 = (f32[3,32,256]{2,1,0:T(8,128)S(1)}, f32[3,32,256]{2,1,0:T(8,128)S(1)}, u32[]{:S(2)}, u32[]{:S(2)}) collective-permute-start(f32[3,32,256]{2,1,0:T(8,128)S(1)} %get-tuple-element.59), channel_id=1, source_target_pairs={{0,8},{4,12},{8,0},{12,4},{16,24},{20,28},{24,16},{28,20},{1,9},{5... | collective-permute-start | bytes 294920 | tf_op jit(solution)/shard_map/ppermute | solution.py:313
  82.7 7.0 %collective-permute-start.30 = (f32[3,32,256]{2,1,0:T(8,128)S(1)}, f32[3,32,256]{2,1,0:T(8,128)S(1)}, u32[]{:S(2)}, u32[]{:S(2)}) collective-permute-start(f32[3,32,256]{2,1,0:T(8,128)S(1)} %get-tuple-element.60), channel_id=1, source_target_pairs={{0,16},{4,20},{8,24},{12,28},{16,0},{20,4},{24,8},{28,12},{1,17},{... | collective-permute-start | bytes 294920 | tf_op jit(solution)/shard_map/ppermute | solution.py:313
  83.8 5.9 %collective-permute-start.31 = (f32[3,32,256]{2,1,0:T(8,128)S(1)}, f32[3,32,256]{2,1,0:T(8,128)S(1)}, u32[]{:S(2)}, u32[]{:S(2)}) collective-permute-start(f32[3,32,256]{2,1,0:T(8,128)S(1)} %get-tuple-element.61), channel_id=1, source_target_pairs={{0,24},{4,28},{8,16},{12,20},{16,8},{20,12},{24,0},{28,4},{1,25},{... | collective-permute-start | bytes 294920 | tf_op jit(solution)/shard_map/ppermute | solution.py:313
  94.0 5.9 %collective-permute-start.32 = (f32[32,192]{1,0:T(8,128)S(1)}, f32[32,192]{1,0:T(8,128)S(1)}, u32[]{:S(2)}, u32[]{:S(2)}) collective-permute-start(f32[32,192]{1,0:T(8,128)S(1)} %get-tuple-element.63), channel_id=1, source_target_pairs={{0,1},{1,2},{2,3},{3,0},{4,5},{5,6},{6,7},{7,4},{8,9},{9,10},{10,1... | collective-permute-start | bytes 73736 | tf_op jit(solution)/shard_map/ppermute | solution.py:316
  94.1 6.4 %collective-permute-start.33 = (f32[32,192]{1,0:T(8,128)S(1)}, f32[32,192]{1,0:T(8,128)S(1)}, u32[]{:S(2)}, u32[]{:S(2)}) collective-permute-start(f32[32,192]{1,0:T(8,128)S(1)} %get-tuple-element.64), channel_id=1, source_target_pairs={{0,2},{1,3},{2,0},{3,1},{4,6},{5,7},{6,4},{7,5},{8,10},{9,11},{10,... | collective-permute-start | bytes 73736 | tf_op jit(solution)/shard_map/ppermute | solution.py:316
  98.4 3.9 %collective-permute-start.34 = (f32[32,192]{1,0:T(8,128)S(1)}, f32[32,192]{1,0:T(8,128)S(1)}, u32[]{:S(2)}, u32[]{:S(2)}) collective-permute-start(f32[32,192]{1,0:T(8,128)S(1)} %get-tuple-element.65), channel_id=1, source_target_pairs={{0,3},{1,0},{2,1},{3,2},{4,7},{5,4},{6,5},{7,6},{8,11},{9,8},{10,9... | collective-permute-start | bytes 73736 | tf_op jit(solution)/shard_map/ppermute | solution.py:316
  102.3 4.0 %collective-permute-start.36 = (f32[32,192]{1,0:T(8,128)S(1)}, f32[32,192]{1,0:T(8,128)S(1)}, u32[]{:S(2)}, u32[]{:S(2)}) collective-permute-start(f32[32,192]{1,0:T(8,128)S(1)} %add_add_fusion.refs_1_), channel_id=1, source_target_pairs={{0,8},{4,12},{8,0},{12,4},{16,24},{20,28},{24,16},{28,20},{1,9},{5... | collective-permute-start | bytes 73736 | tf_op jit(solution)/shard_map/ppermute | solution.py:313
  103.4 3.9 %collective-permute-start.38 = (f32[32,192]{1,0:T(8,128)S(1)}, f32[32,192]{1,0:T(8,128)S(1)}, u32[]{:S(2)}, u32[]{:S(2)}) collective-permute-start(f32[32,192]{1,0:T(8,128)S(1)} %add_add_fusion.refs_1_), channel_id=1, source_target_pairs={{0,16},{4,20},{8,24},{12,28},{16,0},{20,4},{24,8},{28,12},{1,17},{... | collective-permute-start | bytes 73736 | tf_op jit(solution)/shard_map/ppermute | solution.py:313
  104.4 4.8 %collective-permute-start.40 = (f32[32,192]{1,0:T(8,128)S(1)}, f32[32,192]{1,0:T(8,128)S(1)}, u32[]{:S(2)}, u32[]{:S(2)}) collective-permute-start(f32[32,192]{1,0:T(8,128)S(1)} %add_add_fusion.refs_1_), channel_id=1, source_target_pairs={{0,24},{4,28},{8,16},{12,20},{16,8},{20,12},{24,0},{28,4},{1,25},{... | collective-permute-start | bytes 73736 | tf_op jit(solution)/shard_map/ppermute | solution.py:313
  (17 other events, 116.3 us)

commit v4 on v3

--- a/solution.py
+++ b/solution.py
@@ -38,8 +38,7 @@
 
 
 def gate(g):
-    decay = jnp.exp(-jnp.abs(g))
-    sig = jnp.where(g >= 0, 1.0, decay) / (1.0 + decay)
+    sig = 0.5 * jnp.tanh(0.5 * g) + 0.5
     silu = g * sig
     slope = sig + silu * (1.0 - sig)
     return sig, silu, slope
@@ -131,9 +130,9 @@
     for i, part in enumerate(refs[:messages]):
         size = part.shape[0]
         kv_ref[i * size : (i + 1) * size, :] = part[...].astype(BF16)
-    for i in range(messages // 2):
+    size = refs[messages].shape[1]
+    for i in range(kv_ref.shape[0] // size):
         rates = refs[messages + i]
-        size = rates.shape[1]
         eta_ref[:, i * size : (i + 1) * size] = rates[...]
     ab, c = flat(base_ref)
     acc = sweep(
@@ -336,16 +335,17 @@
 
     def first(start, messages, rates):
         count = len(messages)
+        size = sum(m.shape[0] for m in messages)
         outs = (
             block,
-            jax.ShapeDtypeStruct((count * half, 2 * width), BF16),
-            jax.ShapeDtypeStruct((1, count * half), F32),
+            jax.ShapeDtypeStruct((size, 2 * width), BF16),
+            jax.ShapeDtypeStruct((1, size), F32),
         )
         columns = 0 if len(start) == 2 else len(start) - 1
         return call(
             lambda *refs: first_kernel(count, columns, units, width, *refs),
             (block,) * (columns > 0) + outs,
-            2 * 2 * 6 * count * half * width * units,
+            2 * 2 * 6 * size * width * units,
             start + messages + rates,
             smem=(0,) if columns else (),
             scratch=[pltpu.VMEM((parts, units, share), F32)] if columns else (),
@@ -358,8 +358,9 @@
         x[1], y[0] = swap(own[1], 2), swap(own[0], 4)
         columns = [column] + [turn(column, k) for k in range(1, parts)]
         rates = [eta] + [swap(eta, mask) for mask in range(1, PAIRED)]
-        across = swap(x[0], 4)
-        diagonal = [across, swap(y[1], 2)]
+        quarter = half // 2
+        diagonal = [swap(x[0][:quarter], 4), swap(y[1][:quarter], 2)]
+        diagonal += [swap(x[0][quarter:], 4), swap(y[1][quarter:], 2)]
         near = own + [swap(m, 1) for m in own]
         initial, partial, *store_a = first([row] + columns, near, rates[0:2])
         x[1], y[0], partial = lax.optimization_barrier((x[1], y[0], partial))
@@ -367,10 +368,22 @@
         side = side + [swap(m, 1) for m in side]
         order = [rates[mask] for mask in (2, 4, 3, 5)]
         partial, *store_b = first([partial, initial], side, order)
-        *diagonal, partial = lax.optimization_barrier((*diagonal, partial))
-        far = diagonal + [swap(m, 1) for m in diagonal]
-        middle, *store_c = first([partial, initial], far, rates[6:8])
-        stores = [*store_a, *store_b, *store_c]
+
+        def picked(rate, k):
+            return jnp.concatenate(
+                [rate[:, at + k * quarter : at + (k + 1) * quarter] for at in (0, half)], axis=1
+            )
+
+        early, late = diagonal[:2], diagonal[2:]
+        *early, partial = lax.optimization_barrier((*early, partial))
+        early += [swap(m, 1) for m in early]
+        partial, *store_c = first(
+            [partial, initial], early, [picked(rate, 0) for rate in rates[6:8]]
+        )
+        *late, partial = lax.optimization_barrier((*late, partial))
+        late += [swap(m, 1) for m in late]
+        middle, *store_d = first([partial, initial], late, [picked(rate, 1) for rate in rates[6:8]])
+        stores = [*store_a, *store_b, *store_c, *store_d]
     else:
         initial = lax.all_gather(column, "batch", axis=1, tiled=True)
         initial = jnp.stack(jnp.split(initial, 3, axis=1))

time: 112 us -> 104 us (0.929)
  waiting for transfers between devices: 59.5 us -> 46.5 us
  starting transfers between devices: 32.8 us -> 37.3 us
    ppermute x36 -> x40, waiting for transfers between devices: 44.9 us -> 31.4 us  [swap(): return lax.ppermute(x, 'seq', [(i, i ^ mask) for i in range(shards)])]
    ppermute x36 -> x40, starting transfers between devices: 24 us -> 29.3 us  [swap(): return lax.ppermute(x, 'seq', [(i, i ^ mask) for i in range(shards)])]
    pallas_call x8 -> x9, Pallas kernels: 13.7 us -> 14.8 us  [call(): pl.pallas_call(kernel, out_shape=out_shape, in_specs=specs, out_specs=out...]
    unnamed x14 -> x10, local copies, waits for them, and re-layouts: 3.57 us -> 2.85 us
  transfers between devices with their start and end apart: 42 -> 46, of which waited for: 25 -> 25; matrix products, arithmetic and copies ran while one was open for 1% -> 1% of each run, Pallas kernels for 4% -> 6%
where the time goes in v4:
time: 104 us; the launch traced here: 103 us
  waiting for transfers between devices  46.5 us (45%)
  starting transfers between devices  37.3 us (36%)
  Pallas kernels  14.8 us (14%)
  local copies, waits for them, and re-layouts  2.92 us (3%)
    ppermute x40, waiting for transfers between devices, swap(): return lax.ppermute(x, 'seq', [(i, i ^ mask) for i in range(shards)])  31.4 us
    ppermute x40, starting transfers between devices, swap(): return lax.ppermute(x, 'seq', [(i, i ^ mask) for i in range(shards)])  29.3 us
    ppermute x6, waiting for transfers between devices, turn(): lax.ppermute(x, 'batch', [(i, (i + k) % parts) for i in range(parts)])  15.2 us
    pallas_call x9, Pallas kernels, call(): pl.pallas_call(kernel, out_shape=out_shape, in_specs=specs, out_specs=out...  14.8 us
    ppermute x6, starting transfers between devices, turn(): lax.ppermute(x, 'batch', [(i, (i + k) % parts) for i in range(parts)])  8.03 us
    unnamed x10, local copies, waits for them, and re-layouts  2.85 us
  transfers between devices with their start and end apart: 46, of which 25 were waited for; matrix products, arithmetic and copies ran while one was open for 1% of the time, Pallas kernels for 6%

profile of v4, /device:TPU:0, one launch (start us, length us, event | category | flops | bytes accessed | tf_op | source)
XLA Modules:
  0.0 103.3 jit_solution(5830433111326178064)
XLA Ops:
  0.6 2.2 %shard_map.77 = (f32[256,512]{1,0:T(8,128)}, f32[256,512]{1,0:T(8,128)}, f32[1,512]{1,0:T(1,128)}, f32[32,192]{1,0:T(8,128)}) custom-call(s32[1]{0:T(128)} %bitcast.refs_0_, bf16[512,256]{1,0:T(8,128)(2,1)} %bitcast.12, bf16[512,256]{1,0:T(8,128)(2,1)} %bitcast.13, f32[1,512]{1,0:T(1,128)} %refs_3_.1, f32[192,256]{1,0:T(8,128)} %refs_4_.1), custom_call_target="tpu_custom_call" | custom-call | flops 1000 | tf_op jit(solution)/shard_map/pallas_call | solution.py:283
  3.5 2.9 %collective-permute-start.6 = (f32[256,512]{1,0:T(8,128)}, f32[256,512]{1,0:T(8,128)S(1)}, u32[]{:S(2)}, u32[]{:S(2)}) collective-permute-start(f32[256,512]{1,0:T(8,128)} %get-tuple-element.41.refs_6_), channel_id=1, source_target_pairs={{0,8},{4,12},{8,0},{12,4},{16,24},{20,28},{24,16},{28,20},{1,9},{5... | collective-permute-start | bytes 1572872 | tf_op jit(solution)/shard_map/ppermute | solution.py:312
  6.4 1.5 %collective-permute-start.7 = (f32[256,512]{1,0:T(8,128)}, f32[256,512]{1,0:T(8,128)S(1)}, u32[]{:S(2)}, u32[]{:S(2)}) collective-permute-start(f32[256,512]{1,0:T(8,128)} %get-tuple-element.40.refs_5_), channel_id=1, source_target_pairs={{0,16},{4,20},{8,24},{12,28},{16,0},{20,4},{24,8},{28,12},{1,17},{... | collective-permute-start | bytes 1572872 | tf_op jit(solution)/shard_map/ppermute | solution.py:312
  7.9 1.4 %collective-permute-done.13.refs_10_ = f32[1,512]{1,0:T(1,128)S(1)} collective-permute-done((f32[1,512]{1,0:T(1,128)}, f32[1,512]{1,0:T(1,128)S(1)}, u32[]{:S(2)}, u32[]{:S(2)}) %collective-permute-start.13) | collective-permute-done | bytes 2080 | tf_op jit(solution)/shard_map/ppermute | solution.py:312
  9.3 3.6 %collective-permute-start.10 = (f32[32,192]{1,0:T(8,128)}, f32[32,192]{1,0:T(8,128)S(1)}, u32[]{:S(2)}, u32[]{:S(2)}) collective-permute-start(f32[32,192]{1,0:T(8,128)} %get-tuple-element.42.refs_1_), channel_id=1, source_target_pairs={{0,3},{1,0},{2,1},{3,2},{4,7},{5,4},{6,5},{7,6},{8,11},{9,8},{10,9... | collective-permute-start | bytes 73736 | tf_op jit(solution)/shard_map/ppermute | solution.py:315
  12.9 1.9 %collective-permute-done.10.refs_4_ = f32[32,192]{1,0:T(8,128)S(1)} collective-permute-done((f32[32,192]{1,0:T(8,128)}, f32[32,192]{1,0:T(8,128)S(1)}, u32[]{:S(2)}, u32[]{:S(2)}) %collective-permute-start.10) | collective-permute-done | bytes 24608 | tf_op jit(solution)/shard_map/ppermute | solution.py:315
  15.0 5.9 %collective-permute-done.8.refs_2_ = f32[32,192]{1,0:T(8,128)S(1)} collective-permute-done((f32[32,192]{1,0:T(8,128)}, f32[32,192]{1,0:T(8,128)S(1)}, u32[]{:S(2)}, u32[]{:S(2)}) %collective-permute-start.8) | collective-permute-done | bytes 24608 | tf_op jit(solution)/shard_map/ppermute | solution.py:315
  21.3 4.6 %collective-permute-done.9.refs_3_ = f32[32,192]{1,0:T(8,128)S(1)} collective-permute-done((f32[32,192]{1,0:T(8,128)}, f32[32,192]{1,0:T(8,128)S(1)}, u32[]{:S(2)}, u32[]{:S(2)}) %collective-permute-start.9) | collective-permute-done | bytes 24608 | tf_op jit(solution)/shard_map/ppermute | solution.py:315
  27.0 1.5 %collective-permute-start.18 = (f32[1,512]{1,0:T(1,128)}, f32[1,512]{1,0:T(1,128)S(1)}, u32[]{:S(2)}, u32[]{:S(2)}) collective-permute-start(f32[1,512]{1,0:T(1,128)} %get-tuple-element.43.refs_9_), channel_id=1, source_target_pairs={{0,8},{4,12},{8,0},{12,4},{16,24},{20,28},{24,16},{28,20},{1,9},{5... | collective-permute-start | bytes 6152 | tf_op jit(solution)/shard_map/ppermute | solution.py:312
  28.5 1.5 %collective-permute-start.19 = (f32[1,512]{1,0:T(1,128)}, f32[1,512]{1,0:T(1,128)S(1)}, u32[]{:S(2)}, u32[]{:S(2)}) collective-permute-start(f32[1,512]{1,0:T(1,128)} %get-tuple-element.43.refs_9_), channel_id=1, source_target_pairs={{0,16},{4,20},{8,24},{12,28},{16,0},{20,4},{24,8},{28,12},{1,17},{... | collective-permute-start | bytes 6152 | tf_op jit(solution)/shard_map/ppermute | solution.py:312
  32.9 1.4 %shard_map.78 = (f32[3,32,256]{2,1,0:T(8,128)S(1)}, f32[3,32,256]{2,1,0:T(8,128)S(1)}, bf16[1024,512]{1,0:T(8,128)(2,1)S(1)}, f32[1,1024]{1,0:T(1,128)S(1)}) custom-call(s32[1]{0:T(128)} %bitcast.3.refs_0_, f32[32,192]{1,0:T(8,128)S(1)} %copy-done.4, f32[32,192]{1,0:T(8,128)S(1)} %collective-permute-done.8.refs_2_, ...), custom_call_target="tpu_custom_call" | custom-call | flops 201326592 | tf_op jit(solution)/shard_map/pallas_call | solution.py:283
  34.4 2.7 %collective-permute-done.18.refs_10_ = f32[1,512]{1,0:T(1,128)S(1)} collective-permute-done((f32[1,512]{1,0:T(1,128)}, f32[1,512]{1,0:T(1,128)S(1)}, u32[]{:S(2)}, u32[]{:S(2)}) %collective-permute-start.18) | collective-permute-done | bytes 2080 | tf_op jit(solution)/shard_map/ppermute | solution.py:312
  38.7 2.3 %collective-permute-done.21.refs_13_ = f32[1,512]{1,0:T(1,128)S(1)} collective-permute-done((f32[1,512]{1,0:T(1,128)}, f32[1,512]{1,0:T(1,128)S(1)}, u32[]{:S(2)}, u32[]{:S(2)}) %collective-permute-start.21) | collective-permute-done | bytes 2080 | tf_op jit(solution)/shard_map/ppermute | solution.py:312
  41.0 1.3 %collective-permute-start.25 = (f32[1,512]{1,0:T(1,128)}, f32[1,512]{1,0:T(1,128)S(1)}, u32[]{:S(2)}, u32[]{:S(2)}) collective-permute-start(f32[1,512]{1,0:T(1,128)} %get-tuple-element.43.refs_9_), channel_id=1, source_target_pairs={{0,28},{4,24},{8,20},{12,16},{16,12},{20,8},{24,4},{28,0},{1,29},{... | collective-permute-start | bytes 6152 | tf_op jit(solution)/shard_map/ppermute | solution.py:312
  42.3 2.8 %collective-permute-done.25 = f32[1,512]{1,0:T(1,128)S(1)} collective-permute-done((f32[1,512]{1,0:T(1,128)}, f32[1,512]{1,0:T(1,128)S(1)}, u32[]{:S(2)}, u32[]{:S(2)}) %collective-permute-start.25) | collective-permute-done | bytes 2080 | tf_op jit(solution)/shard_map/ppermute | solution.py:312
  45.9 1.5 %collective-permute-start.5 = (f32[128,512]{1,0:T(8,128)S(1)}, f32[128,512]{1,0:T(8,128)S(1)}, u32[]{:S(2)}, u32[]{:S(2)}) collective-permute-start(f32[128,512]{1,0:T(8,128)S(1)} %get-tuple-element.78), channel_id=1, source_target_pairs={{0,8},{4,12},{8,0},{12,4},{16,24},{20,28},{24,16},{28,20},{1,9},{5... | collective-permute-start | bytes 786440 | tf_op jit(solution)/shard_map/ppermute | solution.py:312
  47.4 1.5 %collective-permute-start.24 = (f32[1,512]{1,0:T(1,128)}, f32[1,512]{1,0:T(1,128)S(1)}, u32[]{:S(2)}, u32[]{:S(2)}) collective-permute-start(f32[1,512]{1,0:T(1,128)} %get-tuple-element.43.refs_9_), channel_id=1, source_target_pairs={{0,24},{4,28},{8,16},{12,20},{16,8},{20,12},{24,0},{28,4},{1,25},{... | collective-permute-start | bytes 6152 | tf_op jit(solution)/shard_map/ppermute | solution.py:312
  50.5 4.0 %collective-permute-done.4.refs_2_ = f32[128,512]{1,0:T(8,128)S(1)} collective-permute-done((f32[128,512]{1,0:T(8,128)S(1)}, f32[128,512]{1,0:T(8,128)S(1)}, u32[]{:S(2)}, u32[]{:S(2)}) %collective-permute-start.4) | collective-permute-done | bytes 262176 | tf_op jit(solution)/shard_map/ppermute | solution.py:312
  54.6 1.5 %collective-permute-start.3 = (f32[128,512]{1,0:T(8,128)S(1)}, f32[128,512]{1,0:T(8,128)S(1)}, u32[]{:S(2)}, u32[]{:S(2)}) collective-permute-start(f32[128,512]{1,0:T(8,128)S(1)} %get-tuple-element.79), channel_id=1, source_target_pairs={{0,8},{4,12},{8,0},{12,4},{16,24},{20,28},{24,16},{28,20},{1,9},{5... | collective-permute-start | bytes 786440 | tf_op jit(solution)/shard_map/ppermute | solution.py:312
  59.5 1.9 %collective-permute-done.3.refs_3_ = f32[128,512]{1,0:T(8,128)S(1)} collective-permute-done((f32[128,512]{1,0:T(8,128)S(1)}, f32[128,512]{1,0:T(8,128)S(1)}, u32[]{:S(2)}, u32[]{:S(2)}) %collective-permute-start.3) | collective-permute-done | bytes 262176 | tf_op jit(solution)/shard_map/ppermute | solution.py:312
  63.8 2.2 %shard_map.82.refs_0_ = f32[3,32,256]{2,1,0:T(8,128)S(1)} custom-call(f32[3,32,256]{2,1,0:T(8,128)S(1)} %get-tuple-element.57.refs_0_.refs_2_, bf16[1024,512]{1,0:T(8,128)(2,1)S(1)} %get-tuple-element.58.refs_1_.refs_7_, f32[1,1024]{1,0:T(1,128)S(1)} %get-tuple-element.59.refs_2_.refs_8_, bf16[2048,512]{1,0:T(8,128)(2,1)S(1)} %get-tuple-element.60.refs_3_.refs_9_, ...), custom_call_target="tpu_custom_call" | custom-call | flops 805306368 | tf_op jit(solution)/shard_map/pallas_call | solution.py:283
  67.6 2.0 %collective-permute-start.30 = (f32[3,32,256]{2,1,0:T(8,128)S(1)}, f32[3,32,256]{2,1,0:T(8,128)S(1)}, u32[]{:S(2)}, u32[]{:S(2)}) collective-permute-start(f32[3,32,256]{2,1,0:T(8,128)S(1)} %shard_map.82.refs_0_), channel_id=1, source_target_pairs={{0,24},{4,28},{8,16},{12,20},{16,8},{20,12},{24,0},{28,4},{1,25},{... | collective-permute-start | bytes 294920 | tf_op jit(solution)/shard_map/ppermute | solution.py:312
  69.6 1.6 %collective-permute-done.28.refs_1_ = f32[3,32,256]{2,1,0:T(8,128)S(1)} collective-permute-done((f32[3,32,256]{2,1,0:T(8,128)S(1)}, f32[3,32,256]{2,1,0:T(8,128)S(1)}, u32[]{:S(2)}, u32[]{:S(2)}) %collective-permute-start.28) | collective-permute-done | bytes 98336 | tf_op jit(solution)/shard_map/ppermute | solution.py:312
  71.1 2.7 %collective-permute-done.29.refs_2_ = f32[3,32,256]{2,1,0:T(8,128)S(1)} collective-permute-done((f32[3,32,256]{2,1,0:T(8,128)S(1)}, f32[3,32,256]{2,1,0:T(8,128)S(1)}, u32[]{:S(2)}, u32[]{:S(2)}) %collective-permute-start.29) | collective-permute-done | bytes 98336 | tf_op jit(solution)/shard_map/ppermute | solution.py:312
  73.8 1.6 %shard_map.83 = (f32[512,256]{1,0:T(8,128)S(1)}, f32[512,256]{1,0:T(8,128)S(1)}, f32[3,32,256]{2,1,0:T(8,128)S(1)}, f32[3,32,256]{2,1,0:T(8,128)S(1)}, f32[3,32,...) custom-call(f32[3,32,256]{2,1,0:T(8,128)S(1)} %shard_map.82.refs_0_, f32[3,32,256]{2,1,0:T(8,128)S(1)} %collective-permute-done.28.refs_1_, ...), custom_call_target="tpu_custom_call" | custom-call | flops 939524096 | tf_op jit(solution)/shard_map/pallas_call | solution.py:283
  77.4 1.6 %collective-permute-start.35 = (f32[3,32,256]{2,1,0:T(8,128)S(1)}, f32[3,32,256]{2,1,0:T(8,128)S(1)}, u32[]{:S(2)}, u32[]{:S(2)}) collective-permute-start(f32[3,32,256]{2,1,0:T(8,128)S(1)} %get-tuple-element.73), channel_id=1, source_target_pairs={{0,24},{4,28},{8,16},{12,20},{16,8},{20,12},{24,0},{28,4},{1,25},{... | collective-permute-start | bytes 294920 | tf_op jit(solution)/shard_map/ppermute | solution.py:312
  80.8 2.7 %collective-permute-done.34.refs_5_ = f32[3,32,256]{2,1,0:T(8,128)S(1)} collective-permute-done((f32[3,32,256]{2,1,0:T(8,128)S(1)}, f32[3,32,256]{2,1,0:T(8,128)S(1)}, u32[]{:S(2)}, u32[]{:S(2)}) %collective-permute-start.34) | collective-permute-done | bytes 98336 | tf_op jit(solution)/shard_map/ppermute | solution.py:312
  83.5 4.5 %shard_map.84 = (f32[32,192]{1,0:T(8,128)S(1)}, f32[32,192]{1,0:T(8,128)S(1)}, f32[32,192]{1,0:T(8,128)S(1)}, f32[32,192]{1,0:T(8,128)S(1)}) custom-call(s32[1]{0:T(128)} %bitcast.3.refs_0_, f32[3,32,256]{2,1,0:T(8,128)S(1)} %get-tuple-element.46.refs_1_, f32[3,32,256]{2,1,0:T(8,128)S(1)} %get-tuple-element.57.refs_0_.refs_2_, ...), custom_call_target="tpu_custom_call" | custom-call | flops 3221225472 | tf_op jit(solution)/shard_map/pallas_call | solution.py:283
  88.1 2.6 %collective-permute-start.37 = (f32[32,192]{1,0:T(8,128)S(1)}, f32[32,192]{1,0:T(8,128)S(1)}, u32[]{:S(2)}, u32[]{:S(2)}) collective-permute-start(f32[32,192]{1,0:T(8,128)S(1)} %get-tuple-element.76), channel_id=1, source_target_pairs={{0,2},{1,3},{2,0},{3,1},{4,6},{5,7},{6,4},{7,5},{8,10},{9,11},{10,... | collective-permute-start | bytes 73736 | tf_op jit(solution)/shard_map/ppermute | solution.py:315
  91.9 1.9 %collective-permute-done.36 = f32[32,192]{1,0:T(8,128)S(1)} collective-permute-done((f32[32,192]{1,0:T(8,128)S(1)}, f32[32,192]{1,0:T(8,128)S(1)}, u32[]{:S(2)}, u32[]{:S(2)}) %collective-permute-start.36) | collective-permute-done | bytes 24608 | tf_op jit(solution)/shard_map/ppermute | solution.py:315
  96.4 1.7 %collective-permute-start.44 = (f32[32,192]{1,0:T(8,128)S(1)}, f32[32,192]{1,0:T(8,128)S(1)}, u32[]{:S(2)}, u32[]{:S(2)}) collective-permute-start(f32[32,192]{1,0:T(8,128)S(1)} %add_add_fusion.refs_1_), channel_id=1, source_target_pairs={{0,24},{4,28},{8,16},{12,20},{16,8},{20,12},{24,0},{28,4},{1,25},{... | collective-permute-start | bytes 73736 | tf_op jit(solution)/shard_map/ppermute | solution.py:312
  99.6 1.7 %collective-permute-done.44.refs_7_ = f32[32,192]{1,0:T(8,128)S(1)} collective-permute-done((f32[32,192]{1,0:T(8,128)S(1)}, f32[32,192]{1,0:T(8,128)S(1)}, u32[]{:S(2)}, u32[]{:S(2)}) %collective-permute-start.44) | collective-permute-done | bytes 24608 | tf_op jit(solution)/shard_map/ppermute | solution.py:312
  (88 shorter events, 27.9 us)
Async XLA Ops:
  2.9 23.6 %collective-permute-start.11 = (f32[256,512]{1,0:T(8,128)}, f32[256,512]{1,0:T(8,128)S(1)}, u32[]{:S(2)}, u32[]{:S(2)}) collective-permute-start(f32[256,512]{1,0:T(8,128)} %get-tuple-element.40.refs_5_), channel_id=1, source_target_pairs={{0,4},{4,0},{8,12},{12,8},{16,20},{20,16},{24,28},{28,24},{1,5},{5... | collective-permute-start | bytes 1572872 | tf_op jit(solution)/shard_map/ppermute | solution.py:312
  3.4 23.6 %collective-permute-start.12 = (f32[256,512]{1,0:T(8,128)}, f32[256,512]{1,0:T(8,128)S(1)}, u32[]{:S(2)}, u32[]{:S(2)}) collective-permute-start(f32[256,512]{1,0:T(8,128)} %get-tuple-element.41.refs_6_), channel_id=1, source_target_pairs={{0,4},{4,0},{8,12},{12,8},{16,20},{20,16},{24,28},{28,24},{1,5},{5... | collective-permute-start | bytes 1572872 | tf_op jit(solution)/shard_map/ppermute | solution.py:312
  3.5 25.0 %collective-permute-start.6 = (f32[256,512]{1,0:T(8,128)}, f32[256,512]{1,0:T(8,128)S(1)}, u32[]{:S(2)}, u32[]{:S(2)}) collective-permute-start(f32[256,512]{1,0:T(8,128)} %get-tuple-element.41.refs_6_), channel_id=1, source_target_pairs={{0,8},{4,12},{8,0},{12,4},{16,24},{20,28},{24,16},{28,20},{1,9},{5... | collective-permute-start | bytes 1572872 | tf_op jit(solution)/shard_map/ppermute | solution.py:312
  6.4 27.9 %collective-permute-start.7 = (f32[256,512]{1,0:T(8,128)}, f32[256,512]{1,0:T(8,128)S(1)}, u32[]{:S(2)}, u32[]{:S(2)}) collective-permute-start(f32[256,512]{1,0:T(8,128)} %get-tuple-element.40.refs_5_), channel_id=1, source_target_pairs={{0,16},{4,20},{8,24},{12,28},{16,0},{20,4},{24,8},{28,12},{1,17},{... | collective-permute-start | bytes 1572872 | tf_op jit(solution)/shard_map/ppermute | solution.py:312
  9.3 5.5 %collective-permute-start.10 = (f32[32,192]{1,0:T(8,128)}, f32[32,192]{1,0:T(8,128)S(1)}, u32[]{:S(2)}, u32[]{:S(2)}) collective-permute-start(f32[32,192]{1,0:T(8,128)} %get-tuple-element.42.refs_1_), channel_id=1, source_target_pairs={{0,3},{1,0},{2,1},{3,2},{4,7},{5,4},{6,5},{7,6},{8,11},{9,8},{10,9... | collective-permute-start | bytes 73736 | tf_op jit(solution)/shard_map/ppermute | solution.py:315
  14.8 6.1 %collective-permute-start.8 = (f32[32,192]{1,0:T(8,128)}, f32[32,192]{1,0:T(8,128)S(1)}, u32[]{:S(2)}, u32[]{:S(2)}) collective-permute-start(f32[32,192]{1,0:T(8,128)} %get-tuple-element.42.refs_1_), channel_id=1, source_target_pairs={{0,1},{1,2},{2,3},{3,0},{4,5},{5,6},{6,7},{7,4},{8,9},{9,10},{10,1... | collective-permute-start | bytes 73736 | tf_op jit(solution)/shard_map/ppermute | solution.py:315
  20.9 5.0 %collective-permute-start.9 = (f32[32,192]{1,0:T(8,128)}, f32[32,192]{1,0:T(8,128)S(1)}, u32[]{:S(2)}, u32[]{:S(2)}) collective-permute-start(f32[32,192]{1,0:T(8,128)} %get-tuple-element.42.refs_1_), channel_id=1, source_target_pairs={{0,2},{1,3},{2,0},{3,1},{4,6},{5,7},{6,4},{7,5},{8,10},{9,11},{10,... | collective-permute-start | bytes 73736 | tf_op jit(solution)/shard_map/ppermute | solution.py:315
  25.9 12.2 %collective-permute-start = (f32[256,512]{1,0:T(8,128)}, f32[256,512]{1,0:T(8,128)S(1)}, u32[]{:S(2)}, u32[]{:S(2)}) collective-permute-start(f32[256,512]{1,0:T(8,128)} %get-tuple-element.40.refs_5_), channel_id=1, source_target_pairs={{0,8},{4,12},{8,0},{12,4},{16,24},{20,28},{24,16},{28,20},{1,9},{5... | collective-permute-start | bytes 1572872 | tf_op jit(solution)/shard_map/ppermute | solution.py:312
  26.5 11.9 %collective-permute-start.2 = (f32[256,512]{1,0:T(8,128)}, f32[256,512]{1,0:T(8,128)S(1)}, u32[]{:S(2)}, u32[]{:S(2)}) collective-permute-start(f32[256,512]{1,0:T(8,128)} %get-tuple-element.41.refs_6_), channel_id=1, source_target_pairs={{0,16},{4,20},{8,24},{12,28},{16,0},{20,4},{24,8},{28,12},{1,17},{... | collective-permute-start | bytes 1572872 | tf_op jit(solution)/shard_map/ppermute | solution.py:312
  27.0 10.0 %collective-permute-start.18 = (f32[1,512]{1,0:T(1,128)}, f32[1,512]{1,0:T(1,128)S(1)}, u32[]{:S(2)}, u32[]{:S(2)}) collective-permute-start(f32[1,512]{1,0:T(1,128)} %get-tuple-element.43.refs_9_), channel_id=1, source_target_pairs={{0,8},{4,12},{8,0},{12,4},{16,24},{20,28},{24,16},{28,20},{1,9},{5... | collective-permute-start | bytes 6152 | tf_op jit(solution)/shard_map/ppermute | solution.py:312
  28.5 8.8 %collective-permute-start.19 = (f32[1,512]{1,0:T(1,128)}, f32[1,512]{1,0:T(1,128)S(1)}, u32[]{:S(2)}, u32[]{:S(2)}) collective-permute-start(f32[1,512]{1,0:T(1,128)} %get-tuple-element.43.refs_9_), channel_id=1, source_target_pairs={{0,16},{4,20},{8,24},{12,28},{16,0},{20,4},{24,8},{28,12},{1,17},{... | collective-permute-start | bytes 6152 | tf_op jit(solution)/shard_map/ppermute | solution.py:312
  37.0 8.3 %collective-permute-start.15 = (f32[256,512]{1,0:T(8,128)S(1)}, f32[256,512]{1,0:T(8,128)S(1)}, u32[]{:S(2)}, u32[]{:S(2)}) collective-permute-start(f32[256,512]{1,0:T(8,128)S(1)} %collective-permute-done.6.refs_3_), channel_id=1, source_target_pairs={{0,4},{4,0},{8,12},{12,8},{16,20},{20,16},{24,28},{28,24},{1,5},{5... | collective-permute-start | bytes 1572872 | tf_op jit(solution)/shard_map/ppermute | solution.py:312
  37.3 8.6 %collective-permute-start.16 = (f32[256,512]{1,0:T(8,128)S(1)}, f32[256,512]{1,0:T(8,128)S(1)}, u32[]{:S(2)}, u32[]{:S(2)}) collective-permute-start(f32[256,512]{1,0:T(8,128)S(1)} %collective-permute-done.7.refs_4_), channel_id=1, source_target_pairs={{0,4},{4,0},{8,12},{12,8},{16,20},{20,16},{24,28},{28,24},{1,5},{5... | collective-permute-start | bytes 1572872 | tf_op jit(solution)/shard_map/ppermute | solution.py:312
  38.1 9.2 %collective-permute-start.14 = (f32[256,512]{1,0:T(8,128)S(1)}, f32[256,512]{1,0:T(8,128)S(1)}, u32[]{:S(2)}, u32[]{:S(2)}) collective-permute-start(f32[256,512]{1,0:T(8,128)S(1)} %collective-permute-done.refs_2_), channel_id=1, source_target_pairs={{0,4},{4,0},{8,12},{12,8},{16,20},{20,16},{24,28},{28,24},{1,5},{5... | collective-permute-start | bytes 1572872 | tf_op jit(solution)/shard_map/ppermute | solution.py:312
  38.4 10.5 %collective-permute-start.17 = (f32[256,512]{1,0:T(8,128)S(1)}, f32[256,512]{1,0:T(8,128)S(1)}, u32[]{:S(2)}, u32[]{:S(2)}) collective-permute-start(f32[256,512]{1,0:T(8,128)S(1)} %collective-permute-done.2.refs_5_), channel_id=1, source_target_pairs={{0,4},{4,0},{8,12},{12,8},{16,20},{20,16},{24,28},{28,24},{1,5},{5... | collective-permute-start | bytes 1572872 | tf_op jit(solution)/shard_map/ppermute | solution.py:312
  41.0 4.1 %collective-permute-start.25 = (f32[1,512]{1,0:T(1,128)}, f32[1,512]{1,0:T(1,128)S(1)}, u32[]{:S(2)}, u32[]{:S(2)}) collective-permute-start(f32[1,512]{1,0:T(1,128)} %get-tuple-element.43.refs_9_), channel_id=1, source_target_pairs={{0,28},{4,24},{8,20},{12,16},{16,12},{20,8},{24,4},{28,0},{1,29},{... | collective-permute-start | bytes 6152 | tf_op jit(solution)/shard_map/ppermute | solution.py:312
  45.1 24.5 %collective-permute-start.31 = (f32[512,512]{1,0:T(8,128)S(1)}, f32[512,512]{1,0:T(8,128)S(1)}, u32[]{:S(2)}, u32[]{:S(2)}) collective-permute-start(f32[512,512]{1,0:T(8,128)S(1)} %maximum_convert_fusion), channel_id=1, source_target_pairs={{0,4},{4,0},{8,12},{12,8},{16,20},{20,16},{24,28},{28,24},{1,5},{5... | collective-permute-start | bytes 3145736 | tf_op jit(solution)/shard_map/ppermute | solution.py:312
  45.4 9.2 %collective-permute-start.4 = (f32[128,512]{1,0:T(8,128)S(1)}, f32[128,512]{1,0:T(8,128)S(1)}, u32[]{:S(2)}, u32[]{:S(2)}) collective-permute-start(f32[128,512]{1,0:T(8,128)S(1)} %get-tuple-element.80), channel_id=1, source_target_pairs={{0,16},{4,20},{8,24},{12,28},{16,0},{20,4},{24,8},{28,12},{1,17},{... | collective-permute-start | bytes 786440 | tf_op jit(solution)/shard_map/ppermute | solution.py:312
  45.9 10.2 %collective-permute-start.5 = (f32[128,512]{1,0:T(8,128)S(1)}, f32[128,512]{1,0:T(8,128)S(1)}, u32[]{:S(2)}, u32[]{:S(2)}) collective-permute-start(f32[128,512]{1,0:T(8,128)S(1)} %get-tuple-element.78), channel_id=1, source_target_pairs={{0,8},{4,12},{8,0},{12,4},{16,24},{20,28},{24,16},{28,20},{1,9},{5... | collective-permute-start | bytes 786440 | tf_op jit(solution)/shard_map/ppermute | solution.py:312
  47.4 8.7 %collective-permute-start.24 = (f32[1,512]{1,0:T(1,128)}, f32[1,512]{1,0:T(1,128)S(1)}, u32[]{:S(2)}, u32[]{:S(2)}) collective-permute-start(f32[1,512]{1,0:T(1,128)} %get-tuple-element.43.refs_9_), channel_id=1, source_target_pairs={{0,24},{4,28},{8,16},{12,20},{16,8},{20,12},{24,0},{28,4},{1,25},{... | collective-permute-start | bytes 6152 | tf_op jit(solution)/shard_map/ppermute | solution.py:312
  48.9 10.6 %collective-permute-start.1 = (f32[128,512]{1,0:T(8,128)S(1)}, f32[128,512]{1,0:T(8,128)S(1)}, u32[]{:S(2)}, u32[]{:S(2)}) collective-permute-start(f32[128,512]{1,0:T(8,128)S(1)} %get-tuple-element.81), channel_id=1, source_target_pairs={{0,16},{4,20},{8,24},{12,28},{16,0},{20,4},{24,8},{28,12},{1,17},{... | collective-permute-start | bytes 786440 | tf_op jit(solution)/shard_map/ppermute | solution.py:312
  54.6 6.9 %collective-permute-start.3 = (f32[128,512]{1,0:T(8,128)S(1)}, f32[128,512]{1,0:T(8,128)S(1)}, u32[]{:S(2)}, u32[]{:S(2)}) collective-permute-start(f32[128,512]{1,0:T(8,128)S(1)} %get-tuple-element.79), channel_id=1, source_target_pairs={{0,8},{4,12},{8,0},{12,4},{16,24},{20,28},{24,16},{28,20},{1,9},{5... | collective-permute-start | bytes 786440 | tf_op jit(solution)/shard_map/ppermute | solution.py:312
  66.0 5.1 %collective-permute-start.28 = (f32[3,32,256]{2,1,0:T(8,128)S(1)}, f32[3,32,256]{2,1,0:T(8,128)S(1)}, u32[]{:S(2)}, u32[]{:S(2)}) collective-permute-start(f32[3,32,256]{2,1,0:T(8,128)S(1)} %shard_map.82.refs_0_), channel_id=1, source_target_pairs={{0,8},{4,12},{8,0},{12,4},{16,24},{20,28},{24,16},{28,20},{1,9},{5... | collective-permute-start | bytes 294920 | tf_op jit(solution)/shard_map/ppermute | solution.py:312
  67.1 6.7 %collective-permute-start.29 = (f32[3,32,256]{2,1,0:T(8,128)S(1)}, f32[3,32,256]{2,1,0:T(8,128)S(1)}, u32[]{:S(2)}, u32[]{:S(2)}) collective-permute-start(f32[3,32,256]{2,1,0:T(8,128)S(1)} %shard_map.82.refs_0_), channel_id=1, source_target_pairs={{0,16},{4,20},{8,24},{12,28},{16,0},{20,4},{24,8},{28,12},{1,17},{... | collective-permute-start | bytes 294920 | tf_op jit(solution)/shard_map/ppermute | solution.py:312
  67.6 6.2 %collective-permute-start.30 = (f32[3,32,256]{2,1,0:T(8,128)S(1)}, f32[3,32,256]{2,1,0:T(8,128)S(1)}, u32[]{:S(2)}, u32[]{:S(2)}) collective-permute-start(f32[3,32,256]{2,1,0:T(8,128)S(1)} %shard_map.82.refs_0_), channel_id=1, source_target_pairs={{0,24},{4,28},{8,16},{12,20},{16,8},{20,12},{24,0},{28,4},{1,25},{... | collective-permute-start | bytes 294920 | tf_op jit(solution)/shard_map/ppermute | solution.py:312
  75.5 5.4 %collective-permute-start.33 = (f32[3,32,256]{2,1,0:T(8,128)S(1)}, f32[3,32,256]{2,1,0:T(8,128)S(1)}, u32[]{:S(2)}, u32[]{:S(2)}) collective-permute-start(f32[3,32,256]{2,1,0:T(8,128)S(1)} %get-tuple-element.71), channel_id=1, source_target_pairs={{0,8},{4,12},{8,0},{12,4},{16,24},{20,28},{24,16},{28,20},{1,9},{5... | collective-permute-start | bytes 294920 | tf_op jit(solution)/shard_map/ppermute | solution.py:312
  76.6 7.0 %collective-permute-start.34 = (f32[3,32,256]{2,1,0:T(8,128)S(1)}, f32[3,32,256]{2,1,0:T(8,128)S(1)}, u32[]{:S(2)}, u32[]{:S(2)}) collective-permute-start(f32[3,32,256]{2,1,0:T(8,128)S(1)} %get-tuple-element.72), channel_id=1, source_target_pairs={{0,16},{4,20},{8,24},{12,28},{16,0},{20,4},{24,8},{28,12},{1,17},{... | collective-permute-start | bytes 294920 | tf_op jit(solution)/shard_map/ppermute | solution.py:312
  77.4 6.1 %collective-permute-start.35 = (f32[3,32,256]{2,1,0:T(8,128)S(1)}, f32[3,32,256]{2,1,0:T(8,128)S(1)}, u32[]{:S(2)}, u32[]{:S(2)}) collective-permute-start(f32[3,32,256]{2,1,0:T(8,128)S(1)} %get-tuple-element.73), channel_id=1, source_target_pairs={{0,24},{4,28},{8,16},{12,20},{16,8},{20,12},{24,0},{28,4},{1,25},{... | collective-permute-start | bytes 294920 | tf_op jit(solution)/shard_map/ppermute | solution.py:312
  88.0 5.8 %collective-permute-start.36 = (f32[32,192]{1,0:T(8,128)S(1)}, f32[32,192]{1,0:T(8,128)S(1)}, u32[]{:S(2)}, u32[]{:S(2)}) collective-permute-start(f32[32,192]{1,0:T(8,128)S(1)} %get-tuple-element.75), channel_id=1, source_target_pairs={{0,1},{1,2},{2,3},{3,0},{4,5},{5,6},{6,7},{7,4},{8,9},{9,10},{10,1... | collective-permute-start | bytes 73736 | tf_op jit(solution)/shard_map/ppermute | solution.py:315
  88.1 5.7 %collective-permute-start.37 = (f32[32,192]{1,0:T(8,128)S(1)}, f32[32,192]{1,0:T(8,128)S(1)}, u32[]{:S(2)}, u32[]{:S(2)}) collective-permute-start(f32[32,192]{1,0:T(8,128)S(1)} %get-tuple-element.76), channel_id=1, source_target_pairs={{0,2},{1,3},{2,0},{3,1},{4,6},{5,7},{6,4},{7,5},{8,10},{9,11},{10,... | collective-permute-start | bytes 73736 | tf_op jit(solution)/shard_map/ppermute | solution.py:315
  94.6 4.0 %collective-permute-start.40 = (f32[32,192]{1,0:T(8,128)S(1)}, f32[32,192]{1,0:T(8,128)S(1)}, u32[]{:S(2)}, u32[]{:S(2)}) collective-permute-start(f32[32,192]{1,0:T(8,128)S(1)} %add_add_fusion.refs_1_), channel_id=1, source_target_pairs={{0,8},{4,12},{8,0},{12,4},{16,24},{20,28},{24,16},{28,20},{1,9},{5... | collective-permute-start | bytes 73736 | tf_op jit(solution)/shard_map/ppermute | solution.py:312
  96.4 4.8 %collective-permute-start.44 = (f32[32,192]{1,0:T(8,128)S(1)}, f32[32,192]{1,0:T(8,128)S(1)}, u32[]{:S(2)}, u32[]{:S(2)}) collective-permute-start(f32[32,192]{1,0:T(8,128)S(1)} %add_add_fusion.refs_1_), channel_id=1, source_target_pairs={{0,24},{4,28},{8,16},{12,20},{16,8},{20,12},{24,0},{28,4},{1,25},{... | collective-permute-start | bytes 73736 | tf_op jit(solution)/shard_map/ppermute | solution.py:312
  (19 other events, 79.6 us)
